TPU v7x, 32 devices: a whole 2x2x4 slice. The times are simulated.
32 devices in a mesh: robot: 8 (over y, x, core), seed: 4 (over z).
Axes of the slice: x: 2, y: 2, z: 4, core: 2. Of those that a mesh axis runs over, the one named last changes fastest.
Arguments:
- centres: float32 [16, 3, 52, 1024], P('robot', None, None, 'seed'), may hold values from -36 to 36
- sphere_radius: float32 [16, 52], P('robot'), may hold values from 0.2 to 0.8
- counts: int32 [16], P('robot'), may hold values from 26 to 52
- adjacency: int32 [16, 16], P('robot'), may hold values from 0 to 1, as said below
Outputs:
- collision_cost: float32 [16, 1024], P('robot', 'seed')
- blended_path: float32 [16, 3, 52, 32], P('robot')
Inputs may be any that keep to these rules, and one draw needn't show every extreme that they name: `adjacency`: symmetric, with zeros on the diagonal.
All inputs are finite; a program needn't handle non-finite values.
Results may differ from a plain program's by a relative error of at most 0.0003.
Values sent between devices are 32-bit elements; how exact they have to be, the bound alone decides.
No kernel may reach another device: no remote copies, remote signals or barrier semaphores. Data moves between devices by JAX's collectives and lax.ppermute only.
A program may use at most 64 MiB of HBM per device.

v0:
```python
import jax
import jax.numpy as jnp
from jax import lax
from jax.sharding import PartitionSpec as P

W = 32


lane_width = 128


def shifted(block, axis, distance):
    devices = range(lax.axis_size(axis))
    route = [((i - distance) % len(devices), i) for i in devices]
    return lax.ppermute(block, axis, route)


def swept_blocks(centres, sphere_radius):
    robots_here, _, spheres, columns = centres.shape
    shaped = centres.reshape(robots_here, 3, spheres, columns // W, W)
    ahead_point = jnp.concatenate([shaped[..., 1:], shaped[..., -1:]], axis=4)
    middle = 0.5 * (shaped + ahead_point)
    step_length = jnp.sqrt(jnp.sum((ahead_point - shaped) ** 2, axis=1) + 1e-06)
    swept_radius = sphere_radius[:, :, None, None] + 0.5 * step_length
    swept_block = jnp.concatenate([middle, swept_radius[:, None]], axis=1)
    return swept_block.reshape(robots_here, 4, spheres, columns)


def active_spheres(counts, spheres):
    return (jnp.arange(spheres, dtype=jnp.int32)[None, :] < counts[:, None]).astype(jnp.float32)


def pair_cost(first_block, first_active, second_block, second_active, sphere_mask):
    spheres = first_block.shape[1]
    columns = first_block.shape[2]
    weights = first_active[:, None] * second_active[None, :] * sphere_mask

    def tile_cost(tile_index):
        offset = tile_index * lane_width
        first_tile = lax.dynamic_slice_in_dim(first_block, offset, lane_width, 2)
        second_tile = lax.dynamic_slice_in_dim(second_block, offset, lane_width, 2)
        distance = jnp.zeros((spheres, spheres, lane_width), jnp.float32)
        for axis_index in range(3):
            gap = first_tile[axis_index][:, None, :] - second_tile[axis_index][None, :, :]
            distance = distance + gap * gap
        spread = first_tile[3][:, None, :] + second_tile[3][None, :, :]
        return jnp.sum(weights[:, :, None] * jnp.exp(-distance / (spread * spread)), axis=(0, 1))

    tiles = lax.map(tile_cost, jnp.arange(columns // lane_width, dtype=jnp.int32))
    return tiles.reshape(columns) / (spheres * spheres)


def self_costs(own_blocks, own_active):
    spheres = own_blocks.shape[2]
    order = jnp.arange(spheres, dtype=jnp.int32)
    apart = (order[None, :] >= order[:, None] + 2).astype(jnp.float32)

    def single(robot_row):
        return pair_cost(
            own_blocks[robot_row],
            own_active[robot_row],
            own_blocks[robot_row],
            own_active[robot_row],
            apart,
        )

    return lax.map(single, jnp.arange(own_blocks.shape[0], dtype=jnp.int32))


def cross_costs(own_blocks, own_active, other_blocks, other_active, link_rows):
    robots_here = own_blocks.shape[0]
    arrived_count = other_blocks.shape[0]
    spheres = own_blocks.shape[2]
    columns = own_blocks.shape[3]
    full_mask = jnp.ones((spheres, spheres), jnp.float32)

    def one_pair(pair_index):
        first_row = pair_index // arrived_count
        second_row = pair_index % arrived_count
        return lax.cond(
            link_rows[first_row, second_row] != 0,
            lambda: pair_cost(
                own_blocks[first_row],
                own_active[first_row],
                other_blocks[second_row],
                other_active[second_row],
                full_mask,
            ),
            lambda: jnp.zeros((columns,), jnp.float32),
        )

    pair_terms = lax.map(one_pair, jnp.arange(robots_here * arrived_count, dtype=jnp.int32))
    return pair_terms.reshape(robots_here, arrived_count, columns)


def seed_weights(centres, robot_cost):
    robots_here, _, spheres, columns = centres.shape
    seed_count = columns // W
    seed_cost = jnp.sum(robot_cost.reshape(robots_here, seed_count, W), axis=2)
    weight = 1.0 / (1.0 + seed_cost)
    shaped = centres.reshape(robots_here, 3, spheres, seed_count, W)
    weighted = jnp.sum(shaped * weight[:, None, None, :, None], axis=3)
    return (weighted, jnp.sum(weight, axis=1))


def local(centres, sphere_radius, counts, adjacency):
    own_blocks = swept_blocks(centres, sphere_radius)
    spheres = own_blocks.shape[2]
    robots_here = own_blocks.shape[0]
    own_active = active_spheres(counts, spheres)
    robot_cost = self_costs(own_blocks, own_active)
    group_size = lax.axis_size("robot")
    halfway = group_size // 2
    position = lax.axis_index("robot")
    order = jnp.arange(robots_here, dtype=jnp.int32)
    local_links = lax.dynamic_slice_in_dim(adjacency, position * robots_here, robots_here, 1)
    local_links = jnp.where(order[:, None] < order[None, :], local_links, 0)
    local_terms = cross_costs(own_blocks, own_active, own_blocks, own_active, local_links)
    robot_cost = robot_cost + jnp.sum(local_terms, axis=1) + jnp.sum(local_terms, axis=0)

    def turn(turn_index, state_now):
        totals_now, visiting, visiting_counts, returned = state_now
        visiting, visiting_counts, returned = shifted(
            (visiting, visiting_counts, returned), "robot", 1
        )
        anchor = (position - turn_index) % group_size
        taken = (turn_index < halfway) | (position < halfway)
        link_rows = lax.dynamic_slice_in_dim(adjacency, anchor * robots_here, robots_here, 1)
        link_rows = jnp.where(taken, link_rows, 0)
        pair_terms = cross_costs(
            own_blocks, own_active, visiting, active_spheres(visiting_counts, spheres), link_rows
        )
        return (
            totals_now + jnp.sum(pair_terms, axis=1),
            visiting,
            visiting_counts,
            returned + jnp.sum(pair_terms, axis=0),
        )

    start_state = (robot_cost, own_blocks, counts, jnp.zeros_like(robot_cost))
    robot_cost, _, _, returned = lax.fori_loop(1, halfway + 1, turn, start_state)
    robot_cost = robot_cost + shifted(returned, "robot", -halfway)
    weighted, totals = seed_weights(centres, robot_cost)
    weighted, totals = lax.psum((weighted, totals), "seed")
    return (robot_cost, weighted / totals[:, None, None, None])


def solution(mesh):
    return jax.shard_map(
        local,
        mesh=mesh,
        in_specs=(P("robot", None, None, "seed"), P("robot", None), P("robot"), P("robot", None)),
        out_specs=(P("robot", "seed"), P("robot", None, None, None)),
        check_vma=False,
    )
```

profile of v0, /device:TPU:0, one launch (start us, length us, event | category | flops | bytes accessed | tf_op | source)
XLA Modules:
  0.0 232.4 jit_solution(429933886269901990)
XLA Ops:
  5.3 23.8 %while.118 = (s32[]{:T(128)}, f32[4,256]{1,0:T(4,128)S(1)}, s32[4]{0:T(128)S(1)}, s32[2,2]{1,0:T(2,128)S(1)}, f32[2,4,52,256]{3,2,1,0:T(8,128)S(1)}, /*index=5*/...) while((s32[]{:T(128)}, f32[4,256]{1,0:T(4,128)S(1)}, ...), condition=%wide.region_12.13_spmd.clone, body=%wide.region_6.12_spmd.clone.sunk | while | flops 4848652 | bytes 1520785 | solution.py:92
  14.4 5.5 %conditional.6 = (f32[1,256]{1,0:T(1,128)S(1)}) conditional(s32[]{:T(128)} %bitcast.108, () %tuple.238, (s32[]{:T(128)}, f32[2,4,52,256]{3,2,1,0:T(8,128)S(1)}, s32[]{:T(128)}, f32[2,52]{1,0:T(2,128)S(1)}) %tuple.239), branch_computations={%region_7.7_spmd, %region_8.11_spmd} | conditional | flops 4848415 | bytes 1517875 | solution.py:80
  14.5 5.4 %while.112 = (s32[]{:T(128)}, f32[2,128]{1,0:T(2,128)S(1)}, s32[2]{0:T(128)S(1)}, f32[4,52,256]{2,1,0:T(8,128)S(1)}, f32[4,52,256]{2,1,0:T(8,128)S(1)}, /*index=...) while((s32[]{:T(128)}, f32[2,128]{1,0:T(2,128)S(1)}, ...), condition=%wide.region_11.10_spmd.clone, body=%wide.region_9.9_spmd.clone.sunk | while | flops 4848153 | bytes 662807 | solution.py:49
  18.5 1.3 multiply_reduce_fusion.8
  29.2 16.2 %while.117 = (s32[]{:T(128)}, f32[2,256]{1,0:T(2,128)S(1)}, s32[2]{0:T(128)S(1)}, f32[2,4,52,256]{3,2,1,0:T(8,128)S(1)}, f32[2,52]{1,0:T(2,128)S(1)}, /*index=5*...) while((s32[]{:T(128)}, f32[2,256]{1,0:T(2,128)S(1)}, ...), condition=%wide.region_5.6_spmd.clone, body=%wide.region_1.5_spmd.clone.sunk | while | flops 4853822 | bytes 774118 | solution.py:67
  31.9 5.3 %while.121 = (s32[]{:T(128)}, f32[2,128]{1,0:T(2,128)S(1)}, f32[52,52]{1,0:T(8,128)S(1)}, s32[2]{0:T(128)S(1)}, f32[4,52,256]{2,1,0:T(8,128)S(1)}, /*index=5*/s3...) while((s32[]{:T(128)}, f32[2,128]{1,0:T(2,128)S(1)}, f32[52,52]{1,0:T(8,128)S(1)}, ...), condition=%wide.region_4.4_spmd, body=%wide.region_2.3_spmd.sunk | while | flops 4845449 | bytes 332071 | solution.py:49
  33.2 1.3 multiply_reduce_fusion.9
  35.8 1.3 multiply_reduce_fusion.9
  40.0 5.3 %while.121 = (s32[]{:T(128)}, f32[2,128]{1,0:T(2,128)S(1)}, f32[52,52]{1,0:T(8,128)S(1)}, s32[2]{0:T(128)S(1)}, f32[4,52,256]{2,1,0:T(8,128)S(1)}, /*index=5*/s3...) while((s32[]{:T(128)}, f32[2,128]{1,0:T(2,128)S(1)}, f32[52,52]{1,0:T(8,128)S(1)}, ...), condition=%wide.region_4.4_spmd, body=%wide.region_2.3_spmd.sunk | while | flops 4845449 | bytes 332071 | solution.py:49
  41.3 1.3 multiply_reduce_fusion.9
  43.9 1.3 multiply_reduce_fusion.9
  45.4 160.6 %while.120 = (s32[]{:T(128)}, f32[2,256]{1,0:T(2,128)S(1)}, f32[2,4,52,256]{3,2,1,0:T(8,128)S(1)}, s32[2]{0:T(128)S(1)}, f32[2,256]{1,0:T(2,128)S(1)}, /*index=5...) while((s32[]{:T(128)}, f32[2,256]{1,0:T(2,128)S(1)}, ...), condition=%wide.region_25.26_spmd.clone, body=%wide.region_15.25_spmd.clone.sunk | while | flops 4851445 | bytes 4118824 | solution.py:141
  45.8 9.3 %collective-permute-done.1 = s32[2]{0:T(128)S(1)} collective-permute-done((s32[2]{0:T(128)S(1)}, s32[2]{0:T(128)S(1)}, u32[]{:S(2)}, u32[]{:S(2)}) %collective-permute-start.1) | collective-permute-done | bytes 40 | tf_op jit(solution)/shard_map/while/body/eval_jaxpr/ppermute | solution.py:15
  55.1 35.0 %while.122 = (s32[]{:T(128)}, f32[4,256]{1,0:T(4,128)S(1)}, s32[4]{0:T(128)S(1)}, s32[2,2]{1,0:T(2,128)S(1)}, f32[2,4,52,256]{3,2,1,0:T(8,128)S(1)}, /*index=5*/...) while((s32[]{:T(128)}, f32[4,256]{1,0:T(4,128)S(1)}, ...), condition=%wide.region_22.22_spmd.clone, body=%wide.region_16.21_spmd.clone.sunk | while | flops 4848652 | bytes 1520817 | solution.py:92
  59.6 5.5 %conditional.7 = (f32[1,256]{1,0:T(1,128)S(1)}) conditional(s32[]{:T(128)} %bitcast.110, () %tuple.244, (s32[]{:T(128)}, f32[2,4,52,256]{3,2,1,0:T(8,128)S(1)}, s32[]{:T(128)}, f32[2,4,52,256]{3,2,1,0:T(8,128)S(1)}, f32[2,52]{1,0:T(2,128)S(1)}, /*index=5*/f32[2,52]{1,0:T(2,128)S(1)}) %tuple.245), branch_computations={%region_17.16_spmd, %region_18.20_spmd} | conditional | flops 4848415 | bytes 1517875 | solution.py:80
  59.7 5.4 %while.113 = (s32[]{:T(128)}, f32[2,128]{1,0:T(2,128)S(1)}, s32[2]{0:T(128)S(1)}, f32[4,52,256]{2,1,0:T(8,128)S(1)}, f32[4,52,256]{2,1,0:T(8,128)S(1)}, /*index=...) while((s32[]{:T(128)}, f32[2,128]{1,0:T(2,128)S(1)}, ...), condition=%wide.region_21.19_spmd.clone, body=%wide.region_19.18_spmd.clone.sunk | while | flops 4848153 | bytes 662807 | solution.py:49
  61.1 1.3 multiply_reduce_fusion.7
  74.3 5.5 %conditional.7 = (f32[1,256]{1,0:T(1,128)S(1)}) conditional(s32[]{:T(128)} %bitcast.110, () %tuple.244, (s32[]{:T(128)}, f32[2,4,52,256]{3,2,1,0:T(8,128)S(1)}, s32[]{:T(128)}, f32[2,4,52,256]{3,2,1,0:T(8,128)S(1)}, f32[2,52]{1,0:T(2,128)S(1)}, /*index=5*/f32[2,52]{1,0:T(2,128)S(1)}) %tuple.245), branch_computations={%region_17.16_spmd, %region_18.20_spmd} | conditional | flops 4848415 | bytes 1517875 | solution.py:80
  74.5 5.4 %while.113 = (s32[]{:T(128)}, f32[2,128]{1,0:T(2,128)S(1)}, s32[2]{0:T(128)S(1)}, f32[4,52,256]{2,1,0:T(8,128)S(1)}, f32[4,52,256]{2,1,0:T(8,128)S(1)}, /*index=...) while((s32[]{:T(128)}, f32[2,128]{1,0:T(2,128)S(1)}, ...), condition=%wide.region_21.19_spmd.clone, body=%wide.region_19.18_spmd.clone.sunk | while | flops 4848153 | bytes 662807 | solution.py:49
  75.8 1.3 multiply_reduce_fusion.7
  84.5 5.5 %conditional.7 = (f32[1,256]{1,0:T(1,128)S(1)}) conditional(s32[]{:T(128)} %bitcast.110, () %tuple.244, (s32[]{:T(128)}, f32[2,4,52,256]{3,2,1,0:T(8,128)S(1)}, s32[]{:T(128)}, f32[2,4,52,256]{3,2,1,0:T(8,128)S(1)}, f32[2,52]{1,0:T(2,128)S(1)}, /*index=5*/f32[2,52]{1,0:T(2,128)S(1)}) %tuple.245), branch_computations={%region_17.16_spmd, %region_18.20_spmd} | conditional | flops 4848415 | bytes 1517875 | solution.py:80
  84.6 5.4 %while.113 = (s32[]{:T(128)}, f32[2,128]{1,0:T(2,128)S(1)}, s32[2]{0:T(128)S(1)}, f32[4,52,256]{2,1,0:T(8,128)S(1)}, f32[4,52,256]{2,1,0:T(8,128)S(1)}, /*index=...) while((s32[]{:T(128)}, f32[2,128]{1,0:T(2,128)S(1)}, ...), condition=%wide.region_21.19_spmd.clone, body=%wide.region_19.18_spmd.clone.sunk | while | flops 4848153 | bytes 662807 | solution.py:49
  86.0 1.3 multiply_reduce_fusion.7
  90.6 8.5 %collective-permute-done.1 = s32[2]{0:T(128)S(1)} collective-permute-done((s32[2]{0:T(128)S(1)}, s32[2]{0:T(128)S(1)}, u32[]{:S(2)}, u32[]{:S(2)}) %collective-permute-start.1) | collective-permute-done | bytes 40 | tf_op jit(solution)/shard_map/while/body/eval_jaxpr/ppermute | solution.py:15
  99.1 24.0 %while.122 = (s32[]{:T(128)}, f32[4,256]{1,0:T(4,128)S(1)}, s32[4]{0:T(128)S(1)}, s32[2,2]{1,0:T(2,128)S(1)}, f32[2,4,52,256]{3,2,1,0:T(8,128)S(1)}, /*index=5*/...) while((s32[]{:T(128)}, f32[4,256]{1,0:T(4,128)S(1)}, ...), condition=%wide.region_22.22_spmd.clone, body=%wide.region_16.21_spmd.clone.sunk | while | flops 4848652 | bytes 1520817 | solution.py:92
  117.5 5.5 %conditional.7 = (f32[1,256]{1,0:T(1,128)S(1)}) conditional(s32[]{:T(128)} %bitcast.110, () %tuple.244, (s32[]{:T(128)}, f32[2,4,52,256]{3,2,1,0:T(8,128)S(1)}, s32[]{:T(128)}, f32[2,4,52,256]{3,2,1,0:T(8,128)S(1)}, f32[2,52]{1,0:T(2,128)S(1)}, /*index=5*/f32[2,52]{1,0:T(2,128)S(1)}) %tuple.245), branch_computations={%region_17.16_spmd, %region_18.20_spmd} | conditional | flops 4848415 | bytes 1517875 | solution.py:80
  117.7 5.4 %while.113 = (s32[]{:T(128)}, f32[2,128]{1,0:T(2,128)S(1)}, s32[2]{0:T(128)S(1)}, f32[4,52,256]{2,1,0:T(8,128)S(1)}, f32[4,52,256]{2,1,0:T(8,128)S(1)}, /*index=...) while((s32[]{:T(128)}, f32[2,128]{1,0:T(2,128)S(1)}, ...), condition=%wide.region_21.19_spmd.clone, body=%wide.region_19.18_spmd.clone.sunk | while | flops 4848153 | bytes 662807 | solution.py:49
  119.0 1.3 multiply_reduce_fusion.7
  123.7 8.5 %collective-permute-done.1 = s32[2]{0:T(128)S(1)} collective-permute-done((s32[2]{0:T(128)S(1)}, s32[2]{0:T(128)S(1)}, u32[]{:S(2)}, u32[]{:S(2)}) %collective-permute-start.1) | collective-permute-done | bytes 40 | tf_op jit(solution)/shard_map/while/body/eval_jaxpr/ppermute | solution.py:15
  132.2 24.0 %while.122 = (s32[]{:T(128)}, f32[4,256]{1,0:T(4,128)S(1)}, s32[4]{0:T(128)S(1)}, s32[2,2]{1,0:T(2,128)S(1)}, f32[2,4,52,256]{3,2,1,0:T(8,128)S(1)}, /*index=5*/...) while((s32[]{:T(128)}, f32[4,256]{1,0:T(4,128)S(1)}, ...), condition=%wide.region_22.22_spmd.clone, body=%wide.region_16.21_spmd.clone.sunk | while | flops 4848652 | bytes 1520817 | solution.py:92
  146.0 5.5 %conditional.7 = (f32[1,256]{1,0:T(1,128)S(1)}) conditional(s32[]{:T(128)} %bitcast.110, () %tuple.244, (s32[]{:T(128)}, f32[2,4,52,256]{3,2,1,0:T(8,128)S(1)}, s32[]{:T(128)}, f32[2,4,52,256]{3,2,1,0:T(8,128)S(1)}, f32[2,52]{1,0:T(2,128)S(1)}, /*index=5*/f32[2,52]{1,0:T(2,128)S(1)}) %tuple.245), branch_computations={%region_17.16_spmd, %region_18.20_spmd} | conditional | flops 4848415 | bytes 1517875 | solution.py:80
  146.1 5.4 %while.113 = (s32[]{:T(128)}, f32[2,128]{1,0:T(2,128)S(1)}, s32[2]{0:T(128)S(1)}, f32[4,52,256]{2,1,0:T(8,128)S(1)}, f32[4,52,256]{2,1,0:T(8,128)S(1)}, /*index=...) while((s32[]{:T(128)}, f32[2,128]{1,0:T(2,128)S(1)}, ...), condition=%wide.region_21.19_spmd.clone, body=%wide.region_19.18_spmd.clone.sunk | while | flops 4848153 | bytes 662807 | solution.py:49
  147.5 1.3 multiply_reduce_fusion.7
  156.3 3.2 %collective-permute-start = (f32[2,4,52,256]{3,2,1,0:T(8,128)S(1)}, f32[2,4,52,256]{3,2,1,0:T(8,128)S(1)}, u32[]{:S(2)}, u32[]{:S(2)}) collective-permute-start(f32[2,4,52,256]{3,2,1,0:T(8,128)S(1)} %get-tuple-element.1672), channel_id=1, source_target_pairs={{28,0},{0,4},{4,8},{8,12},{12,16},{16,20},{20,24},{24,28},{29,1},{... | collective-permute-start | bytes 1277960 | tf_op jit(solution)/shard_map/while/body/eval_jaxpr/ppermute | solution.py:15
  159.9 5.4 %collective-permute-done.1 = s32[2]{0:T(128)S(1)} collective-permute-done((s32[2]{0:T(128)S(1)}, s32[2]{0:T(128)S(1)}, u32[]{:S(2)}, u32[]{:S(2)}) %collective-permute-start.1) | collective-permute-done | bytes 40 | tf_op jit(solution)/shard_map/while/body/eval_jaxpr/ppermute | solution.py:15
  165.3 40.5 %while.122 = (s32[]{:T(128)}, f32[4,256]{1,0:T(4,128)S(1)}, s32[4]{0:T(128)S(1)}, s32[2,2]{1,0:T(2,128)S(1)}, f32[2,4,52,256]{3,2,1,0:T(8,128)S(1)}, /*index=5*/...) while((s32[]{:T(128)}, f32[4,256]{1,0:T(4,128)S(1)}, ...), condition=%wide.region_22.22_spmd.clone, body=%wide.region_16.21_spmd.clone.sunk | while | flops 4848652 | bytes 1520817 | solution.py:92
  169.8 5.5 %conditional.7 = (f32[1,256]{1,0:T(1,128)S(1)}) conditional(s32[]{:T(128)} %bitcast.110, () %tuple.244, (s32[]{:T(128)}, f32[2,4,52,256]{3,2,1,0:T(8,128)S(1)}, s32[]{:T(128)}, f32[2,4,52,256]{3,2,1,0:T(8,128)S(1)}, f32[2,52]{1,0:T(2,128)S(1)}, /*index=5*/f32[2,52]{1,0:T(2,128)S(1)}) %tuple.245), branch_computations={%region_17.16_spmd, %region_18.20_spmd} | conditional | flops 4848415 | bytes 1517875 | solution.py:80
  170.0 5.4 %while.113 = (s32[]{:T(128)}, f32[2,128]{1,0:T(2,128)S(1)}, s32[2]{0:T(128)S(1)}, f32[4,52,256]{2,1,0:T(8,128)S(1)}, f32[4,52,256]{2,1,0:T(8,128)S(1)}, /*index=...) while((s32[]{:T(128)}, f32[2,128]{1,0:T(2,128)S(1)}, ...), condition=%wide.region_21.19_spmd.clone, body=%wide.region_19.18_spmd.clone.sunk | while | flops 4848153 | bytes 662807 | solution.py:49
  171.3 1.3 multiply_reduce_fusion.7
  180.0 5.5 %conditional.7 = (f32[1,256]{1,0:T(1,128)S(1)}) conditional(s32[]{:T(128)} %bitcast.110, () %tuple.244, (s32[]{:T(128)}, f32[2,4,52,256]{3,2,1,0:T(8,128)S(1)}, s32[]{:T(128)}, f32[2,4,52,256]{3,2,1,0:T(8,128)S(1)}, f32[2,52]{1,0:T(2,128)S(1)}, /*index=5*/f32[2,52]{1,0:T(2,128)S(1)}) %tuple.245), branch_computations={%region_17.16_spmd, %region_18.20_spmd} | conditional | flops 4848415 | bytes 1517875 | solution.py:80
  180.1 5.4 %while.113 = (s32[]{:T(128)}, f32[2,128]{1,0:T(2,128)S(1)}, s32[2]{0:T(128)S(1)}, f32[4,52,256]{2,1,0:T(8,128)S(1)}, f32[4,52,256]{2,1,0:T(8,128)S(1)}, /*index=...) while((s32[]{:T(128)}, f32[2,128]{1,0:T(2,128)S(1)}, ...), condition=%wide.region_21.19_spmd.clone, body=%wide.region_19.18_spmd.clone.sunk | while | flops 4848153 | bytes 662807 | solution.py:49
  181.4 1.3 multiply_reduce_fusion.7
  190.1 5.5 %conditional.7 = (f32[1,256]{1,0:T(1,128)S(1)}) conditional(s32[]{:T(128)} %bitcast.110, () %tuple.244, (s32[]{:T(128)}, f32[2,4,52,256]{3,2,1,0:T(8,128)S(1)}, s32[]{:T(128)}, f32[2,4,52,256]{3,2,1,0:T(8,128)S(1)}, f32[2,52]{1,0:T(2,128)S(1)}, /*index=5*/f32[2,52]{1,0:T(2,128)S(1)}) %tuple.245), branch_computations={%region_17.16_spmd, %region_18.20_spmd} | conditional | flops 4848415 | bytes 1517875 | solution.py:80
  190.2 5.4 %while.113 = (s32[]{:T(128)}, f32[2,128]{1,0:T(2,128)S(1)}, s32[2]{0:T(128)S(1)}, f32[4,52,256]{2,1,0:T(8,128)S(1)}, f32[4,52,256]{2,1,0:T(8,128)S(1)}, /*index=...) while((s32[]{:T(128)}, f32[2,128]{1,0:T(2,128)S(1)}, ...), condition=%wide.region_21.19_spmd.clone, body=%wide.region_19.18_spmd.clone.sunk | while | flops 4848153 | bytes 662807 | solution.py:49
  200.2 5.5 %conditional.7 = (f32[1,256]{1,0:T(1,128)S(1)}) conditional(s32[]{:T(128)} %bitcast.110, () %tuple.244, (s32[]{:T(128)}, f32[2,4,52,256]{3,2,1,0:T(8,128)S(1)}, s32[]{:T(128)}, f32[2,4,52,256]{3,2,1,0:T(8,128)S(1)}, f32[2,52]{1,0:T(2,128)S(1)}, /*index=5*/f32[2,52]{1,0:T(2,128)S(1)}) %tuple.245), branch_computations={%region_17.16_spmd, %region_18.20_spmd} | conditional | flops 4848415 | bytes 1517875 | solution.py:80
  200.3 5.4 %while.113 = (s32[]{:T(128)}, f32[2,128]{1,0:T(2,128)S(1)}, s32[2]{0:T(128)S(1)}, f32[4,52,256]{2,1,0:T(8,128)S(1)}, f32[4,52,256]{2,1,0:T(8,128)S(1)}, /*index=...) while((s32[]{:T(128)}, f32[2,128]{1,0:T(2,128)S(1)}, ...), condition=%wide.region_21.19_spmd.clone, body=%wide.region_19.18_spmd.clone.sunk | while | flops 4848153 | bytes 662807 | solution.py:49
  206.0 3.6 %collective-permute-done.3 = f32[2,256]{1,0:T(2,128)S(1)} collective-permute-done((f32[2,256]{1,0:T(2,128)S(1)}, f32[2,256]{1,0:T(2,128)S(1)}, u32[]{:S(2)}, u32[]{:S(2)}) %collective-permute-start.3) | collective-permute-done | bytes 2080 | tf_op jit(solution)/shard_map/ppermute | solution.py:15
  210.0 21.6 %all-reduce = (f32[2,3,52,32]{2,3,1,0:T(8,128)S(1)}, f32[2]{0:T(128)S(1)}) all-reduce(f32[2,3,52,32]{2,3,1,0:T(8,128)S(1)} %multiply_reduce_fusion.3, f32[2]{0:T(128)S(1)} %get-tuple-element.991), channel_id=1, replica_groups=mesh['robot'=8,'seed'=4] {'seed'}, use_global_device_ids=true, to_apply=%region_28.29 | all-reduce | flops 9986 | bytes 79888 | tf_op jit(solution)/shard_map/psum | solution.py:144
  (374 shorter events, 70.9 us)
Async XLA Ops:
  1.9 0.7 copy-start.3
  2.9 0.7 copy-start.2
  4.5 0.7 copy-start
  45.4 9.7 %collective-permute-start = (f32[2,4,52,256]{3,2,1,0:T(8,128)S(1)}, f32[2,4,52,256]{3,2,1,0:T(8,128)S(1)}, u32[]{:S(2)}, u32[]{:S(2)}) collective-permute-start(f32[2,4,52,256]{3,2,1,0:T(8,128)S(1)} %get-tuple-element.1672), channel_id=1, source_target_pairs={{28,0},{0,4},{4,8},{8,12},{12,16},{16,20},{20,24},{24,28},{29,1},{... | collective-permute-start | bytes 1277960 | tf_op jit(solution)/shard_map/while/body/eval_jaxpr/ppermute | solution.py:15
  45.4 9.6 %collective-permute-start.1 = (s32[2]{0:T(128)S(1)}, s32[2]{0:T(128)S(1)}, u32[]{:S(2)}, u32[]{:S(2)}) collective-permute-start(s32[2]{0:T(128)S(1)} %get-tuple-element.1673), channel_id=1, source_target_pairs={{28,0},{0,4},{4,8},{8,12},{12,16},{16,20},{20,24},{24,28},{29,1},{... | collective-permute-start | bytes 32 | tf_op jit(solution)/shard_map/while/body/eval_jaxpr/ppermute | solution.py:15
  45.5 44.6 %collective-permute-start.2 = (f32[2,256]{1,0:T(2,128)S(1)}, f32[2,256]{1,0:T(2,128)S(1)}, u32[]{:S(2)}, u32[]{:S(2)}) collective-permute-start(f32[2,256]{1,0:T(2,128)S(1)} %broadcast_select_fusion.2), channel_id=1, source_target_pairs={{28,0},{0,4},{4,8},{8,12},{12,16},{16,20},{20,24},{24,28},{29,1},{... | collective-permute-start | bytes 6152 | tf_op jit(solution)/shard_map/while/body/eval_jaxpr/ppermute | solution.py:15
  90.2 8.9 %collective-permute-start = (f32[2,4,52,256]{3,2,1,0:T(8,128)S(1)}, f32[2,4,52,256]{3,2,1,0:T(8,128)S(1)}, u32[]{:S(2)}, u32[]{:S(2)}) collective-permute-start(f32[2,4,52,256]{3,2,1,0:T(8,128)S(1)} %get-tuple-element.1672), channel_id=1, source_target_pairs={{28,0},{0,4},{4,8},{8,12},{12,16},{16,20},{20,24},{24,28},{29,1},{... | collective-permute-start | bytes 1277960 | tf_op jit(solution)/shard_map/while/body/eval_jaxpr/ppermute | solution.py:15
  90.3 8.9 %collective-permute-start.1 = (s32[2]{0:T(128)S(1)}, s32[2]{0:T(128)S(1)}, u32[]{:S(2)}, u32[]{:S(2)}) collective-permute-start(s32[2]{0:T(128)S(1)} %get-tuple-element.1673), channel_id=1, source_target_pairs={{28,0},{0,4},{4,8},{8,12},{12,16},{16,20},{20,24},{24,28},{29,1},{... | collective-permute-start | bytes 32 | tf_op jit(solution)/shard_map/while/body/eval_jaxpr/ppermute | solution.py:15
  90.3 32.9 %collective-permute-start.2 = (f32[2,256]{1,0:T(2,128)S(1)}, f32[2,256]{1,0:T(2,128)S(1)}, u32[]{:S(2)}, u32[]{:S(2)}) collective-permute-start(f32[2,256]{1,0:T(2,128)S(1)} %broadcast_select_fusion.2), channel_id=1, source_target_pairs={{28,0},{0,4},{4,8},{8,12},{12,16},{16,20},{20,24},{24,28},{29,1},{... | collective-permute-start | bytes 6152 | tf_op jit(solution)/shard_map/while/body/eval_jaxpr/ppermute | solution.py:15
  123.3 8.9 %collective-permute-start = (f32[2,4,52,256]{3,2,1,0:T(8,128)S(1)}, f32[2,4,52,256]{3,2,1,0:T(8,128)S(1)}, u32[]{:S(2)}, u32[]{:S(2)}) collective-permute-start(f32[2,4,52,256]{3,2,1,0:T(8,128)S(1)} %get-tuple-element.1672), channel_id=1, source_target_pairs={{28,0},{0,4},{4,8},{8,12},{12,16},{16,20},{20,24},{24,28},{29,1},{... | collective-permute-start | bytes 1277960 | tf_op jit(solution)/shard_map/while/body/eval_jaxpr/ppermute | solution.py:15
  123.3 8.9 %collective-permute-start.1 = (s32[2]{0:T(128)S(1)}, s32[2]{0:T(128)S(1)}, u32[]{:S(2)}, u32[]{:S(2)}) collective-permute-start(s32[2]{0:T(128)S(1)} %get-tuple-element.1673), channel_id=1, source_target_pairs={{28,0},{0,4},{4,8},{8,12},{12,16},{16,20},{20,24},{24,28},{29,1},{... | collective-permute-start | bytes 32 | tf_op jit(solution)/shard_map/while/body/eval_jaxpr/ppermute | solution.py:15
  123.4 32.9 %collective-permute-start.2 = (f32[2,256]{1,0:T(2,128)S(1)}, f32[2,256]{1,0:T(2,128)S(1)}, u32[]{:S(2)}, u32[]{:S(2)}) collective-permute-start(f32[2,256]{1,0:T(2,128)S(1)} %broadcast_select_fusion.2), channel_id=1, source_target_pairs={{28,0},{0,4},{4,8},{8,12},{12,16},{16,20},{20,24},{24,28},{29,1},{... | collective-permute-start | bytes 6152 | tf_op jit(solution)/shard_map/while/body/eval_jaxpr/ppermute | solution.py:15
  156.3 8.9 %collective-permute-start = (f32[2,4,52,256]{3,2,1,0:T(8,128)S(1)}, f32[2,4,52,256]{3,2,1,0:T(8,128)S(1)}, u32[]{:S(2)}, u32[]{:S(2)}) collective-permute-start(f32[2,4,52,256]{3,2,1,0:T(8,128)S(1)} %get-tuple-element.1672), channel_id=1, source_target_pairs={{28,0},{0,4},{4,8},{8,12},{12,16},{16,20},{20,24},{24,28},{29,1},{... | collective-permute-start | bytes 1277960 | tf_op jit(solution)/shard_map/while/body/eval_jaxpr/ppermute | solution.py:15
  159.6 5.7 %collective-permute-start.1 = (s32[2]{0:T(128)S(1)}, s32[2]{0:T(128)S(1)}, u32[]{:S(2)}, u32[]{:S(2)}) collective-permute-start(s32[2]{0:T(128)S(1)} %get-tuple-element.1673), channel_id=1, source_target_pairs={{28,0},{0,4},{4,8},{8,12},{12,16},{16,20},{20,24},{24,28},{29,1},{... | collective-permute-start | bytes 32 | tf_op jit(solution)/shard_map/while/body/eval_jaxpr/ppermute | solution.py:15
  159.6 46.3 %collective-permute-start.2 = (f32[2,256]{1,0:T(2,128)S(1)}, f32[2,256]{1,0:T(2,128)S(1)}, u32[]{:S(2)}, u32[]{:S(2)}) collective-permute-start(f32[2,256]{1,0:T(2,128)S(1)} %broadcast_select_fusion.2), channel_id=1, source_target_pairs={{28,0},{0,4},{4,8},{8,12},{12,16},{16,20},{20,24},{24,28},{29,1},{... | collective-permute-start | bytes 6152 | tf_op jit(solution)/shard_map/while/body/eval_jaxpr/ppermute | solution.py:15
  205.9 3.7 %collective-permute-start.3 = (f32[2,256]{1,0:T(2,128)S(1)}, f32[2,256]{1,0:T(2,128)S(1)}, u32[]{:S(2)}, u32[]{:S(2)}) collective-permute-start(f32[2,256]{1,0:T(2,128)S(1)} %get-tuple-element.653), channel_id=1, source_target_pairs={{16,0},{20,4},{24,8},{28,12},{0,16},{4,20},{8,24},{12,28},{17,1},{... | collective-permute-start | bytes 6152 | tf_op jit(solution)/shard_map/ppermute | solution.py:15
  209.6 22.8 %copy-start.1 = (f32[2,256]{1,0:T(2,128)}, f32[2,256]{1,0:T(2,128)S(1)}, u32[]{:S(2)}) copy-start(f32[2,256]{1,0:T(2,128)S(1)} %add.325) | copy-start | bytes 6148
where the time goes:
time: 229 us; the launch traced here: 232 us
  loops' own time  84.9 us (37%)
  local copies, waits for them, and re-layouts  48.3 us (21%)
  other arithmetic  37.4 us (16%)
  waiting for transfers between devices  35.3 us (15%)
  blocking collectives  21.6 us (9%)
  starting transfers between devices  3.96 us (2%)
    another operation x5, loops' own time, cross_costs(): lax.map(one_pair, jnp.arange(robots_here * arrived_count, dtype=jnp.int32))  64.3 us
    ppermute x13, waiting for transfers between devices, shifted(): return lax.ppermute(block, axis, route)  35.3 us
    reduce_sum x24, other arithmetic, tile_cost(): jnp.sum(weights[:, :, None] * jnp.exp(-distance / (spread * spread)), axi...  31.5 us
    psum x1, blocking collectives, local(): weighted, totals = lax.psum((weighted, totals), 'seed')  21.6 us
    dynamic_slice x26, local copies, waits for them, and re-layouts, self_costs(): return lax.map(single, jnp.arange(own_blocks.shape[0], dtype=jnp.int32))  15.9 us
    another operation x12, loops' own time, pair_cost(): lax.map(tile_cost, jnp.arange(columns // lane_width, dtype=jnp.int32))  15.4 us
    dynamic_slice x20, local copies, waits for them, and re-layouts, one_pair(): link_rows[first_row, second_row] != 0  12.8 us
    dynamic_slice x20, local copies, waits for them, and re-layouts, cross_costs(): lax.map(one_pair, jnp.arange(robots_here * arrived_count, dtype=jnp.int32))  12.4 us
  transfers between devices with their start and end apart: 13, of which 5 were waited for; matrix products, arithmetic and copies ran while one was open for 26% of the time, Pallas kernels for 0%

commit v1 on v0

v1 whole, which is shorter than its diff:
```python
import functools
import math

import jax
import jax.numpy as jnp
from jax import lax
from jax.experimental import pallas as pl
from jax.experimental.pallas import tpu as pltpu
from jax.sharding import PartitionSpec as P

W = 32
LANES = 128
SUB = 8
SCALE = math.sqrt(math.log2(math.e))
FAR = 1e15
VMEM = pl.BlockSpec(memory_space=pltpu.VMEM)
SMEM = pl.BlockSpec(memory_space=pltpu.SMEM)


def round_up(value, step):
    return -(-value // step) * step


class Plan:
    def __init__(self, group, robots_here, spheres, columns):
        self.group = group
        self.here = robots_here
        self.spheres = spheres
        self.columns = columns
        self.width = columns // group
        self.lane_groups = LANES // self.width
        self.rows = -(-spheres // self.lane_groups)
        self.padded = self.rows * self.lane_groups
        self.block_rows = round_up(self.rows, SUB)
        self.slots = group * robots_here
        self.halves = -(-self.slots // 16)
        self.data_rows = robots_here * 4 * self.rows
        self.chunk_rows = round_up(self.data_rows + 1, SUB)
        self.tiles = columns // LANES


def iota(shape, axis):
    return lax.broadcasted_iota(jnp.int32, shape, axis)


def pack_kernel(plan, counts, radius, adjacency, centres, *refs):
    outs, raw, swept = refs[:-2], refs[-2], refs[-1]
    me = lax.axis_index("robot")
    n, g, rows, width = plan.spheres, plan.lane_groups, plan.rows, plan.width
    last = iota((n, LANES), 1) % W == W - 1
    order = iota((n, LANES), 0)
    diagonal = iota((n, n), 0) == iota((n, n), 1)
    for l in range(plan.here):
        column = jnp.sum(jnp.where(diagonal, radius[l : l + 1, :], 0.0), axis=1, keepdims=True)
        robot = me * plan.here + l
        off = FAR * (1 + order + plan.padded * robot).astype(jnp.float32)
        for t in range(plan.tiles):
            squares = jnp.zeros((n, LANES), jnp.float32)
            for c in range(3):
                x = centres[l, c, :, t * LANES : (t + 1) * LANES]
                raw[t, l * 3 + c] = x
                ahead = jnp.where(last, x, pltpu.roll(x, LANES - 1, 1))
                middle = (0.5 * SCALE) * (x + ahead)
                if c == 0:
                    middle = jnp.where(order < counts[l], middle, off)
                swept[t, l * 4 + c, 0:n, :] = middle
                squares = squares + (ahead - x) * (ahead - x)
            swept[t, l * 4 + 3, 0:n, :] = column + 0.5 * jnp.sqrt(squares + 1e-06)
            if plan.padded > n:
                spare = plan.padded - n
                index = n + iota((spare, LANES), 0) + plan.padded * robot
                swept[t, l * 4, n:, :] = FAR * (1 + index).astype(jnp.float32)
                for c in range(1, 4):
                    swept[t, l * 4 + c, n:, :] = jnp.ones((spare, LANES), jnp.float32)
    lane = iota((1, LANES), 1)
    head = jnp.zeros((1, LANES), jnp.float32)
    links = iota((1, plan.slots), 1)
    for l in range(plan.here):
        at = l * (1 + plan.halves)
        head = jnp.where(lane == at, counts[l].astype(jnp.float32), head)
        for h in range(plan.halves):
            bits = jnp.where(
                (adjacency[l : l + 1, :] != 0) & (links // 16 == h), 1 << (links % 16), 0
            ).astype(jnp.float32)
            head = jnp.where(lane == at + 1 + h, jnp.sum(bits, axis=1, keepdims=True), head)
    lane_group = iota((rows, LANES), 1) // width
    for k in range(plan.group):
        dest = me ^ k
        tile = dest // g
        spot = dest % g
        for rc in range(plan.here * 4):
            y = jnp.zeros((rows, LANES), jnp.float32)
            for j in range(g):
                x = swept[tile, rc, pl.ds(j, rows, stride=g), :]
                x = pltpu.roll(x, ((j + g - spot) % g) * width, 1)
                y = jnp.where(lane_group == j, x, y)
            outs[k][rc * rows : (rc + 1) * rows, :] = y
        outs[k][plan.data_rows : plan.data_rows + 1, :] = head


def pack(plan, counts, radius, adjacency, centres):
    chunk = jax.ShapeDtypeStruct((plan.chunk_rows, LANES), jnp.float32)
    return pl.pallas_call(
        functools.partial(pack_kernel, plan),
        out_shape=[chunk] * plan.group
        + [jax.ShapeDtypeStruct((plan.tiles, plan.here * 3, plan.spheres, LANES), jnp.float32)],
        in_specs=[SMEM, VMEM, VMEM, VMEM],
        out_specs=[VMEM] * (plan.group + 1),
        scratch_shapes=[pltpu.VMEM((plan.tiles, plan.here * 4, plan.padded, LANES), jnp.float32)],
        name="pack",
    )(counts, radius, adjacency, centres)


def term(first, second):
    gap = first[0] - second[0]
    square = gap * gap
    for c in (1, 2):
        gap = first[c] - second[c]
        square = square + gap * gap
    inverse = 1.0 / (first[3] + second[3])
    return jnp.exp2(-(square * (inverse * inverse)))


def cost_kernel(plan, *refs):
    chunks = refs[: plan.group]
    out, blocks, totals, heads, sem = refs[plan.group :]
    me = lax.axis_index("robot")
    g, rows, width, here = plan.lane_groups, plan.rows, plan.width, plan.here
    parts = plan.block_rows // SUB
    copies = [
        pltpu.make_async_copy(
            chunks[k].at[pl.ds(plan.data_rows, 1)], heads.at[pl.ds(k, 1)], sem.at[k]
        )
        for k in range(plan.group)
    ]
    for copy in copies:
        copy.start()
    spare = plan.block_rows - rows
    for k in range(plan.group):
        for l in range(here):
            for c in range(4):
                x = chunks[k][(l * 4 + c) * rows : (l * 4 + c + 1) * rows, :]
                for m in range(g):
                    blocks[k * here + l, c, m, 0:rows, :] = pltpu.roll(x, m * width, 1) if m else x
                if spare:
                    fill = -FAR if c == 0 else 1.0
                    blocks[k * here + l, c, 0, rows:, :] = jnp.full((spare, LANES), fill, jnp.float32)
    totals[...] = jnp.zeros_like(totals)
    for copy in copies:
        copy.wait()

    def row(slot, m, r):
        return [blocks[slot, c, m, r : r + 1, :] for c in range(4)]

    def part(slot, i):
        return [blocks[slot, c, 0, i * SUB : (i + 1) * SUB, :] for c in range(4)]

    later = g * iota((SUB, LANES), 0) + iota((SUB, LANES), 1) // width

    @pl.loop(0, plan.slots)
    def _(u):
        total = jnp.zeros((SUB, LANES), jnp.float32)
        for i in range(parts):
            second = part(u, i)
            for m in range(g):
                ahead = later - (iota((SUB, LANES), 1) // width + g - m) % g + g * SUB * i
                for r in range(min(rows, (i + 1) * SUB)):
                    value = term(row(u, m, r), second)
                    if (r + 1) * g + 1 > g * SUB * i:
                        value = jnp.where(ahead >= g * r + 2, value, 0.0)
                    total = total + value
        totals[u] = totals[u] + total
        links = [
            heads[u // here, (u % here) * (1 + plan.halves) + 1 + h].astype(jnp.int32)
            for h in range(plan.halves)
        ]

        @pl.loop(u + 1, plan.slots)
        def _(v):
            robot = v ^ (me * here)
            mask = links[0]
            for h in range(1, plan.halves):
                mask = jnp.where(robot // 16 == h, links[h], mask)

            @pl.when((mask >> (robot % 16)) & 1 == 1)
            def _():
                total = jnp.zeros((SUB, LANES), jnp.float32)
                for i in range(parts):
                    second = part(v, i)
                    for m in range(g):
                        for r in range(rows):
                            total = total + term(row(u, m, r), second)
                totals[u] = totals[u] + total
                totals[v] = totals[v] + total

    spot = iota((1, LANES), 1) // width == me % g
    for k in range(plan.group):
        for l in range(here):
            value = jnp.sum(totals[k * here + l], axis=0, keepdims=True)
            shift = width
            while shift < LANES:
                value = value + pltpu.roll(value, shift, 1)
                shift *= 2
            value = jnp.where(spot, value, 0.0) / (plan.spheres * plan.spheres)
            out[pl.ds((me ^ k) * here + l, 1), :] = value


def cost(plan, chunks):
    slots, g = plan.slots, plan.lane_groups
    return pl.pallas_call(
        functools.partial(cost_kernel, plan),
        out_shape=jax.ShapeDtypeStruct((plan.slots, LANES), jnp.float32),
        in_specs=[VMEM] * plan.group,
        out_specs=VMEM,
        scratch_shapes=[
            pltpu.VMEM((slots, 4, g, plan.block_rows, LANES), jnp.float32),
            pltpu.VMEM((slots, SUB, LANES), jnp.float32),
            pltpu.SMEM((plan.group, LANES), jnp.float32),
            pltpu.SemaphoreType.DMA((plan.group,)),
        ],
        name="cost",
    )(*chunks)


def blend_kernel(plan, seeds_here, costs, raw, cost_out, sums):
    n, here, g = plan.spheres, plan.here, plan.lane_groups
    n_rows = n // 4
    seed_of = iota((seeds_here, LANES), 1) // W
    seed = iota((seeds_here, LANES), 0)
    fold = iota((n_rows, LANES), 1) // W
    per_tile = LANES // W
    for l in range(here):
        lines = []
        seed_cost = jnp.zeros((seeds_here, 1), jnp.float32)
        for t in range(plan.tiles):
            line = costs[t * g * here + l : t * g * here + l + 1, :]
            for d in range(t * g + 1, (t + 1) * g):
                line = line + costs[d * here + l : d * here + l + 1, :]
            cost_out[l : l + 1, t * LANES : (t + 1) * LANES] = line
            lines.append(line)
            mine = seed_of + t * per_tile == seed
            seed_cost = seed_cost + jnp.sum(jnp.where(mine, line, 0.0), axis=1, keepdims=True)
        weight = 1.0 / (1.0 + seed_cost)
        spread = []
        for t in range(plan.tiles):
            mine = seed_of + t * per_tile == seed
            spread.append(jnp.sum(jnp.where(mine, weight, 0.0), axis=0, keepdims=True))
        total = jnp.sum(weight, axis=0, keepdims=True)
        sums[here * 3 * n_rows + l : here * 3 * n_rows + l + 1, :] = jnp.broadcast_to(total, (1, LANES))
        for c in range(3):
            pieces = []
            for j in range(4):
                x = jnp.zeros((n_rows, LANES), jnp.float32)
                for t in range(plan.tiles):
                    part = raw[t, l * 3 + c, pl.ds(j, n_rows, stride=4), :]
                    x = x + part * spread[t]
                pieces.append(x)
            y = jnp.zeros((n_rows, LANES), jnp.float32)
            for turn in range(4):
                z = pieces[0]
                for j in range(4):
                    z = jnp.where(fold == (j - turn) % 4, pieces[j], z)
                y = y + (pltpu.roll(z, turn * W, 1) if turn else z)
            at = (l * 3 + c) * n_rows
            sums[at : at + n_rows, :] = y


def blend(plan, costs, raw):
    seeds_here = plan.columns // W
    rows = round_up(plan.here * (3 * plan.spheres // 4 + 1), SUB)
    return pl.pallas_call(
        functools.partial(blend_kernel, plan, seeds_here),
        out_shape=[
            jax.ShapeDtypeStruct((plan.here, plan.columns), jnp.float32),
            jax.ShapeDtypeStruct((rows, LANES), jnp.float32),
        ],
        in_specs=[VMEM, VMEM],
        out_specs=[VMEM, VMEM],
        name="blend",
    )(costs, raw)


def finish_kernel(plan, *refs):
    parts, out, wide = refs[:-2], refs[-2], refs[-1]
    n_rows = plan.spheres // 4
    for l in range(plan.here):
        at = plan.here * 3 * n_rows + l
        total = parts[0][at : at + 1, :]
        for p in parts[1:]:
            total = total + p[at : at + 1, :]
        inverse = 1.0 / total
        for c in range(3):
            at = (l * 3 + c) * n_rows
            y = parts[0][at : at + n_rows, :]
            for p in parts[1:]:
                y = y + p[at : at + n_rows, :]
            y = y * inverse
            for j in range(4):
                z = pltpu.roll(y, (LANES - j * W) % LANES, 1) if j else y
                wide[pl.ds(j, n_rows, stride=4), :] = z
            out[l, c] = wide[:, :W]


def finish(plan, parts):
    return pl.pallas_call(
        functools.partial(finish_kernel, plan),
        out_shape=jax.ShapeDtypeStruct((plan.here, 3, plan.spheres, W), jnp.float32),
        in_specs=[VMEM] * len(parts),
        out_specs=VMEM,
        scratch_shapes=[pltpu.VMEM((plan.spheres, LANES), jnp.float32)],
        name="finish",
    )(*parts)


def exchanged(block, axis, k):
    size = lax.axis_size(axis)
    return lax.ppermute(block, axis, [(i, i ^ k) for i in range(size)])


def local(centres, sphere_radius, counts, adjacency):
    here, _, spheres, columns = centres.shape
    plan = Plan(lax.axis_size("robot"), here, spheres, columns)
    *chunks, raw = pack(plan, counts, sphere_radius, adjacency, centres)
    chunks = [chunks[0]] + [exchanged(chunks[k], "robot", k) for k in range(1, plan.group)]
    costs = cost(plan, chunks)
    costs = lax.all_to_all(costs, "robot", 0, 0, tiled=True)
    robot_cost, sums = blend(plan, costs, raw)
    parts = [sums] + [exchanged(sums, "seed", k) for k in range(1, lax.axis_size("seed"))]
    return robot_cost, finish(plan, parts)


def solution(mesh):
    return jax.shard_map(
        local,
        mesh=mesh,
        in_specs=(P("robot", None, None, "seed"), P("robot", None), P("robot"), P("robot", None)),
        out_specs=(P("robot", "seed"), P("robot", None, None, None)),
        check_vma=False,
    )
```

time: 229 us -> 58.9 us (0.26); the launches traced: 232 us -> 58.5 us
  loops' own time: 84.9 us -> 0 us
  local copies, waits for them, and re-layouts: 48.3 us -> 5.22 us
  other arithmetic: 37.4 us -> 0 us
  waiting for transfers between devices: 35.3 us -> 8.93 us
  Pallas kernels: 0 us -> 23.1 us
  blocking collectives: 21.6 us -> 8.44 us
  starting transfers between devices: 3.96 us -> 12.1 us
    another operation x39 -> x0, loops' own time: 84.9 us -> none  [the longest x5 64.3 us: cross_costs(): lax.map(one_pair, jnp.arange(robots_here * arrived_count, dtype=jnp.int32))]
    dynamic_slice x66 -> x0, local copies, waits for them, and re-layouts: 41.1 us -> none  [the longest x26 15.9 us: self_costs(): return lax.map(single, jnp.arange(own_blocks.shape[0], dtype=jnp.int32))]
    reduce_sum x32 -> x0, other arithmetic: 32 us -> none  [the longest x24 31.5 us: tile_cost(): jnp.sum(weights[:, :, None] * jnp.exp(-distance / (spread * spread)), axi...]
    ppermute x13 -> x10, waiting for transfers between devices: 35.3 us -> 8.93 us  [exchanged(): return lax.ppermute(block, axis, [(i, i ^ k) for i in range(size)])]
    pallas_call x0 -> x4, Pallas kernels: none -> 23.1 us  [the longest x1 17.1 us: cost(): pl.pallas_call(functools.partial(cost_kernel, plan), out_shape=jax.ShapeD...]
    psum x1 -> x0, blocking collectives: 21.6 us -> none  [local(): weighted, totals = lax.psum((weighted, totals), 'seed')]
    all_to_all x0 -> x1, blocking collectives: none -> 8.44 us  [local(): costs = lax.all_to_all(costs, 'robot', 0, 0, tiled=True)]
    ppermute x13 -> x10, starting transfers between devices: 3.96 us -> 12.1 us  [exchanged(): return lax.ppermute(block, axis, [(i, i ^ k) for i in range(size)])]
  transfers between devices with their start and end apart: 13 -> 10, of which waited for: 5 -> 4; matrix products, arithmetic and copies ran while one was open for 26% -> 0% of each run, Pallas kernels for 0% -> 0%
where the time goes in v1:
time: 58.9 us; the launch traced here: 58.5 us
  Pallas kernels  23.1 us (39%)
  starting transfers between devices  12.1 us (21%)
  waiting for transfers between devices  8.93 us (15%)
  blocking collectives  8.44 us (14%)
  local copies, waits for them, and re-layouts  5.22 us (9%)
  between operations  0.7 us (1%)
    pallas_call x1, Pallas kernels, cost(): pl.pallas_call(functools.partial(cost_kernel, plan), out_shape=jax.ShapeD...  17.1 us
    ppermute x10, starting transfers between devices, exchanged(): return lax.ppermute(block, axis, [(i, i ^ k) for i in range(size)])  12.1 us
    ppermute x10, waiting for transfers between devices, exchanged(): return lax.ppermute(block, axis, [(i, i ^ k) for i in range(size)])  8.93 us
    all_to_all x1, blocking collectives, local(): costs = lax.all_to_all(costs, 'robot', 0, 0, tiled=True)  8.44 us
    unnamed x22, local copies, waits for them, and re-layouts  5.22 us
    pallas_call x1, Pallas kernels, pack(): pl.pallas_call(functools.partial(pack_kernel, plan), out_shape=[chunk] *...  2.61 us
    pallas_call x1, Pallas kernels, blend(): pl.pallas_call(functools.partial(blend_kernel, plan, seeds_here), out_sha...  1.83 us
    pallas_call x1, Pallas kernels, finish(): pl.pallas_call(functools.partial(finish_kernel, plan), out_shape=jax.Shap...  1.63 us
  transfers between devices with their start and end apart: 10, of which 4 were waited for; matrix products, arithmetic and copies ran while one was open for 0% of the time, Pallas kernels for 0%

profile of v1, /device:TPU:0, one launch (start us, length us, event | category | flops | bytes accessed | tf_op | source)
XLA Modules:
  0.0 58.5 jit_solution(15915468219031429188)
XLA Ops:
  0.6 1.7 %copy.6.centres = f32[2,3,52,256]{3,2,1,0:T(8,128)} copy(f32[2,3,52,256]{3,0,2,1:T(2,128)} %param.4) | data formatting | bytes 638976 | tf_op args[0]
  2.4 2.6 %pack.1 = (f32[112,128]{1,0:T(8,128)}, f32[112,128]{1,0:T(8,128)}, f32[112,128]{1,0:T(8,128)}, f32[112,128]{1,0:T(8,128)}, f32[112,128]{1,0:T(8,128)}, /*index=5...) custom-call(s32[2]{0:T(128)} %counts.1, f32[2,52]{1,0:T(2,128)} %radius.1, ...), custom_call_target="tpu_custom_call" | custom-call | tf_op jit(solution)/shard_map/pack/pallas_call | solution.py:103
  5.0 0.5 collective-permute-start
  5.5 2.5 %collective-permute-start.1 = (f32[112,128]{1,0:T(8,128)}, f32[112,128]{1,0:T(8,128)S(1)}, u32[]{:S(2)}, u32[]{:S(2)}) collective-permute-start(f32[112,128]{1,0:T(8,128)} %get-tuple-element.15), channel_id=1, source_target_pairs={{0,8},{4,12},{8,0},{12,4},{16,24},{20,28},{24,16},{28,20},{1,9},{5... | collective-permute-start | bytes 172040 | tf_op jit(solution)/shard_map/ppermute | solution.py:317
  8.0 0.1 collective-permute-start.2
  8.1 1.8 %collective-permute-start.3 = (f32[112,128]{1,0:T(8,128)}, f32[112,128]{1,0:T(8,128)S(1)}, u32[]{:S(2)}, u32[]{:S(2)}) collective-permute-start(f32[112,128]{1,0:T(8,128)} %get-tuple-element.17), channel_id=1, source_target_pairs={{0,16},{4,20},{8,24},{12,28},{16,0},{20,4},{24,8},{28,12},{1,17},{... | collective-permute-start | bytes 172040 | tf_op jit(solution)/shard_map/ppermute | solution.py:317
  9.8 0.0 collective-permute-start.4
  9.8 0.0 collective-permute-done.refs_1_
  9.8 0.0 copy-start
  9.9 2.6 %collective-permute-start.5 = (f32[112,128]{1,0:T(8,128)}, f32[112,128]{1,0:T(8,128)S(1)}, u32[]{:S(2)}, u32[]{:S(2)}) collective-permute-start(f32[112,128]{1,0:T(8,128)} %get-tuple-element.19), channel_id=1, source_target_pairs={{0,24},{4,28},{8,16},{12,20},{16,8},{20,12},{24,0},{28,4},{1,25},{... | collective-permute-start | bytes 172040 | tf_op jit(solution)/shard_map/ppermute | solution.py:317
  12.4 0.0 collective-permute-done.1.refs_2_
  12.4 0.0 copy-start.1
  12.4 0.3 collective-permute-start.6
  12.7 0.0 collective-permute-done.2.refs_3_
  12.7 0.0 copy-start.2
  12.7 0.0 collective-permute-done.3.refs_4_
  12.7 0.0 copy-start.3
  12.7 2.6 %collective-permute-done.4.refs_5_ = f32[112,128]{1,0:T(8,128)S(1)} collective-permute-done((f32[112,128]{1,0:T(8,128)}, f32[112,128]{1,0:T(8,128)S(1)}, u32[]{:S(2)}, u32[]{:S(2)}) %collective-permute-start.4) | collective-permute-done | bytes 57376 | tf_op jit(solution)/shard_map/ppermute | solution.py:317
  15.3 0.0 copy-start.4
  15.3 0.0 collective-permute-done.5.refs_6_
  15.3 0.0 copy-start.5
  15.3 2.0 %collective-permute-done.6.refs_7_ = f32[112,128]{1,0:T(8,128)S(1)} collective-permute-done((f32[112,128]{1,0:T(8,128)}, f32[112,128]{1,0:T(8,128)S(1)}, u32[]{:S(2)}, u32[]{:S(2)}) %collective-permute-start.6) | collective-permute-done | bytes 57376 | tf_op jit(solution)/shard_map/ppermute | solution.py:317
  17.3 0.0 copy-start.6
  17.3 0.0 copy-done
  17.3 0.0 copy-done.1
  17.3 0.0 copy-done.2
  17.3 0.0 copy-done.3
  17.4 0.0 copy-done.4
  17.4 0.0 copy-done.5
  17.4 0.6 copy-done.6
  17.9 17.1 %cost.1 = f32[16,128]{1,0:T(8,128)} custom-call(f32[112,128]{1,0:T(8,128)} %get-tuple-element.13.refs_0_, f32[112,128]{1,0:T(8,128)} %copy-done, f32[112,128]{1,0:T(8,128)} %copy-done.1, f32[112,128]{1,0:T(8,128)} %copy-done.2, f32[112,128]{1,0:T(8,128)} %copy-done.3, f32[112,128]{1,0:T(8,128)} %copy-done.4, f32[112,128]{1,0:T(8,128)} %copy-done.5, ...), custom_call_target="tpu_custom_call" | custom-call | tf_op jit(solution)/shard_map/cost/pallas_call | solution.py:210
  35.0 8.4 %all_to_all.11 = f32[8,2,128]{2,1,0:T(2,128)} all-to-all(f32[8,2,128]{2,1,0:T(2,128)} %bitcast.2), channel_id=1, replica_groups=mesh['robot'=8,'seed'=4] {'robot'}, dimensions={0} | all-to-all | bytes 16384 | tf_op jit(solution)/shard_map/all_to_all | solution.py:326
  43.5 1.8 %blend.1 = (f32[2,256]{1,0:T(2,128)}, f32[80,128]{1,0:T(8,128)}) custom-call(f32[16,128]{1,0:T(8,128)} %bitcast.3, f32[2,6,52,128]{3,2,1,0:T(8,128)} %get-tuple-element.21.raw), custom_call_target="tpu_custom_call" | custom-call | tf_op jit(solution)/shard_map/blend/pallas_call | solution.py:271
  45.3 3.6 %collective-permute-start.9 = (f32[80,128]{1,0:T(8,128)}, f32[80,128]{1,0:T(8,128)S(1)}, u32[]{:S(2)}, u32[]{:S(2)}) collective-permute-start(f32[80,128]{1,0:T(8,128)} %get-tuple-element.23.refs_0_), channel_id=1, source_target_pairs={{0,3},{1,2},{2,1},{3,0},{4,7},{5,6},{6,5},{7,4},{8,11},{9,10},{10,... | collective-permute-start | bytes 122888 | tf_op jit(solution)/shard_map/ppermute | solution.py:317
  48.9 0.0 collective-permute-start.8
  48.9 0.8 %collective-permute-start.7 = (f32[80,128]{1,0:T(8,128)}, f32[80,128]{1,0:T(8,128)S(1)}, u32[]{:S(2)}, u32[]{:S(2)}) collective-permute-start(f32[80,128]{1,0:T(8,128)} %get-tuple-element.23.refs_0_), channel_id=1, source_target_pairs={{0,1},{1,0},{2,3},{3,2},{4,5},{5,4},{6,7},{7,6},{8,9},{9,8},{10,11... | collective-permute-start | bytes 122888 | tf_op jit(solution)/shard_map/ppermute | solution.py:317
  49.7 1.7 %collective-permute-done.9.refs_3_ = f32[80,128]{1,0:T(8,128)S(1)} collective-permute-done((f32[80,128]{1,0:T(8,128)}, f32[80,128]{1,0:T(8,128)S(1)}, u32[]{:S(2)}, u32[]{:S(2)}) %collective-permute-start.9) | collective-permute-done | bytes 40992 | tf_op jit(solution)/shard_map/ppermute | solution.py:317
  51.4 0.0 copy-start.7
  51.4 2.7 %collective-permute-done.8.refs_2_ = f32[80,128]{1,0:T(8,128)S(1)} collective-permute-done((f32[80,128]{1,0:T(8,128)}, f32[80,128]{1,0:T(8,128)S(1)}, u32[]{:S(2)}, u32[]{:S(2)}) %collective-permute-start.8) | collective-permute-done | bytes 40992 | tf_op jit(solution)/shard_map/ppermute | solution.py:317
  54.0 0.0 copy-start.8
  54.0 0.0 collective-permute-done.7.refs_1_
  54.0 0.0 copy-done.7
  54.0 0.6 %copy-done.8 = f32[80,128]{1,0:T(8,128)} copy-done((f32[80,128]{1,0:T(8,128)}, f32[80,128]{1,0:T(8,128)S(1)}, u32[]{:S(2)}) %copy-start.8) | copy-done | bytes 40984
  54.6 0.0 copy-start.9
  54.6 0.6 %copy-done.9 = f32[80,128]{1,0:T(8,128)} copy-done((f32[80,128]{1,0:T(8,128)}, f32[80,128]{1,0:T(8,128)S(1)}, u32[]{:S(2)}) %copy-start.9) | copy-done | bytes 40984
  55.2 1.6 %finish.1 = f32[2,3,52,32]{3,2,1,0:T(8,128)} custom-call(f32[80,128]{1,0:T(8,128)} %get-tuple-element.23.refs_0_, f32[80,128]{1,0:T(8,128)} %copy-done.9, f32[80,128]{1,0:T(8,128)} %copy-done.8, f32[80,128]{1,0:T(8,128)} %copy-done.7), custom_call_target="tpu_custom_call" | custom-call | tf_op jit(solution)/shard_map/finish/pallas_call | solution.py:305
  56.9 1.7 %copy.7 = f32[2,3,52,32]{2,3,1,0:T(8,128)} copy(f32[2,3,52,32]{3,2,1,0:T(8,128)} %finish.1) | data formatting | bytes 79872
Async XLA Ops:
  5.0 4.9 %collective-permute-start = (f32[112,128]{1,0:T(8,128)}, f32[112,128]{1,0:T(8,128)S(1)}, u32[]{:S(2)}, u32[]{:S(2)}) collective-permute-start(f32[112,128]{1,0:T(8,128)} %get-tuple-element.14), channel_id=1, source_target_pairs={{0,4},{4,0},{8,12},{12,8},{16,20},{20,16},{24,28},{28,24},{1,5},{5... | collective-permute-start | bytes 172040 | tf_op jit(solution)/shard_map/ppermute | solution.py:317
  5.5 6.9 %collective-permute-start.1 = (f32[112,128]{1,0:T(8,128)}, f32[112,128]{1,0:T(8,128)S(1)}, u32[]{:S(2)}, u32[]{:S(2)}) collective-permute-start(f32[112,128]{1,0:T(8,128)} %get-tuple-element.15), channel_id=1, source_target_pairs={{0,8},{4,12},{8,0},{12,4},{16,24},{20,28},{24,16},{28,20},{1,9},{5... | collective-permute-start | bytes 172040 | tf_op jit(solution)/shard_map/ppermute | solution.py:317
  8.0 4.8 %collective-permute-start.2 = (f32[112,128]{1,0:T(8,128)}, f32[112,128]{1,0:T(8,128)S(1)}, u32[]{:S(2)}, u32[]{:S(2)}) collective-permute-start(f32[112,128]{1,0:T(8,128)} %get-tuple-element.16), channel_id=1, source_target_pairs={{0,12},{4,8},{8,4},{12,0},{16,28},{20,24},{24,20},{28,16},{1,13},{... | collective-permute-start | bytes 172040 | tf_op jit(solution)/shard_map/ppermute | solution.py:317
  8.1 4.6 %collective-permute-start.3 = (f32[112,128]{1,0:T(8,128)}, f32[112,128]{1,0:T(8,128)S(1)}, u32[]{:S(2)}, u32[]{:S(2)}) collective-permute-start(f32[112,128]{1,0:T(8,128)} %get-tuple-element.17), channel_id=1, source_target_pairs={{0,16},{4,20},{8,24},{12,28},{16,0},{20,4},{24,8},{28,12},{1,17},{... | collective-permute-start | bytes 172040 | tf_op jit(solution)/shard_map/ppermute | solution.py:317
  9.8 5.5 %collective-permute-start.4 = (f32[112,128]{1,0:T(8,128)}, f32[112,128]{1,0:T(8,128)S(1)}, u32[]{:S(2)}, u32[]{:S(2)}) collective-permute-start(f32[112,128]{1,0:T(8,128)} %get-tuple-element.18), channel_id=1, source_target_pairs={{0,20},{4,16},{8,28},{12,24},{16,4},{20,0},{24,12},{28,8},{1,21},{... | collective-permute-start | bytes 172040 | tf_op jit(solution)/shard_map/ppermute | solution.py:317
  9.8 7.5 %copy-start = (f32[112,128]{1,0:T(8,128)}, f32[112,128]{1,0:T(8,128)S(1)}, u32[]{:S(2)}) copy-start(f32[112,128]{1,0:T(8,128)S(1)} %collective-permute-done.refs_1_) | copy-start | bytes 172036
  9.9 5.5 %collective-permute-start.5 = (f32[112,128]{1,0:T(8,128)}, f32[112,128]{1,0:T(8,128)S(1)}, u32[]{:S(2)}, u32[]{:S(2)}) collective-permute-start(f32[112,128]{1,0:T(8,128)} %get-tuple-element.19), channel_id=1, source_target_pairs={{0,24},{4,28},{8,16},{12,20},{16,8},{20,12},{24,0},{28,4},{1,25},{... | collective-permute-start | bytes 172040 | tf_op jit(solution)/shard_map/ppermute | solution.py:317
  12.4 4.9 %copy-start.1 = (f32[112,128]{1,0:T(8,128)}, f32[112,128]{1,0:T(8,128)S(1)}, u32[]{:S(2)}) copy-start(f32[112,128]{1,0:T(8,128)S(1)} %collective-permute-done.1.refs_2_) | copy-start | bytes 172036
  12.4 4.9 %collective-permute-start.6 = (f32[112,128]{1,0:T(8,128)}, f32[112,128]{1,0:T(8,128)S(1)}, u32[]{:S(2)}, u32[]{:S(2)}) collective-permute-start(f32[112,128]{1,0:T(8,128)} %get-tuple-element.20), channel_id=1, source_target_pairs={{0,28},{4,24},{8,20},{12,16},{16,12},{20,8},{24,4},{28,0},{1,29},{... | collective-permute-start | bytes 172040 | tf_op jit(solution)/shard_map/ppermute | solution.py:317
  12.7 4.6 %copy-start.2 = (f32[112,128]{1,0:T(8,128)}, f32[112,128]{1,0:T(8,128)S(1)}, u32[]{:S(2)}) copy-start(f32[112,128]{1,0:T(8,128)S(1)} %collective-permute-done.2.refs_3_) | copy-start | bytes 172036
  12.7 4.6 %copy-start.3 = (f32[112,128]{1,0:T(8,128)}, f32[112,128]{1,0:T(8,128)S(1)}, u32[]{:S(2)}) copy-start(f32[112,128]{1,0:T(8,128)S(1)} %collective-permute-done.3.refs_4_) | copy-start | bytes 172036
  15.3 2.0 %copy-start.4 = (f32[112,128]{1,0:T(8,128)}, f32[112,128]{1,0:T(8,128)S(1)}, u32[]{:S(2)}) copy-start(f32[112,128]{1,0:T(8,128)S(1)} %collective-permute-done.4.refs_5_) | copy-start | bytes 172036
  15.3 2.0 %copy-start.5 = (f32[112,128]{1,0:T(8,128)}, f32[112,128]{1,0:T(8,128)S(1)}, u32[]{:S(2)}) copy-start(f32[112,128]{1,0:T(8,128)S(1)} %collective-permute-done.5.refs_6_) | copy-start | bytes 172036
  17.3 0.6 %copy-start.6 = (f32[112,128]{1,0:T(8,128)}, f32[112,128]{1,0:T(8,128)S(1)}, u32[]{:S(2)}) copy-start(f32[112,128]{1,0:T(8,128)S(1)} %collective-permute-done.6.refs_7_) | copy-start | bytes 172036
  45.3 6.1 %collective-permute-start.9 = (f32[80,128]{1,0:T(8,128)}, f32[80,128]{1,0:T(8,128)S(1)}, u32[]{:S(2)}, u32[]{:S(2)}) collective-permute-start(f32[80,128]{1,0:T(8,128)} %get-tuple-element.23.refs_0_), channel_id=1, source_target_pairs={{0,3},{1,2},{2,1},{3,0},{4,7},{5,6},{6,5},{7,4},{8,11},{9,10},{10,... | collective-permute-start | bytes 122888 | tf_op jit(solution)/shard_map/ppermute | solution.py:317
  48.9 5.1 %collective-permute-start.8 = (f32[80,128]{1,0:T(8,128)}, f32[80,128]{1,0:T(8,128)S(1)}, u32[]{:S(2)}, u32[]{:S(2)}) collective-permute-start(f32[80,128]{1,0:T(8,128)} %get-tuple-element.23.refs_0_), channel_id=1, source_target_pairs={{0,2},{1,3},{2,0},{3,1},{4,6},{5,7},{6,4},{7,5},{8,10},{9,11},{10,... | collective-permute-start | bytes 122888 | tf_op jit(solution)/shard_map/ppermute | solution.py:317
  48.9 5.1 %collective-permute-start.7 = (f32[80,128]{1,0:T(8,128)}, f32[80,128]{1,0:T(8,128)S(1)}, u32[]{:S(2)}, u32[]{:S(2)}) collective-permute-start(f32[80,128]{1,0:T(8,128)} %get-tuple-element.23.refs_0_), channel_id=1, source_target_pairs={{0,1},{1,0},{2,3},{3,2},{4,5},{5,4},{6,7},{7,6},{8,9},{9,8},{10,11... | collective-permute-start | bytes 122888 | tf_op jit(solution)/shard_map/ppermute | solution.py:317
  51.4 2.7 %copy-start.7 = (f32[80,128]{1,0:T(8,128)}, f32[80,128]{1,0:T(8,128)S(1)}, u32[]{:S(2)}) copy-start(f32[80,128]{1,0:T(8,128)S(1)} %collective-permute-done.9.refs_3_) | copy-start | bytes 122884
  54.0 0.6 %copy-start.8 = (f32[80,128]{1,0:T(8,128)}, f32[80,128]{1,0:T(8,128)S(1)}, u32[]{:S(2)}) copy-start(f32[80,128]{1,0:T(8,128)S(1)} %collective-permute-done.8.refs_2_) | copy-start | bytes 122884
  54.6 0.6 %copy-start.9 = (f32[80,128]{1,0:T(8,128)}, f32[80,128]{1,0:T(8,128)S(1)}, u32[]{:S(2)}) copy-start(f32[80,128]{1,0:T(8,128)S(1)} %collective-permute-done.7.refs_1_) | copy-start | bytes 122884

commit v2 on v1

--- a/solution.py
+++ b/solution.py
@@ -15,6 +15,7 @@
 FAR = 1e15
 VMEM = pl.BlockSpec(memory_space=pltpu.VMEM)
 SMEM = pl.BlockSpec(memory_space=pltpu.SMEM)
+PARAMS = pltpu.CompilerParams(vmem_limit_bytes=16 * 1024 * 1024)
 
 
 def round_up(value, step):
@@ -57,7 +58,8 @@
         for t in range(plan.tiles):
             squares = jnp.zeros((n, LANES), jnp.float32)
             for c in range(3):
-                x = centres[l, c, :, t * LANES : (t + 1) * LANES]
+                at = (c * n * plan.tiles + t) * plan.here + l
+                x = centres[pl.ds(at, n, stride=plan.tiles * plan.here), :]
                 raw[t, l * 3 + c] = x
                 ahead = jnp.where(last, x, pltpu.roll(x, LANES - 1, 1))
                 middle = (0.5 * SCALE) * (x + ahead)
@@ -107,6 +109,7 @@
         in_specs=[SMEM, VMEM, VMEM, VMEM],
         out_specs=[VMEM] * (plan.group + 1),
         scratch_shapes=[pltpu.VMEM((plan.tiles, plan.here * 4, plan.padded, LANES), jnp.float32)],
+        compiler_params=PARAMS,
         name="pack",
     )(counts, radius, adjacency, centres)
 
@@ -218,6 +221,7 @@
             pltpu.SMEM((plan.group, LANES), jnp.float32),
             pltpu.SemaphoreType.DMA((plan.group,)),
         ],
+        compiler_params=PARAMS,
         name="cost",
     )(*chunks)
 
@@ -276,6 +280,7 @@
         ],
         in_specs=[VMEM, VMEM],
         out_specs=[VMEM, VMEM],
+        compiler_params=PARAMS,
         name="blend",
     )(costs, raw)
 
@@ -298,16 +303,17 @@
             for j in range(4):
                 z = pltpu.roll(y, (LANES - j * W) % LANES, 1) if j else y
                 wide[pl.ds(j, n_rows, stride=4), :] = z
-            out[l, c] = wide[:, :W]
+            out[l, c] = wide[...].T[:W]
 
 
 def finish(plan, parts):
     return pl.pallas_call(
         functools.partial(finish_kernel, plan),
-        out_shape=jax.ShapeDtypeStruct((plan.here, 3, plan.spheres, W), jnp.float32),
+        out_shape=jax.ShapeDtypeStruct((plan.here, 3, W, plan.spheres), jnp.float32),
         in_specs=[VMEM] * len(parts),
         out_specs=VMEM,
         scratch_shapes=[pltpu.VMEM((plan.spheres, LANES), jnp.float32)],
+        compiler_params=PARAMS,
         name="finish",
     )(*parts)
 
@@ -320,13 +326,15 @@
 def local(centres, sphere_radius, counts, adjacency):
     here, _, spheres, columns = centres.shape
     plan = Plan(lax.axis_size("robot"), here, spheres, columns)
-    *chunks, raw = pack(plan, counts, sphere_radius, adjacency, centres)
+    stored = centres.reshape(here, 3, spheres, plan.tiles, LANES)
+    stored = stored.transpose(1, 2, 3, 0, 4).reshape(-1, LANES)
+    *chunks, raw = pack(plan, counts, sphere_radius, adjacency, stored)
     chunks = [chunks[0]] + [exchanged(chunks[k], "robot", k) for k in range(1, plan.group)]
     costs = cost(plan, chunks)
     costs = lax.all_to_all(costs, "robot", 0, 0, tiled=True)
     robot_cost, sums = blend(plan, costs, raw)
     parts = [sums] + [exchanged(sums, "seed", k) for k in range(1, lax.axis_size("seed"))]
-    return robot_cost, finish(plan, parts)
+    return robot_cost, finish(plan, parts).transpose(0, 1, 3, 2)
 
 
 def solution(mesh):

time: 58.9 us -> 49.9 us (0.85)
  Pallas kernels: 23.1 us -> 18.4 us
  local copies, waits for them, and re-layouts: 5.22 us -> 2.33 us
  blocking collectives: 8.44 us -> 7.38 us
    unnamed x22 -> x8, local copies, waits for them, and re-layouts: 5.22 us -> 2.33 us
    pallas_call x1, Pallas kernels: 17.1 us -> 15.5 us  [cost(): pl.pallas_call(functools.partial(cost_kernel, plan), out_shape=jax.ShapeD...]
    pallas_call x1, Pallas kernels: 2.61 us -> 1.37 us  [pack(): pl.pallas_call(functools.partial(pack_kernel, plan), out_shape=[chunk] *...]
    pallas_call x1, Pallas kernels: 1.83 us -> 0.71 us  [blend(): pl.pallas_call(functools.partial(blend_kernel, plan, seeds_here), out_sha...]
    all_to_all x1, blocking collectives: 8.44 us -> 7.38 us  [local(): costs = lax.all_to_all(costs, 'robot', 0, 0, tiled=True)]
    pallas_call x1, Pallas kernels: 1.63 us -> 0.85 us  [finish(): pl.pallas_call(functools.partial(finish_kernel, plan), out_shape=jax.Shap...]
  transfers between devices with their start and end apart: 10 -> 10, of which waited for: 4 -> 5; matrix products, arithmetic and copies ran while one was open for 0% -> 0% of each run, Pallas kernels for 0% -> 0%
where the time goes in v2:
time: 49.9 us; the launch traced here: 49.7 us
  Pallas kernels  18.4 us (37%)
  starting transfers between devices  12.1 us (24%)
  waiting for transfers between devices  8.8 us (18%)
  blocking collectives  7.38 us (15%)
  local copies, waits for them, and re-layouts  2.33 us (5%)
  between operations  0.68 us (1%)
    pallas_call x1, Pallas kernels, cost(): pl.pallas_call(functools.partial(cost_kernel, plan), out_shape=jax.ShapeD...  15.5 us
    ppermute x10, starting transfers between devices, exchanged(): return lax.ppermute(block, axis, [(i, i ^ k) for i in range(size)])  12.1 us
    ppermute x10, waiting for transfers between devices, exchanged(): return lax.ppermute(block, axis, [(i, i ^ k) for i in range(size)])  8.8 us
    all_to_all x1, blocking collectives, local(): costs = lax.all_to_all(costs, 'robot', 0, 0, tiled=True)  7.38 us
    unnamed x8, local copies, waits for them, and re-layouts  2.33 us
    pallas_call x1, Pallas kernels, pack(): pl.pallas_call(functools.partial(pack_kernel, plan), out_shape=[chunk] *...  1.37 us
  transfers between devices with their start and end apart: 10, of which 5 were waited for; matrix products, arithmetic and copies ran while one was open for 0% of the time, Pallas kernels for 0%

profile of v2, /device:TPU:0, one launch (start us, length us, event | category | flops | bytes accessed | tf_op | source)
XLA Modules:
  0.0 49.7 jit_solution(8135176503371381005)
XLA Ops:
  0.6 0.0 copy-start.3
  0.6 0.0 copy-start.1
  0.7 0.6 %copy-done.3 = s32[2]{0:T(128)S(1)} copy-done((s32[2]{0:T(128)S(1)}, s32[2]{0:T(128)}, u32[]{:S(2)}) %copy-start.3) | copy-done | bytes 32
  1.3 0.0 copy-done.1
  1.3 0.0 copy-start
  1.3 1.0 %copy-done = f32[2,3,52,256]{3,0,2,1:T(2,128)S(1)} copy-done((f32[2,3,52,256]{3,0,2,1:T(2,128)S(1)}, f32[2,3,52,256]{3,0,2,1:T(2,128)}, u32[]{:S(2)}) %copy-start) | copy-done | bytes 319512
  2.3 0.0 copy-start.2
  2.3 0.7 %copy-done.2 = s32[2,16]{1,0:T(2,128)S(1)} copy-done((s32[2,16]{1,0:T(2,128)S(1)}, s32[2,16]{1,0:T(2,128)}, u32[]{:S(2)}) %copy-start.2) | copy-done | bytes 152
  3.0 1.4 %pack.1 = (f32[112,128]{1,0:T(8,128)S(1)}, f32[112,128]{1,0:T(8,128)S(1)}, f32[112,128]{1,0:T(8,128)S(1)}, f32[112,128]{1,0:T(8,128)S(1)}, f32[112,128]{1,0:T(8,...) custom-call(s32[2]{0:T(128)S(1)} %copy-done.3, ...), custom_call_target="tpu_custom_call" | custom-call | tf_op jit(solution)/shard_map/pack/pallas_call | solution.py:105
  4.4 0.6 %collective-permute-start = (f32[112,128]{1,0:T(8,128)S(1)}, f32[112,128]{1,0:T(8,128)S(1)}, u32[]{:S(2)}, u32[]{:S(2)}) collective-permute-start(f32[112,128]{1,0:T(8,128)S(1)} %get-tuple-element.14), channel_id=1, source_target_pairs={{0,4},{4,0},{8,12},{12,8},{16,20},{20,16},{24,28},{28,24},{1,5},{5... | collective-permute-start | bytes 172040 | tf_op jit(solution)/shard_map/ppermute | solution.py:323
  4.9 2.6 %collective-permute-start.1 = (f32[112,128]{1,0:T(8,128)S(1)}, f32[112,128]{1,0:T(8,128)S(1)}, u32[]{:S(2)}, u32[]{:S(2)}) collective-permute-start(f32[112,128]{1,0:T(8,128)S(1)} %get-tuple-element.15), channel_id=1, source_target_pairs={{0,8},{4,12},{8,0},{12,4},{16,24},{20,28},{24,16},{28,20},{1,9},{5... | collective-permute-start | bytes 172040 | tf_op jit(solution)/shard_map/ppermute | solution.py:323
  7.5 0.0 collective-permute-start.2
  7.5 1.8 %collective-permute-start.3 = (f32[112,128]{1,0:T(8,128)S(1)}, f32[112,128]{1,0:T(8,128)S(1)}, u32[]{:S(2)}, u32[]{:S(2)}) collective-permute-start(f32[112,128]{1,0:T(8,128)S(1)} %get-tuple-element.17), channel_id=1, source_target_pairs={{0,16},{4,20},{8,24},{12,28},{16,0},{20,4},{24,8},{28,12},{1,17},{... | collective-permute-start | bytes 172040 | tf_op jit(solution)/shard_map/ppermute | solution.py:323
  9.3 0.0 collective-permute-start.4
  9.3 0.0 collective-permute-done.refs_1_
  9.3 2.6 %collective-permute-start.5 = (f32[112,128]{1,0:T(8,128)S(1)}, f32[112,128]{1,0:T(8,128)S(1)}, u32[]{:S(2)}, u32[]{:S(2)}) collective-permute-start(f32[112,128]{1,0:T(8,128)S(1)} %get-tuple-element.19), channel_id=1, source_target_pairs={{0,24},{4,28},{8,16},{12,20},{16,8},{20,12},{24,0},{28,4},{1,25},{... | collective-permute-start | bytes 172040 | tf_op jit(solution)/shard_map/ppermute | solution.py:323
  11.9 0.0 collective-permute-done.1.refs_2_
  11.9 0.1 collective-permute-start.6
  12.0 0.0 collective-permute-done.2.refs_3_
  12.0 0.0 collective-permute-done.3.refs_4_
  12.0 1.2 %collective-permute-done.4.refs_5_ = f32[112,128]{1,0:T(8,128)S(1)} collective-permute-done((f32[112,128]{1,0:T(8,128)S(1)}, f32[112,128]{1,0:T(8,128)S(1)}, u32[]{:S(2)}, u32[]{:S(2)}) %collective-permute-start.4) | collective-permute-done | bytes 57376 | tf_op jit(solution)/shard_map/ppermute | solution.py:323
  13.2 1.3 %collective-permute-done.5.refs_6_ = f32[112,128]{1,0:T(8,128)S(1)} collective-permute-done((f32[112,128]{1,0:T(8,128)S(1)}, f32[112,128]{1,0:T(8,128)S(1)}, u32[]{:S(2)}, u32[]{:S(2)}) %collective-permute-start.5) | collective-permute-done | bytes 57376 | tf_op jit(solution)/shard_map/ppermute | solution.py:323
  14.5 2.2 %collective-permute-done.6.refs_7_ = f32[112,128]{1,0:T(8,128)S(1)} collective-permute-done((f32[112,128]{1,0:T(8,128)S(1)}, f32[112,128]{1,0:T(8,128)S(1)}, u32[]{:S(2)}, u32[]{:S(2)}) %collective-permute-start.6) | collective-permute-done | bytes 57376 | tf_op jit(solution)/shard_map/ppermute | solution.py:323
  16.7 15.5 %cost.1 = f32[16,128]{1,0:T(8,128)S(1)} custom-call(f32[112,128]{1,0:T(8,128)S(1)} %get-tuple-element.13.refs_0_, f32[112,128]{1,0:T(8,128)S(1)} %collective-permute-done.refs_1_, f32[112,128]{1,0:T(8,128)S(1)} %collective-permute-done.1.refs_2_, f32[112,128]{1,0:T(8,128)S(1)} %collective-permute-done.2.refs_3_, ...), custom_call_target="tpu_custom_call" | custom-call | tf_op jit(solution)/shard_map/cost/pallas_call | solution.py:213
  32.2 7.4 %all_to_all.11 = f32[8,2,128]{2,1,0:T(2,128)S(1)} all-to-all(f32[8,2,128]{2,1,0:T(2,128)S(1)} %bitcast.9), channel_id=1, replica_groups=mesh['robot'=8,'seed'=4] {'robot'}, dimensions={0} | all-to-all | bytes 16384 | tf_op jit(solution)/shard_map/all_to_all | solution.py:334
  39.6 0.7 %blend.1 = (f32[2,256]{1,0:T(2,128)}, f32[80,128]{1,0:T(8,128)S(1)}) custom-call(f32[16,128]{1,0:T(8,128)S(1)} %bitcast.10, f32[2,6,52,128]{3,2,1,0:T(8,128)S(1)} %get-tuple-element.21.raw), custom_call_target="tpu_custom_call" | custom-call | tf_op jit(solution)/shard_map/blend/pallas_call | solution.py:275
  40.3 3.6 %collective-permute-start.9 = (f32[80,128]{1,0:T(8,128)S(1)}, f32[80,128]{1,0:T(8,128)S(1)}, u32[]{:S(2)}, u32[]{:S(2)}) collective-permute-start(f32[80,128]{1,0:T(8,128)S(1)} %get-tuple-element.23.refs_0_), channel_id=1, source_target_pairs={{0,3},{1,2},{2,1},{3,0},{4,7},{5,6},{6,5},{7,4},{8,11},{9,10},{10,... | collective-permute-start | bytes 122888 | tf_op jit(solution)/shard_map/ppermute | solution.py:323
  43.9 0.0 collective-permute-start.8
  43.9 0.8 %collective-permute-start.7 = (f32[80,128]{1,0:T(8,128)S(1)}, f32[80,128]{1,0:T(8,128)S(1)}, u32[]{:S(2)}, u32[]{:S(2)}) collective-permute-start(f32[80,128]{1,0:T(8,128)S(1)} %get-tuple-element.23.refs_0_), channel_id=1, source_target_pairs={{0,1},{1,0},{2,3},{3,2},{4,5},{5,4},{6,7},{7,6},{8,9},{9,8},{10,11... | collective-permute-start | bytes 122888 | tf_op jit(solution)/shard_map/ppermute | solution.py:323
  44.7 1.6 %collective-permute-done.9.refs_3_ = f32[80,128]{1,0:T(8,128)S(1)} collective-permute-done((f32[80,128]{1,0:T(8,128)S(1)}, f32[80,128]{1,0:T(8,128)S(1)}, u32[]{:S(2)}, u32[]{:S(2)}) %collective-permute-start.9) | collective-permute-done | bytes 40992 | tf_op jit(solution)/shard_map/ppermute | solution.py:323
  46.3 2.5 %collective-permute-done.8.refs_2_ = f32[80,128]{1,0:T(8,128)S(1)} collective-permute-done((f32[80,128]{1,0:T(8,128)S(1)}, f32[80,128]{1,0:T(8,128)S(1)}, u32[]{:S(2)}, u32[]{:S(2)}) %collective-permute-start.8) | collective-permute-done | bytes 40992 | tf_op jit(solution)/shard_map/ppermute | solution.py:323
  48.8 0.0 collective-permute-done.7.refs_1_
  48.8 0.9 %finish.1 = f32[2,3,32,52]{3,2,1,0:T(8,128)} custom-call(f32[80,128]{1,0:T(8,128)S(1)} %get-tuple-element.23.refs_0_, f32[80,128]{1,0:T(8,128)S(1)} %collective-permute-done.7.refs_1_, f32[80,128]{1,0:T(8,128)S(1)} %collective-permute-done.8.refs_2_, f32[80,128]{1,0:T(8,128)S(1)} %collective-permute-done.9.refs_3_), custom_call_target="tpu_custom_call" | custom-call | tf_op jit(solution)/shard_map/finish/pallas_call | solution.py:310
Async XLA Ops:
  0.6 0.7 %copy-start.3 = (s32[2]{0:T(128)S(1)}, s32[2]{0:T(128)}, u32[]{:S(2)}) copy-start(s32[2]{0:T(128)} %counts.1) | copy-start | bytes 28
  0.6 0.7 %copy-start.1 = (f32[2,52]{1,0:T(2,128)S(1)}, f32[2,52]{1,0:T(2,128)}, u32[]{:S(2)}) copy-start(f32[2,52]{1,0:T(2,128)} %radius.1) | copy-start | bytes 1252
  1.3 1.0 %copy-start = (f32[2,3,52,256]{3,0,2,1:T(2,128)S(1)}, f32[2,3,52,256]{3,0,2,1:T(2,128)}, u32[]{:S(2)}) copy-start(f32[2,3,52,256]{3,0,2,1:T(2,128)} %param.4) | copy-start | bytes 958468
  2.3 0.7 %copy-start.2 = (s32[2,16]{1,0:T(2,128)S(1)}, s32[2,16]{1,0:T(2,128)}, u32[]{:S(2)}) copy-start(s32[2,16]{1,0:T(2,128)} %adjacency.1) | copy-start | bytes 388
  4.4 4.9 %collective-permute-start = (f32[112,128]{1,0:T(8,128)S(1)}, f32[112,128]{1,0:T(8,128)S(1)}, u32[]{:S(2)}, u32[]{:S(2)}) collective-permute-start(f32[112,128]{1,0:T(8,128)S(1)} %get-tuple-element.14), channel_id=1, source_target_pairs={{0,4},{4,0},{8,12},{12,8},{16,20},{20,16},{24,28},{28,24},{1,5},{5... | collective-permute-start | bytes 172040 | tf_op jit(solution)/shard_map/ppermute | solution.py:323
  4.9 7.0 %collective-permute-start.1 = (f32[112,128]{1,0:T(8,128)S(1)}, f32[112,128]{1,0:T(8,128)S(1)}, u32[]{:S(2)}, u32[]{:S(2)}) collective-permute-start(f32[112,128]{1,0:T(8,128)S(1)} %get-tuple-element.15), channel_id=1, source_target_pairs={{0,8},{4,12},{8,0},{12,4},{16,24},{20,28},{24,16},{28,20},{1,9},{5... | collective-permute-start | bytes 172040 | tf_op jit(solution)/shard_map/ppermute | solution.py:323
  7.5 4.6 %collective-permute-start.2 = (f32[112,128]{1,0:T(8,128)S(1)}, f32[112,128]{1,0:T(8,128)S(1)}, u32[]{:S(2)}, u32[]{:S(2)}) collective-permute-start(f32[112,128]{1,0:T(8,128)S(1)} %get-tuple-element.16), channel_id=1, source_target_pairs={{0,12},{4,8},{8,4},{12,0},{16,28},{20,24},{24,20},{28,16},{1,13},{... | collective-permute-start | bytes 172040 | tf_op jit(solution)/shard_map/ppermute | solution.py:323
  7.5 4.5 %collective-permute-start.3 = (f32[112,128]{1,0:T(8,128)S(1)}, f32[112,128]{1,0:T(8,128)S(1)}, u32[]{:S(2)}, u32[]{:S(2)}) collective-permute-start(f32[112,128]{1,0:T(8,128)S(1)} %get-tuple-element.17), channel_id=1, source_target_pairs={{0,16},{4,20},{8,24},{12,28},{16,0},{20,4},{24,8},{28,12},{1,17},{... | collective-permute-start | bytes 172040 | tf_op jit(solution)/shard_map/ppermute | solution.py:323
  9.3 4.0 %collective-permute-start.4 = (f32[112,128]{1,0:T(8,128)S(1)}, f32[112,128]{1,0:T(8,128)S(1)}, u32[]{:S(2)}, u32[]{:S(2)}) collective-permute-start(f32[112,128]{1,0:T(8,128)S(1)} %get-tuple-element.18), channel_id=1, source_target_pairs={{0,20},{4,16},{8,28},{12,24},{16,4},{20,0},{24,12},{28,8},{1,21},{... | collective-permute-start | bytes 172040 | tf_op jit(solution)/shard_map/ppermute | solution.py:323
  9.3 5.2 %collective-permute-start.5 = (f32[112,128]{1,0:T(8,128)S(1)}, f32[112,128]{1,0:T(8,128)S(1)}, u32[]{:S(2)}, u32[]{:S(2)}) collective-permute-start(f32[112,128]{1,0:T(8,128)S(1)} %get-tuple-element.19), channel_id=1, source_target_pairs={{0,24},{4,28},{8,16},{12,20},{16,8},{20,12},{24,0},{28,4},{1,25},{... | collective-permute-start | bytes 172040 | tf_op jit(solution)/shard_map/ppermute | solution.py:323
  11.9 4.8 %collective-permute-start.6 = (f32[112,128]{1,0:T(8,128)S(1)}, f32[112,128]{1,0:T(8,128)S(1)}, u32[]{:S(2)}, u32[]{:S(2)}) collective-permute-start(f32[112,128]{1,0:T(8,128)S(1)} %get-tuple-element.20), channel_id=1, source_target_pairs={{0,28},{4,24},{8,20},{12,16},{16,12},{20,8},{24,4},{28,0},{1,29},{... | collective-permute-start | bytes 172040 | tf_op jit(solution)/shard_map/ppermute | solution.py:323
  40.3 6.0 %collective-permute-start.9 = (f32[80,128]{1,0:T(8,128)S(1)}, f32[80,128]{1,0:T(8,128)S(1)}, u32[]{:S(2)}, u32[]{:S(2)}) collective-permute-start(f32[80,128]{1,0:T(8,128)S(1)} %get-tuple-element.23.refs_0_), channel_id=1, source_target_pairs={{0,3},{1,2},{2,1},{3,0},{4,7},{5,6},{6,5},{7,4},{8,11},{9,10},{10,... | collective-permute-start | bytes 122888 | tf_op jit(solution)/shard_map/ppermute | solution.py:323
  43.9 4.9 %collective-permute-start.8 = (f32[80,128]{1,0:T(8,128)S(1)}, f32[80,128]{1,0:T(8,128)S(1)}, u32[]{:S(2)}, u32[]{:S(2)}) collective-permute-start(f32[80,128]{1,0:T(8,128)S(1)} %get-tuple-element.23.refs_0_), channel_id=1, source_target_pairs={{0,2},{1,3},{2,0},{3,1},{4,6},{5,7},{6,4},{7,5},{8,10},{9,11},{10,... | collective-permute-start | bytes 122888 | tf_op jit(solution)/shard_map/ppermute | solution.py:323
  43.9 4.9 %collective-permute-start.7 = (f32[80,128]{1,0:T(8,128)S(1)}, f32[80,128]{1,0:T(8,128)S(1)}, u32[]{:S(2)}, u32[]{:S(2)}) collective-permute-start(f32[80,128]{1,0:T(8,128)S(1)} %get-tuple-element.23.refs_0_), channel_id=1, source_target_pairs={{0,1},{1,0},{2,3},{3,2},{4,5},{5,4},{6,7},{7,6},{8,9},{9,8},{10,11... | collective-permute-start | bytes 122888 | tf_op jit(solution)/shard_map/ppermute | solution.py:323

commit v3 on v2

v3 whole, which is shorter than its diff:
```python
import functools
import math

import jax
import jax.numpy as jnp
from jax import lax
from jax.experimental import pallas as pl
from jax.experimental.pallas import tpu as pltpu
from jax.sharding import PartitionSpec as P

W = 32
LANES = 128
SUB = 8
SCALE = math.sqrt(math.log2(math.e))
FAR = 1e15
VMEM = pl.BlockSpec(memory_space=pltpu.VMEM)
SMEM = pl.BlockSpec(memory_space=pltpu.SMEM)
PARAMS = pltpu.CompilerParams(vmem_limit_bytes=16 * 1024 * 1024)


def round_up(value, step):
    return -(-value // step) * step


class Plan:
    def __init__(self, group, robots_here, spheres, columns):
        self.group = group
        self.chips = group // 2
        self.here = robots_here
        self.spheres = spheres
        self.columns = columns
        self.width = columns // group
        self.lane_groups = LANES // self.width
        self.rows = -(-spheres // self.lane_groups)
        self.padded = self.rows * self.lane_groups
        self.parts = -(-self.rows // SUB)
        self.slots = group * robots_here
        self.halves = -(-self.slots // 16)
        self.sweep_late = self.width % W == 0
        self.fields = 3 if self.sweep_late else 4
        self.data_rows = robots_here * self.fields * self.rows
        self.chunk_rows = round_up(self.data_rows + robots_here, SUB)
        self.tiles = columns // LANES


def iota(shape, axis):
    return lax.broadcasted_iota(jnp.int32, shape, axis)


def sweep(points, last, radius):
    squares = None
    middles = []
    for x in points:
        ahead = jnp.where(last, x, pltpu.roll(x, LANES - 1, 1))
        middles.append((0.5 * SCALE) * (x + ahead))
        square = (ahead - x) * (ahead - x)
        squares = square if squares is None else squares + square
    return middles, radius + 0.5 * jnp.sqrt(squares + 1e-06)


def pack_kernel(plan, counts, radius, adjacency, stored, mine, theirs, source):
    me = lax.axis_index("robot")
    n, g, rows, width = plan.spheres, plan.lane_groups, plan.rows, plan.width
    step = plan.tiles * plan.here
    order = iota((n, LANES), 0)
    for l in range(plan.here):
        for t in range(plan.tiles):
            points = [
                stored[pl.ds(c * n * step + t * plan.here + l, n, stride=step), :] for c in range(3)
            ]
            if not plan.sweep_late:
                diagonal = iota((n, n), 0) == iota((n, n), 1)
                column = jnp.sum(
                    jnp.where(diagonal, radius[l : l + 1, :], 0.0), axis=1, keepdims=True
                )
                points, swept = sweep(points, iota((n, LANES), 1) % W == W - 1, column)
                robot = me * plan.here + l
                off = FAR * (1 + order + plan.padded * robot).astype(jnp.float32)
                points[0] = jnp.where(order < counts[l], points[0], off)
                points.append(swept)
                spare = plan.padded - n
                if spare:
                    index = n + iota((spare, LANES), 0) + plan.padded * robot
                    fill = FAR * (1 + index).astype(jnp.float32)
                    for c in range(4):
                        source[t, l * 4 + c, n:, :] = fill if c == 0 else jnp.ones_like(fill)
            for c, x in enumerate(points):
                source[t, l * plan.fields + c, 0:n, :] = x
    lane = iota((1, LANES), 1)
    links = iota((1, plan.slots), 1)
    heads = []
    for l in range(plan.here):
        head = jnp.where(lane == n, counts[l].astype(jnp.float32), 0.0)
        for h in range(plan.halves):
            bits = jnp.where(
                (adjacency[l : l + 1, :] != 0) & (links // 16 == h), 1 << (links % 16), 0
            ).astype(jnp.float32)
            head = jnp.where(lane == n + 1 + h, jnp.sum(bits, axis=1, keepdims=True), head)
        heads.append(head)
    lane_group = iota((rows, LANES), 1) // width
    for k in range(plan.group):
        out = (mine, theirs)[k % 2]
        dest = me ^ k
        tile = dest // g
        spot = dest % g
        for f in range(plan.here * plan.fields):
            y = jnp.zeros((rows, LANES), jnp.float32)
            for j in range(g):
                x = source[tile, f, pl.ds(j, rows, stride=g), :]
                x = pltpu.roll(x, ((j + g - spot) % g) * width, 1)
                y = jnp.where(lane_group == j, x, y)
            out[k // 2, f * rows : (f + 1) * rows, :] = y
        for l in range(plan.here):
            at = plan.data_rows + l
            out[k // 2, at : at + 1, :] = heads[l]
            out[k // 2, at : at + 1, 0:n] = radius[l : l + 1, :]


def pack(plan, counts, radius, adjacency, stored):
    half = jax.ShapeDtypeStruct((plan.chips, plan.chunk_rows, LANES), jnp.float32)
    return pl.pallas_call(
        functools.partial(pack_kernel, plan),
        out_shape=[half, half],
        in_specs=[SMEM, VMEM, VMEM, VMEM],
        out_specs=[VMEM, VMEM],
        scratch_shapes=[
            pltpu.VMEM((plan.tiles, plan.here * plan.fields, plan.padded, LANES), jnp.float32)
        ],
        compiler_params=PARAMS,
        name="pack",
    )(counts, radius, adjacency, stored)


def join_kernel(plan, mine, theirs, *outs):
    for k in range(plan.chips):
        outs[k][0] = mine[k]
        outs[k][1] = theirs[k]


def join(plan, mine, theirs):
    pair = jax.ShapeDtypeStruct((2, plan.chunk_rows, LANES), jnp.float32)
    return pl.pallas_call(
        functools.partial(join_kernel, plan),
        out_shape=[pair] * plan.chips,
        in_specs=[VMEM, VMEM],
        out_specs=[VMEM] * plan.chips,
        compiler_params=PARAMS,
        name="join",
    )(mine, theirs)


def term(first, second):
    gap = first[0] - second[0]
    square = gap * gap
    for c in (1, 2):
        gap = first[c] - second[c]
        square = square + gap * gap
    inverse = 1.0 / (first[3] + second[3])
    return jnp.exp2(-(square * (inverse * inverse)))


def masked(value, keep):
    return value if keep is None else jnp.where(keep, value, 0.0)


def cost_kernel(plan, stage, *refs):
    chunks, refs = refs[: stage + 1], refs[stage + 1 :]
    known, refs = refs[:stage], refs[stage:]
    before, refs = refs[: 1 if stage else 0], refs[1 if stage else 0 :]
    ends = stage == plan.chips - 1
    if ends:
        out, blocks, packed, sums, totals, names, starts = refs
    else:
        blocks, totals, packed, sums, names, starts = refs
    me = lax.axis_index("robot")
    g, rows, width, here, n = plan.lane_groups, plan.rows, plan.width, plan.here, plan.spheres
    parts, fresh = plan.parts, 2 * plan.here
    first_slot = stage * fresh
    deep = parts * SUB

    def line_of(slot):
        at = plan.data_rows + slot % here
        return chunks[slot // fresh][slot % fresh // here, at : at + 1, :]

    for u in range(first_slot + fresh):
        count = line_of(u)[0, n].astype(jnp.int32)
        starts[u] = jnp.minimum((count + g - 1) // g, rows)
    for i in range(fresh):
        line = line_of(first_slot + i)
        links = [line[0, n + 1 + h].astype(jnp.int32) for h in range(plan.halves)]
        for k in range(stage + 1):
            found = jnp.int32(0)
            for v in range(fresh if k < stage else i):
                robot = (k * fresh + v) ^ (me * here)
                mask = links[0]
                for h in range(1, plan.halves):
                    mask = jnp.where(robot // 16 == h, links[h], mask)
                names[k, i, found] = v
                found = found + ((mask >> (robot % 16)) & 1)
            names[k, i, fresh] = found

    sphere = iota((rows, LANES), 0) * g + iota((rows, LANES), 1) // width
    last = iota((rows, LANES), 1) % W == W - 1
    for i in range(fresh):
        slot = first_slot + i
        chunk = chunks[stage].at[i // here]
        at = i % here * plan.fields * rows
        fields = [chunk[at + f * rows : at + (f + 1) * rows, :] for f in range(plan.fields)]
        if plan.sweep_late:
            line = line_of(slot)
            wide = jnp.broadcast_to(line, (SUB, LANES))
            pick = iota((SUB, LANES), 0) * g + iota((SUB, LANES), 1) // width
            radius = [
                jnp.take_along_axis(
                    wide, jnp.minimum(pick + p * SUB * g, LANES - 1), axis=1,
                    mode="promise_in_bounds",
                )
                for p in range(parts)
            ]
            fields, swept = sweep(fields, last, jnp.concatenate(radius, axis=0)[:rows])
            count = line[:, n : n + 1].astype(jnp.int32)
            off = FAR * (1 + sphere + plan.padded * slot).astype(jnp.float32)
            fields[0] = jnp.where(sphere < count, fields[0], off)
            fields.append(swept)
        for c in range(4):
            for m in range(g):
                x = fields[c]
                blocks[i, c, m, 0:rows, :] = pltpu.roll(x, m * width, 1) if m else x
            if deep > rows:
                fill = -FAR if c == 0 else 1.0
                blocks[i, c, 0, rows:deep, :] = jnp.full((deep - rows, LANES), fill, jnp.float32)
    for u in range(first_slot):
        totals[u] = before[0][u]
    for i in range(fresh):
        totals[first_slot + i] = jnp.zeros((SUB, LANES), jnp.float32)

    def row(i, m, r):
        return [blocks[i, c, m, r : r + 1, :] for c in range(4)]

    def part(i, m, p):
        return [blocks[i, c, m, p * SUB : (p + 1) * SUB, :] for c in range(4)]

    sub = iota((SUB, LANES), 0)
    lane_group = iota((SUB, LANES), 1) // width

    def self_terms(u, high):
        total = jnp.zeros((SUB, LANES), jnp.float32)
        second = part(u, 0, 0)
        turned = second
        for d in range(SUB // 2 + 1):
            if d:
                turned = [pltpu.roll(x, SUB - d, 0) for x in second]
            low = (sub + d) % SUB
            for m in range(g):
                other = (lane_group + g - m) % g
                if d == 0:
                    if m < 2:
                        continue
                    keep = lane_group >= m
                elif d == 1 and m == 1:
                    keep = jnp.abs((low - sub) * g + lane_group - other) >= 2
                elif 2 * d == SUB:
                    keep = sub < d
                else:
                    keep = None
                total = total + masked(term(part(u, m, 0), turned), keep)
        for r in range(SUB, high):
            for p in range(parts):
                if p * SUB > r:
                    continue
                second = part(u, 0, p)
                for m in range(g):
                    other = (lane_group + g - m) % g
                    ahead = (r - p * SUB - sub) * g + other - lane_group
                    near = r < (p + 1) * SUB + 1
                    total = total + masked(term(row(u, m, r), second), ahead >= 2 if near else None)
        return total

    def with_rows(u, trips, high):
        total = self_terms(u, high)

        def trip(j, total):
            at = pl.multiple_of(j * SUB, SUB)
            second = [packed[c, pl.ds(at, SUB), :] for c in range(4)]
            value = jnp.zeros((SUB, LANES), jnp.float32)
            for r in range(high):
                for m in range(g):
                    value = value + term(row(u, m, r), second)
            sums[pl.ds(at, SUB), :] = value
            return total + value

        totals[first_slot + u] = totals[first_slot + u] + lax.fori_loop(0, trips, trip, total)

    lowest = max(1, -(-(n // 2) // g))

    def choose(u, trips, low, high):
        if low == high:
            with_rows(u, trips, high)
            return
        middle = (low + high) // 2

        @pl.when(starts[first_slot + u] <= middle)
        def _():
            choose(u, trips, low, middle)

        @pl.when(starts[first_slot + u] > middle)
        def _():
            choose(u, trips, middle + 1, high)

    @pl.loop(0, fresh)
    def _(u):
        filled = jnp.int32(0)
        for k in range(stage + 1):

            def gather(e, filled, k=k):
                v = names[k, u, e]
                for c in range(4):
                    packed[c, pl.ds(filled, deep), :] = (known[k] if k < stage else blocks)[v, c, 0]
                return filled + starts[k * fresh + v]

            filled = lax.fori_loop(0, names[k, u, fresh], gather, filled)
        for c in range(4):
            fill = -FAR if c == 0 else 1.0
            packed[c, pl.ds(filled, SUB), :] = jnp.full((SUB, LANES), fill, jnp.float32)
        choose(u, (filled + SUB - 1) // SUB, lowest, rows)

        filled = jnp.int32(0)
        for k in range(stage + 1):

            def hand_out(e, filled, k=k):
                v = k * fresh + names[k, u, e]
                value = totals[v]
                for p in range(parts):
                    line = sums[pl.ds(filled + p * SUB, SUB), :]
                    value = value + jnp.where(sub + p * SUB < starts[v], line, 0.0)
                totals[v] = value
                return filled + starts[v]

            filled = lax.fori_loop(0, names[k, u, fresh], hand_out, filled)

    if not ends:
        return
    spot = iota((1, LANES), 1) // width == me % g
    for k in range(plan.group):
        for l in range(here):
            value = jnp.sum(totals[k * here + l], axis=0, keepdims=True)
            shift = width
            while shift < LANES:
                value = value + pltpu.roll(value, shift, 1)
                shift *= 2
            value = jnp.where(spot, value, 0.0) / (n * n)
            out[pl.ds((me ^ k) * here + l, 1), :] = value


def cost(plan, stage, chunks, known, before):
    fresh, g = 2 * plan.here, plan.lane_groups
    slots = (stage + 1) * fresh
    deep = plan.parts * SUB
    long = round_up(slots * plan.rows + deep + SUB, SUB)
    block = (fresh, 4, g, deep, LANES)
    total = (slots, SUB, LANES)
    ends = stage == plan.chips - 1
    if ends:
        out_shape = [jax.ShapeDtypeStruct((slots, LANES), jnp.float32)]
    else:
        out_shape = [jax.ShapeDtypeStruct(shape, jnp.float32) for shape in (block, total)]
    return pl.pallas_call(
        functools.partial(cost_kernel, plan, stage),
        out_shape=out_shape,
        in_specs=[VMEM] * (len(chunks) + len(known) + len(before)),
        out_specs=[VMEM] * len(out_shape),
        scratch_shapes=([pltpu.VMEM(block, jnp.float32)] if ends else [])
        + [pltpu.VMEM((4, long, LANES), jnp.float32), pltpu.VMEM((long, LANES), jnp.float32)]
        + ([pltpu.VMEM(total, jnp.float32)] if ends else [])
        + [
            pltpu.SMEM((stage + 1, fresh, fresh + 1), jnp.int32),
            pltpu.SMEM((slots,), jnp.int32),
        ],
        compiler_params=PARAMS,
        cost_estimate=pl.CostEstimate(
            flops=20_000_000 * (stage + 1), bytes_accessed=1000, transcendentals=0
        ),
        name=f"cost{stage}",
    )(*chunks, *known, *before)


def blend_kernel(plan, seeds_here, costs, stored, cost_out, sums):
    n, here, g = plan.spheres, plan.here, plan.lane_groups
    n_rows = n // 4
    step = plan.tiles * here
    seed_of = iota((seeds_here, LANES), 1) // W
    seed = iota((seeds_here, LANES), 0)
    fold = iota((n_rows, LANES), 1) // W
    per_tile = LANES // W
    for l in range(here):
        lines = []
        seed_cost = jnp.zeros((seeds_here, 1), jnp.float32)
        for t in range(plan.tiles):
            line = costs[t * g * here + l : t * g * here + l + 1, :]
            for d in range(t * g + 1, (t + 1) * g):
                line = line + costs[d * here + l : d * here + l + 1, :]
            cost_out[l : l + 1, t * LANES : (t + 1) * LANES] = line
            lines.append(line)
            mine = seed_of + t * per_tile == seed
            seed_cost = seed_cost + jnp.sum(jnp.where(mine, line, 0.0), axis=1, keepdims=True)
        weight = 1.0 / (1.0 + seed_cost)
        spread = []
        for t in range(plan.tiles):
            mine = seed_of + t * per_tile == seed
            spread.append(jnp.sum(jnp.where(mine, weight, 0.0), axis=0, keepdims=True))
        total = jnp.sum(weight, axis=0, keepdims=True)
        sums[here * 3 * n_rows + l : here * 3 * n_rows + l + 1, :] = jnp.broadcast_to(total, (1, LANES))
        for c in range(3):
            pieces = []
            for j in range(4):
                x = jnp.zeros((n_rows, LANES), jnp.float32)
                for t in range(plan.tiles):
                    at = (c * n + j) * step + t * here + l
                    x = x + stored[pl.ds(at, n_rows, stride=4 * step), :] * spread[t]
                pieces.append(x)
            y = jnp.zeros((n_rows, LANES), jnp.float32)
            for turn in range(4):
                z = pieces[0]
                for j in range(4):
                    z = jnp.where(fold == (j - turn) % 4, pieces[j], z)
                y = y + (pltpu.roll(z, turn * W, 1) if turn else z)
            at = (l * 3 + c) * n_rows
            sums[at : at + n_rows, :] = y


def blend(plan, costs, stored):
    seeds_here = plan.columns // W
    rows = round_up(plan.here * (3 * plan.spheres // 4 + 1), SUB)
    return pl.pallas_call(
        functools.partial(blend_kernel, plan, seeds_here),
        out_shape=[
            jax.ShapeDtypeStruct((plan.here, plan.columns), jnp.float32),
            jax.ShapeDtypeStruct((rows, LANES), jnp.float32),
        ],
        in_specs=[VMEM, VMEM],
        out_specs=[VMEM, VMEM],
        compiler_params=PARAMS,
        name="blend",
    )(costs, stored)


def finish_kernel(plan, *refs):
    parts, out, wide = refs[:-2], refs[-2], refs[-1]
    n_rows = plan.spheres // 4
    for l in range(plan.here):
        at = plan.here * 3 * n_rows + l
        total = parts[0][at : at + 1, :]
        for p in parts[1:]:
            total = total + p[at : at + 1, :]
        inverse = 1.0 / total
        for c in range(3):
            at = (l * 3 + c) * n_rows
            y = parts[0][at : at + n_rows, :]
            for p in parts[1:]:
                y = y + p[at : at + n_rows, :]
            y = y * inverse
            for j in range(4):
                z = pltpu.roll(y, (LANES - j * W) % LANES, 1) if j else y
                wide[l * 3 + c, pl.ds(j, n_rows, stride=4), :] = z
            out[l, c] = wide[l * 3 + c].T[:W]


def finish(plan, parts):
    return pl.pallas_call(
        functools.partial(finish_kernel, plan),
        out_shape=jax.ShapeDtypeStruct((plan.here, 3, W, plan.spheres), jnp.float32),
        in_specs=[VMEM] * len(parts),
        out_specs=VMEM,
        scratch_shapes=[pltpu.VMEM((plan.here * 3, plan.spheres, LANES), jnp.float32)],
        compiler_params=PARAMS,
        name="finish",
    )(*parts)


def exchanged(block, axis, k):
    size = lax.axis_size(axis)
    return lax.ppermute(block, axis, [(i, i ^ k) for i in range(size)])


def local(centres, sphere_radius, counts, adjacency):
    here, _, spheres, columns = centres.shape
    plan = Plan(lax.axis_size("robot"), here, spheres, columns)
    stored = centres.reshape(here, 3, spheres, plan.tiles, LANES)
    stored = stored.transpose(1, 2, 3, 0, 4).reshape(-1, LANES)
    mine, theirs = pack(plan, counts, sphere_radius, adjacency, stored)
    chunks = join(plan, mine, exchanged(theirs, "robot", 1))
    chunks = [chunks[0]] + [exchanged(chunks[k], "robot", 2 * k) for k in range(1, plan.chips)]
    known, before = [], []
    for stage in range(plan.chips - 1):
        block, total = cost(plan, stage, chunks[: stage + 1], known, before)
        known.append(block)
        before = [total]
    (costs,) = cost(plan, plan.chips - 1, chunks, known, before)
    costs = lax.all_to_all(costs, "robot", 0, 0, tiled=True)
    robot_cost, sums = blend(plan, costs, stored)
    parts = [sums] + [exchanged(sums, "seed", k) for k in range(1, lax.axis_size("seed"))]
    return robot_cost, finish(plan, parts).transpose(0, 1, 3, 2)


def solution(mesh):
    return jax.shard_map(
        local,
        mesh=mesh,
        in_specs=(P("robot", None, None, "seed"), P("robot", None), P("robot"), P("robot", None)),
        out_specs=(P("robot", "seed"), P("robot", None, None, None)),
        check_vma=False,
    )
```

time: 49.9 us -> 39.8 us (0.80)
  Pallas kernels: 18.4 us -> 13.3 us
  waiting for transfers between devices: 8.8 us -> 5.37 us
  starting transfers between devices: 12.1 us -> 9.39 us
  blocking collectives: 7.38 us -> 8.71 us
    pallas_call x2 -> x6, Pallas kernels: 16.9 us -> 11.8 us  [the longest x4 10.7 us: cost(): pl.pallas_call(functools.partial(cost_kernel, plan, stage), out_shape=out...]
    ppermute x10 -> x7, waiting for transfers between devices: 8.8 us -> 5.37 us  [exchanged(): return lax.ppermute(block, axis, [(i, i ^ k) for i in range(size)])]
    ppermute x10 -> x7, starting transfers between devices: 12.1 us -> 9.39 us  [exchanged(): return lax.ppermute(block, axis, [(i, i ^ k) for i in range(size)])]
    all_to_all x1, blocking collectives: 7.38 us -> 8.71 us  [local(): costs = lax.all_to_all(costs, 'robot', 0, 0, tiled=True)]
    unnamed x8 -> x10, local copies, waits for them, and re-layouts: 2.33 us -> 2.33 us
  transfers between devices with their start and end apart: 10 -> 7, of which waited for: 5 -> 4; matrix products, arithmetic and copies ran while one was open for 0% -> 0% of each run, Pallas kernels for 0% -> 15%
where the time goes in v3:
time: 39.8 us; the launch traced here: 39.9 us
  Pallas kernels  13.3 us (33%)
  starting transfers between devices  9.39 us (24%)
  blocking collectives  8.71 us (22%)
  waiting for transfers between devices  5.37 us (13%)
  local copies, waits for them, and re-layouts  2.33 us (6%)
  between operations  0.72 us (2%)
    pallas_call x4, Pallas kernels, cost(): pl.pallas_call(functools.partial(cost_kernel, plan, stage), out_shape=out...  10.7 us
    ppermute x7, starting transfers between devices, exchanged(): return lax.ppermute(block, axis, [(i, i ^ k) for i in range(size)])  9.39 us
    all_to_all x1, blocking collectives, local(): costs = lax.all_to_all(costs, 'robot', 0, 0, tiled=True)  8.71 us
    ppermute x7, waiting for transfers between devices, exchanged(): return lax.ppermute(block, axis, [(i, i ^ k) for i in range(size)])  5.37 us
    unnamed x10, local copies, waits for them, and re-layouts  2.33 us
    pallas_call x1, Pallas kernels, pack(): pl.pallas_call(functools.partial(pack_kernel, plan), out_shape=[half, hal...  1.05 us
    pallas_call x1, Pallas kernels, finish(): pl.pallas_call(functools.partial(finish_kernel, plan), out_shape=jax.Shap...  0.86 us
  transfers between devices with their start and end apart: 7, of which 4 were waited for; matrix products, arithmetic and copies ran while one was open for 0% of the time, Pallas kernels for 15%

profile of v3, /device:TPU:0, one launch (start us, length us, event | category | flops | bytes accessed | tf_op | source)
XLA Modules:
  0.0 39.9 jit_solution(16277333860228506967)
XLA Ops:
  0.6 0.0 copy-start.4
  0.6 0.0 copy-start.2
  0.7 0.6 %copy-done.4 = s32[2]{0:T(128)S(1)} copy-done((s32[2]{0:T(128)S(1)}, s32[2]{0:T(128)}, u32[]{:S(2)}) %copy-start.4) | copy-done | bytes 32
  1.3 0.0 copy-done.2
  1.3 0.0 copy-start
  1.3 1.0 %copy-done = f32[2,3,52,256]{3,0,2,1:T(2,128)S(1)} copy-done((f32[2,3,52,256]{3,0,2,1:T(2,128)S(1)}, f32[2,3,52,256]{3,0,2,1:T(2,128)}, u32[]{:S(2)}) %copy-start) | copy-done | bytes 319512
  2.3 0.0 copy-start.3
  2.3 0.7 %copy-done.3 = s32[2,16]{1,0:T(2,128)S(1)} copy-done((s32[2,16]{1,0:T(2,128)S(1)}, s32[2,16]{1,0:T(2,128)}, u32[]{:S(2)}) %copy-start.3) | copy-done | bytes 152
  3.0 1.1 %pack.1 = (f32[4,80,128]{2,1,0:T(8,128)S(1)}, f32[4,80,128]{2,1,0:T(8,128)S(1)}) custom-call(s32[2]{0:T(128)S(1)} %copy-done.4, f32[2,52]{1,0:T(2,128)S(1)} %copy-done.2, s32[2,16]{1,0:T(2,128)S(1)} %copy-done.3, f32[624,128]{1,0:T(8,128)S(1)} %bitcast.8), custom_call_target="tpu_custom_call" | custom-call | tf_op jit(solution)/shard_map/pack/pallas_call | solution.py:121
  4.0 0.6 %collective-permute-start = (f32[4,80,128]{2,1,0:T(8,128)S(1)}, f32[4,80,128]{2,1,0:T(8,128)S(1)}, u32[]{:S(2)}, u32[]{:S(2)}) collective-permute-start(f32[4,80,128]{2,1,0:T(8,128)S(1)} %get-tuple-element.17), channel_id=1, source_target_pairs={{0,4},{4,0},{8,12},{12,8},{16,20},{20,16},{24,28},{28,24},{1,5},{5... | collective-permute-start | bytes 491528 | tf_op jit(solution)/shard_map/ppermute | solution.py:482
  4.6 1.0 %collective-permute-done.theirs = f32[4,80,128]{2,1,0:T(8,128)S(1)} collective-permute-done((f32[4,80,128]{2,1,0:T(8,128)S(1)}, f32[4,80,128]{2,1,0:T(8,128)S(1)}, u32[]{:S(2)}, u32[]{:S(2)}) %collective-permute-start) | collective-permute-done | bytes 163872 | tf_op jit(solution)/shard_map/ppermute | solution.py:482
  5.6 2.9 %collective-permute-start.1 = (f32[2,80,128]{2,1,0:T(8,128)S(1)}, f32[2,80,128]{2,1,0:T(8,128)S(1)}, u32[]{:S(2)}, u32[]{:S(2)}) collective-permute-start(f32[2,80,128]{2,1,0:T(8,128)S(1)} %get-tuple-element.19), channel_id=1, source_target_pairs={{0,8},{4,12},{8,0},{12,4},{16,24},{20,28},{24,16},{28,20},{1,9},{5... | collective-permute-start | bytes 245768 | tf_op jit(solution)/shard_map/ppermute | solution.py:482
  8.5 1.5 %collective-permute-start.2 = (f32[2,80,128]{2,1,0:T(8,128)S(1)}, f32[2,80,128]{2,1,0:T(8,128)S(1)}, u32[]{:S(2)}, u32[]{:S(2)}) collective-permute-start(f32[2,80,128]{2,1,0:T(8,128)S(1)} %get-tuple-element.20), channel_id=1, source_target_pairs={{0,16},{4,20},{8,24},{12,28},{16,0},{20,4},{24,8},{28,12},{1,17},{... | collective-permute-start | bytes 245768 | tf_op jit(solution)/shard_map/ppermute | solution.py:482
  10.1 0.0 collective-permute-start.3
  10.1 1.5 %cost0.1 = (f32[4,4,4,16,128]{4,3,2,1,0:T(8,128)S(1)}, f32[4,8,128]{2,1,0:T(8,128)S(1)}) custom-call(f32[2,80,128]{2,1,0:T(8,128)S(1)} %get-tuple-element.18.refs_0_), custom_call_target="tpu_custom_call" | custom-call | flops 20000000 | bytes 1000 | tf_op jit(solution)/shard_map/cost0/pallas_call | solution.py:367
  11.6 0.0 collective-permute-done.1.refs_1_
  11.6 2.0 %cost1.1 = (f32[4,4,4,16,128]{4,3,2,1,0:T(8,128)S(1)}, f32[8,8,128]{2,1,0:T(8,128)S(1)}) custom-call(f32[2,80,128]{2,1,0:T(8,128)S(1)} %get-tuple-element.18.refs_0_, f32[2,80,128]{2,1,0:T(8,128)S(1)} %collective-permute-done.1.refs_1_, f32[4,4,4,16,128]{4,3,2,1,0:T(8,128)S(1)} %get-tuple-element.22.refs_2_.refs_3_.refs_4_, ...), custom_call_target="tpu_custom_call" | custom-call | flops 40000000 | bytes 1000 | tf_op jit(solution)/shard_map/cost1/pallas_call | solution.py:367
  13.6 0.2 collective-permute-done.2.refs_2_
  13.8 2.6 %cost2.1 = (f32[4,4,4,16,128]{4,3,2,1,0:T(8,128)S(1)}, f32[12,8,128]{2,1,0:T(8,128)S(1)}) custom-call(f32[2,80,128]{2,1,0:T(8,128)S(1)} %get-tuple-element.18.refs_0_, f32[2,80,128]{2,1,0:T(8,128)S(1)} %collective-permute-done.1.refs_1_, f32[2,80,128]{2,1,0:T(8,128)S(1)} %collective-permute-done.2.refs_2_, ...), custom_call_target="tpu_custom_call" | custom-call | flops 60000000 | bytes 1000 | tf_op jit(solution)/shard_map/cost2/pallas_call | solution.py:367
  16.5 0.0 collective-permute-done.3.refs_3_
  16.5 0.0 copy-start.1
  16.5 4.6 %cost3.1 = f32[16,128]{1,0:T(8,128)S(1)} custom-call(f32[2,80,128]{2,1,0:T(8,128)S(1)} %get-tuple-element.18.refs_0_, f32[2,80,128]{2,1,0:T(8,128)S(1)} %collective-permute-done.1.refs_1_, f32[2,80,128]{2,1,0:T(8,128)S(1)} %collective-permute-done.2.refs_2_, f32[2,80,128]{2,1,0:T(8,128)S(1)} %collective-permute-done.3.refs_3_, ...), custom_call_target="tpu_custom_call" | custom-call | flops 80000000 | bytes 1000 | tf_op jit(solution)/shard_map/cost3/pallas_call | solution.py:367
  21.1 8.7 %all_to_all.11 = f32[8,2,128]{2,1,0:T(2,128)S(1)} all-to-all(f32[8,2,128]{2,1,0:T(2,128)S(1)} %bitcast.10), channel_id=1, replica_groups=mesh['robot'=8,'seed'=4] {'robot'}, dimensions={0} | all-to-all | bytes 16384 | tf_op jit(solution)/shard_map/all_to_all | solution.py:499
  29.8 0.0 copy-done.1
  29.8 0.7 %blend.1 = (f32[2,256]{1,0:T(2,128)}, f32[80,128]{1,0:T(8,128)S(1)}) custom-call(f32[16,128]{1,0:T(8,128)S(1)} %bitcast.11, f32[624,128]{1,0:T(8,128)S(1)} %bitcast.9), custom_call_target="tpu_custom_call" | custom-call | tf_op jit(solution)/shard_map/blend/pallas_call | solution.py:434
  30.5 3.6 %collective-permute-start.6 = (f32[80,128]{1,0:T(8,128)S(1)}, f32[80,128]{1,0:T(8,128)S(1)}, u32[]{:S(2)}, u32[]{:S(2)}) collective-permute-start(f32[80,128]{1,0:T(8,128)S(1)} %get-tuple-element.29.refs_0_), channel_id=1, source_target_pairs={{0,3},{1,2},{2,1},{3,0},{4,7},{5,6},{6,5},{7,4},{8,11},{9,10},{10,... | collective-permute-start | bytes 122888 | tf_op jit(solution)/shard_map/ppermute | solution.py:482
  34.1 0.0 collective-permute-start.5
  34.1 0.8 %collective-permute-start.4 = (f32[80,128]{1,0:T(8,128)S(1)}, f32[80,128]{1,0:T(8,128)S(1)}, u32[]{:S(2)}, u32[]{:S(2)}) collective-permute-start(f32[80,128]{1,0:T(8,128)S(1)} %get-tuple-element.29.refs_0_), channel_id=1, source_target_pairs={{0,1},{1,0},{2,3},{3,2},{4,5},{5,4},{6,7},{7,6},{8,9},{9,8},{10,11... | collective-permute-start | bytes 122888 | tf_op jit(solution)/shard_map/ppermute | solution.py:482
  34.9 1.6 %collective-permute-done.6.refs_3_ = f32[80,128]{1,0:T(8,128)S(1)} collective-permute-done((f32[80,128]{1,0:T(8,128)S(1)}, f32[80,128]{1,0:T(8,128)S(1)}, u32[]{:S(2)}, u32[]{:S(2)}) %collective-permute-start.6) | collective-permute-done | bytes 40992 | tf_op jit(solution)/shard_map/ppermute | solution.py:482
  36.5 2.5 %collective-permute-done.5.refs_2_ = f32[80,128]{1,0:T(8,128)S(1)} collective-permute-done((f32[80,128]{1,0:T(8,128)S(1)}, f32[80,128]{1,0:T(8,128)S(1)}, u32[]{:S(2)}, u32[]{:S(2)}) %collective-permute-start.5) | collective-permute-done | bytes 40992 | tf_op jit(solution)/shard_map/ppermute | solution.py:482
  39.0 0.0 collective-permute-done.4.refs_1_
  39.0 0.9 %finish.1 = f32[2,3,32,52]{3,2,1,0:T(8,128)} custom-call(f32[80,128]{1,0:T(8,128)S(1)} %get-tuple-element.29.refs_0_, f32[80,128]{1,0:T(8,128)S(1)} %collective-permute-done.4.refs_1_, f32[80,128]{1,0:T(8,128)S(1)} %collective-permute-done.5.refs_2_, f32[80,128]{1,0:T(8,128)S(1)} %collective-permute-done.6.refs_3_), custom_call_target="tpu_custom_call" | custom-call | tf_op jit(solution)/shard_map/finish/pallas_call | solution.py:469
  (1 shorter events, 0.0 us)
Async XLA Ops:
  0.6 0.7 %copy-start.4 = (s32[2]{0:T(128)S(1)}, s32[2]{0:T(128)}, u32[]{:S(2)}) copy-start(s32[2]{0:T(128)} %counts.1) | copy-start | bytes 28
  0.6 0.7 %copy-start.2 = (f32[2,52]{1,0:T(2,128)S(1)}, f32[2,52]{1,0:T(2,128)}, u32[]{:S(2)}) copy-start(f32[2,52]{1,0:T(2,128)} %radius.1) | copy-start | bytes 1252
  1.3 1.0 %copy-start = (f32[2,3,52,256]{3,0,2,1:T(2,128)S(1)}, f32[2,3,52,256]{3,0,2,1:T(2,128)}, u32[]{:S(2)}) copy-start(f32[2,3,52,256]{3,0,2,1:T(2,128)} %param.4) | copy-start | bytes 958468
  2.3 0.7 %copy-start.3 = (s32[2,16]{1,0:T(2,128)S(1)}, s32[2,16]{1,0:T(2,128)}, u32[]{:S(2)}) copy-start(s32[2,16]{1,0:T(2,128)} %adjacency.1) | copy-start | bytes 388
  4.0 1.6 %collective-permute-start = (f32[4,80,128]{2,1,0:T(8,128)S(1)}, f32[4,80,128]{2,1,0:T(8,128)S(1)}, u32[]{:S(2)}, u32[]{:S(2)}) collective-permute-start(f32[4,80,128]{2,1,0:T(8,128)S(1)} %get-tuple-element.17), channel_id=1, source_target_pairs={{0,4},{4,0},{8,12},{12,8},{16,20},{20,16},{24,28},{28,24},{1,5},{5... | collective-permute-start | bytes 491528 | tf_op jit(solution)/shard_map/ppermute | solution.py:482
  5.6 5.9 %collective-permute-start.1 = (f32[2,80,128]{2,1,0:T(8,128)S(1)}, f32[2,80,128]{2,1,0:T(8,128)S(1)}, u32[]{:S(2)}, u32[]{:S(2)}) collective-permute-start(f32[2,80,128]{2,1,0:T(8,128)S(1)} %get-tuple-element.19), channel_id=1, source_target_pairs={{0,8},{4,12},{8,0},{12,4},{16,24},{20,28},{24,16},{28,20},{1,9},{5... | collective-permute-start | bytes 245768 | tf_op jit(solution)/shard_map/ppermute | solution.py:482
  8.5 5.3 %collective-permute-start.2 = (f32[2,80,128]{2,1,0:T(8,128)S(1)}, f32[2,80,128]{2,1,0:T(8,128)S(1)}, u32[]{:S(2)}, u32[]{:S(2)}) collective-permute-start(f32[2,80,128]{2,1,0:T(8,128)S(1)} %get-tuple-element.20), channel_id=1, source_target_pairs={{0,16},{4,20},{8,24},{12,28},{16,0},{20,4},{24,8},{28,12},{1,17},{... | collective-permute-start | bytes 245768 | tf_op jit(solution)/shard_map/ppermute | solution.py:482
  10.1 6.4 %collective-permute-start.3 = (f32[2,80,128]{2,1,0:T(8,128)S(1)}, f32[2,80,128]{2,1,0:T(8,128)S(1)}, u32[]{:S(2)}, u32[]{:S(2)}) collective-permute-start(f32[2,80,128]{2,1,0:T(8,128)S(1)} %get-tuple-element.21), channel_id=1, source_target_pairs={{0,24},{4,28},{8,16},{12,20},{16,8},{20,12},{24,0},{28,4},{1,25},{... | collective-permute-start | bytes 245768 | tf_op jit(solution)/shard_map/ppermute | solution.py:482
  16.5 13.3 %copy-start.1 = (f32[2,3,52,256]{3,0,2,1:T(2,128)S(1)}, f32[2,3,52,256]{3,0,2,1:T(2,128)}, u32[]{:S(2)}) copy-start(f32[2,3,52,256]{3,0,2,1:T(2,128)} %param.4) | copy-start | bytes 958468
  30.5 6.0 %collective-permute-start.6 = (f32[80,128]{1,0:T(8,128)S(1)}, f32[80,128]{1,0:T(8,128)S(1)}, u32[]{:S(2)}, u32[]{:S(2)}) collective-permute-start(f32[80,128]{1,0:T(8,128)S(1)} %get-tuple-element.29.refs_0_), channel_id=1, source_target_pairs={{0,3},{1,2},{2,1},{3,0},{4,7},{5,6},{6,5},{7,4},{8,11},{9,10},{10,... | collective-permute-start | bytes 122888 | tf_op jit(solution)/shard_map/ppermute | solution.py:482
  34.1 4.9 %collective-permute-start.5 = (f32[80,128]{1,0:T(8,128)S(1)}, f32[80,128]{1,0:T(8,128)S(1)}, u32[]{:S(2)}, u32[]{:S(2)}) collective-permute-start(f32[80,128]{1,0:T(8,128)S(1)} %get-tuple-element.29.refs_0_), channel_id=1, source_target_pairs={{0,2},{1,3},{2,0},{3,1},{4,6},{5,7},{6,4},{7,5},{8,10},{9,11},{10,... | collective-permute-start | bytes 122888 | tf_op jit(solution)/shard_map/ppermute | solution.py:482
  34.1 4.9 %collective-permute-start.4 = (f32[80,128]{1,0:T(8,128)S(1)}, f32[80,128]{1,0:T(8,128)S(1)}, u32[]{:S(2)}, u32[]{:S(2)}) collective-permute-start(f32[80,128]{1,0:T(8,128)S(1)} %get-tuple-element.29.refs_0_), channel_id=1, source_target_pairs={{0,1},{1,0},{2,3},{3,2},{4,5},{5,4},{6,7},{7,6},{8,9},{9,8},{10,11... | collective-permute-start | bytes 122888 | tf_op jit(solution)/shard_map/ppermute | solution.py:482

commit v4 on v3

--- a/solution.py
+++ b/solution.py
@@ -58,59 +58,72 @@
     return middles, radius + 0.5 * jnp.sqrt(squares + 1e-06)
 
 
-def pack_kernel(plan, counts, radius, adjacency, stored, mine, theirs, source):
+def pack_kernel(plan, counts_hbm, radius_hbm, adjacency_hbm, stored_hbm, mine, theirs, *scratch):
+    counts, radius, adjacency, stored, source, sem = scratch
     me = lax.axis_index("robot")
-    n, g, rows, width = plan.spheres, plan.lane_groups, plan.rows, plan.width
-    step = plan.tiles * plan.here
-    order = iota((n, LANES), 0)
-    for l in range(plan.here):
-        for t in range(plan.tiles):
-            points = [
-                stored[pl.ds(c * n * step + t * plan.here + l, n, stride=step), :] for c in range(3)
-            ]
-            if not plan.sweep_late:
-                diagonal = iota((n, n), 0) == iota((n, n), 1)
-                column = jnp.sum(
-                    jnp.where(diagonal, radius[l : l + 1, :], 0.0), axis=1, keepdims=True
-                )
-                points, swept = sweep(points, iota((n, LANES), 1) % W == W - 1, column)
-                robot = me * plan.here + l
-                off = FAR * (1 + order + plan.padded * robot).astype(jnp.float32)
-                points[0] = jnp.where(order < counts[l], points[0], off)
-                points.append(swept)
-                spare = plan.padded - n
-                if spare:
-                    index = n + iota((spare, LANES), 0) + plan.padded * robot
-                    fill = FAR * (1 + index).astype(jnp.float32)
-                    for c in range(4):
-                        source[t, l * 4 + c, n:, :] = fill if c == 0 else jnp.ones_like(fill)
-            for c, x in enumerate(points):
-                source[t, l * plan.fields + c, 0:n, :] = x
+    n, g, rows, width, here = plan.spheres, plan.lane_groups, plan.rows, plan.width, plan.here
+    step = plan.tiles * here
+    copies = [
+        pltpu.make_async_copy(src, dst, sem.at[i])
+        for i, (src, dst) in enumerate(
+            zip((stored_hbm, counts_hbm, radius_hbm, adjacency_hbm), (stored, counts, radius, adjacency))
+        )
+    ]
+    for copy in copies:
+        copy.start()
+    for copy in copies[1:]:
+        copy.wait()
     lane = iota((1, LANES), 1)
     links = iota((1, plan.slots), 1)
     heads = []
-    for l in range(plan.here):
-        head = jnp.where(lane == n, counts[l].astype(jnp.float32), 0.0)
+    for l in range(here):
+        head = jnp.where(lane == n, counts[:, l : l + 1].astype(jnp.float32), 0.0)
         for h in range(plan.halves):
             bits = jnp.where(
                 (adjacency[l : l + 1, :] != 0) & (links // 16 == h), 1 << (links % 16), 0
             ).astype(jnp.float32)
             head = jnp.where(lane == n + 1 + h, jnp.sum(bits, axis=1, keepdims=True), head)
         heads.append(head)
+    copies[0].wait()
+    if not plan.sweep_late:
+        order = iota((n, LANES), 0)
+        diagonal = iota((n, n), 0) == iota((n, n), 1)
+        for l in range(here):
+            column = jnp.sum(jnp.where(diagonal, radius[l : l + 1, :], 0.0), axis=1, keepdims=True)
+            robot = me * here + l
+            off = FAR * (1 + order + plan.padded * robot).astype(jnp.float32)
+            for t in range(plan.tiles):
+                points = [
+                    stored[pl.ds(c * n * step + t * here + l, n, stride=step), :] for c in range(3)
+                ]
+                fields, swept = sweep(points, iota((n, LANES), 1) % W == W - 1, column)
+                fields[0] = jnp.where(order < counts[:, l : l + 1], fields[0], off)
+                for c, x in enumerate(fields + [swept]):
+                    source[t, l * 4 + c, 0:n, :] = x
+                if plan.padded > n:
+                    index = n + iota((plan.padded - n, LANES), 0) + plan.padded * robot
+                    fill = FAR * (1 + index).astype(jnp.float32)
+                    for c in range(4):
+                        source[t, l * 4 + c, n:, :] = fill if c == 0 else jnp.ones_like(fill)
     lane_group = iota((rows, LANES), 1) // width
-    for k in range(plan.group):
+    for k in [*range(1, plan.group, 2), *range(0, plan.group, 2)]:
         out = (mine, theirs)[k % 2]
         dest = me ^ k
         tile = dest // g
         spot = dest % g
-        for f in range(plan.here * plan.fields):
-            y = jnp.zeros((rows, LANES), jnp.float32)
-            for j in range(g):
-                x = source[tile, f, pl.ds(j, rows, stride=g), :]
-                x = pltpu.roll(x, ((j + g - spot) % g) * width, 1)
-                y = jnp.where(lane_group == j, x, y)
-            out[k // 2, f * rows : (f + 1) * rows, :] = y
-        for l in range(plan.here):
+        for l in range(here):
+            for c in range(plan.fields):
+                y = jnp.zeros((rows, LANES), jnp.float32)
+                for j in range(g):
+                    if plan.sweep_late:
+                        at = (c * n + j) * step + tile * here + l
+                        x = stored[pl.ds(at, rows, stride=g * step), :]
+                    else:
+                        x = source[tile, l * 4 + c, pl.ds(j, rows, stride=g), :]
+                    x = pltpu.roll(x, ((j + g - spot) % g) * width, 1)
+                    y = jnp.where(lane_group == j, x, y)
+                at = (l * plan.fields + c) * rows
+                out[k // 2, at : at + rows, :] = y
             at = plan.data_rows + l
             out[k // 2, at : at + 1, :] = heads[l]
             out[k // 2, at : at + 1, 0:n] = radius[l : l + 1, :]
@@ -118,17 +131,21 @@
 
 def pack(plan, counts, radius, adjacency, stored):
     half = jax.ShapeDtypeStruct((plan.chips, plan.chunk_rows, LANES), jnp.float32)
+    args = (counts.reshape(1, -1), radius, adjacency, stored)
+    swept = (plan.tiles, plan.here * 4, plan.padded, LANES)
     return pl.pallas_call(
         functools.partial(pack_kernel, plan),
         out_shape=[half, half],
-        in_specs=[SMEM, VMEM, VMEM, VMEM],
+        in_specs=[pl.BlockSpec(memory_space=pltpu.HBM)] * len(args),
         out_specs=[VMEM, VMEM],
-        scratch_shapes=[
-            pltpu.VMEM((plan.tiles, plan.here * plan.fields, plan.padded, LANES), jnp.float32)
+        scratch_shapes=[pltpu.VMEM(x.shape, x.dtype) for x in args]
+        + [
+            pltpu.VMEM((SUB, LANES) if plan.sweep_late else swept, jnp.float32),
+            pltpu.SemaphoreType.DMA((len(args),)),
         ],
         compiler_params=PARAMS,
         name="pack",
-    )(counts, radius, adjacency, stored)
+    )(*args)
 
 
 def join_kernel(plan, mine, theirs, *outs):
@@ -165,13 +182,12 @@
 
 def cost_kernel(plan, stage, *refs):
     chunks, refs = refs[: stage + 1], refs[stage + 1 :]
-    known, refs = refs[:stage], refs[stage:]
-    before, refs = refs[: 1 if stage else 0], refs[1 if stage else 0 :]
+    before, refs = refs[: 2 if stage else 0], refs[2 if stage else 0 :]
     ends = stage == plan.chips - 1
     if ends:
-        out, blocks, packed, sums, totals, names, starts = refs
+        out, store, totals, blocks, tails, sums, starts, links = refs
     else:
-        blocks, totals, packed, sums, names, starts = refs
+        store, totals, blocks, tails, sums, starts, links = refs
     me = lax.axis_index("robot")
     g, rows, width, here, n = plan.lane_groups, plan.rows, plan.width, plan.here, plan.spheres
     parts, fresh = plan.parts, 2 * plan.here
@@ -187,17 +203,17 @@
         starts[u] = jnp.minimum((count + g - 1) // g, rows)
     for i in range(fresh):
         line = line_of(first_slot + i)
-        links = [line[0, n + 1 + h].astype(jnp.int32) for h in range(plan.halves)]
-        for k in range(stage + 1):
-            found = jnp.int32(0)
-            for v in range(fresh if k < stage else i):
-                robot = (k * fresh + v) ^ (me * here)
-                mask = links[0]
-                for h in range(1, plan.halves):
-                    mask = jnp.where(robot // 16 == h, links[h], mask)
-                names[k, i, found] = v
-                found = found + ((mask >> (robot % 16)) & 1)
-            names[k, i, fresh] = found
+        bits = line[0, n + 1].astype(jnp.int32)
+        for h in range(1, plan.halves):
+            bits = bits | (line[0, n + 1 + h].astype(jnp.int32) << (16 * h))
+        step = 1
+        while step < plan.slots:
+            low = sum(1 << b for b in range(plan.slots) if not b & step)
+            low = low - (1 << 32) if low >= 1 << 31 else low
+            turned = ((bits & low) << step) | ((bits >> step) & low)
+            bits = jnp.where((me * here) & step != 0, turned, bits)
+            step *= 2
+        links[i] = bits & ((1 << (first_slot + i)) - 1)
 
     sphere = iota((rows, LANES), 0) * g + iota((rows, LANES), 1) // width
     last = iota((rows, LANES), 1) % W == W - 1
@@ -223,33 +239,33 @@
             fields[0] = jnp.where(sphere < count, fields[0], off)
             fields.append(swept)
         for c in range(4):
+            x = fields[c]
             for m in range(g):
-                x = fields[c]
                 blocks[i, c, m, 0:rows, :] = pltpu.roll(x, m * width, 1) if m else x
+            store[slot, c, 0:rows, :] = x
             if deep > rows:
-                fill = -FAR if c == 0 else 1.0
-                blocks[i, c, 0, rows:deep, :] = jnp.full((deep - rows, LANES), fill, jnp.float32)
+                fill = jnp.full((deep - rows, LANES), -FAR if c == 0 else 1.0, jnp.float32)
+                store[slot, c, rows:deep, :] = fill
+        totals[slot] = jnp.zeros((SUB, LANES), jnp.float32)
     for u in range(first_slot):
-        totals[u] = before[0][u]
-    for i in range(fresh):
-        totals[first_slot + i] = jnp.zeros((SUB, LANES), jnp.float32)
+        store[u] = before[0][u]
+        totals[u] = before[1][u]
 
     def row(i, m, r):
         return [blocks[i, c, m, r : r + 1, :] for c in range(4)]
 
-    def part(i, m, p):
-        return [blocks[i, c, m, p * SUB : (p + 1) * SUB, :] for c in range(4)]
+    def part(slot, p):
+        return [store[slot, c, p * SUB : (p + 1) * SUB, :] for c in range(4)]
 
     sub = iota((SUB, LANES), 0)
     lane_group = iota((SUB, LANES), 1) // width
+    nothing = jnp.zeros((SUB, LANES), jnp.float32)
 
     def self_terms(u, high):
-        total = jnp.zeros((SUB, LANES), jnp.float32)
-        second = part(u, 0, 0)
-        turned = second
+        total = nothing
+        second = part(first_slot + u, 0)
         for d in range(SUB // 2 + 1):
-            if d:
-                turned = [pltpu.roll(x, SUB - d, 0) for x in second]
+            turned = [pltpu.roll(x, SUB - d, 0) for x in second] if d else second
             low = (sub + d) % SUB
             for m in range(g):
                 other = (lane_group + g - m) % g
@@ -263,12 +279,13 @@
                     keep = sub < d
                 else:
                     keep = None
-                total = total + masked(term(part(u, m, 0), turned), keep)
+                first = [blocks[u, c, m, 0:SUB, :] for c in range(4)]
+                total = total + masked(term(first, turned), keep)
         for r in range(SUB, high):
             for p in range(parts):
                 if p * SUB > r:
                     continue
-                second = part(u, 0, p)
+                second = part(first_slot + u, p)
                 for m in range(g):
                     other = (lane_group + g - m) % g
                     ahead = (r - p * SUB - sub) * g + other - lane_group
@@ -276,67 +293,75 @@
                     total = total + masked(term(row(u, m, r), second), ahead >= 2 if near else None)
         return total
 
-    def with_rows(u, trips, high):
+    def against(u, high, second):
+        value = nothing
+        for r in range(high):
+            for m in range(g):
+                value = value + term(row(u, m, r), second)
+        return value
+
+    def lowest_bit(bits):
+        return 31 - lax.clz(bits & -bits)
+
+    def with_rows(u, high):
         total = self_terms(u, high)
 
-        def trip(j, total):
-            at = pl.multiple_of(j * SUB, SUB)
-            second = [packed[c, pl.ds(at, SUB), :] for c in range(4)]
-            value = jnp.zeros((SUB, LANES), jnp.float32)
-            for r in range(high):
-                for m in range(g):
-                    value = value + term(row(u, m, r), second)
-            sums[pl.ds(at, SUB), :] = value
-            return total + value
-
-        totals[first_slot + u] = totals[first_slot + u] + lax.fori_loop(0, trips, trip, total)
+        def neighbour(state):
+            bits, filled, total = state
+            v = lowest_bit(bits)
+            value = against(u, high, part(v, 0))
+            totals[v] = totals[v] + value
+            if parts > 1:
+                for c, x in enumerate(part(v, 1)):
+                    tails[c, pl.ds(filled, SUB), :] = x
+                filled = filled + jnp.maximum(starts[v] - SUB, 0)
+            return bits & (bits - 1), filled, total + value
+
+        state = (links[u], jnp.int32(0), total)
+        _, filled, total = lax.while_loop(lambda state: state[0] != 0, neighbour, state)
+        if parts > 1:
+            for c in range(4):
+                fill = jnp.full((SUB, LANES), -FAR if c == 0 else 1.0, jnp.float32)
+                tails[c, pl.ds(filled, SUB), :] = fill
+
+            def trip(j, total):
+                at = pl.multiple_of(j * SUB, SUB)
+                value = against(u, high, [tails[c, pl.ds(at, SUB), :] for c in range(4)])
+                sums[pl.ds(at, SUB), :] = value
+                return total + value
+
+            total = lax.fori_loop(0, (filled + SUB - 1) // SUB, trip, total)
+        totals[first_slot + u] = totals[first_slot + u] + total
 
     lowest = max(1, -(-(n // 2) // g))
 
-    def choose(u, trips, low, high):
+    def choose(u, low, high):
         if low == high:
-            with_rows(u, trips, high)
+            with_rows(u, high)
             return
         middle = (low + high) // 2
 
         @pl.when(starts[first_slot + u] <= middle)
         def _():
-            choose(u, trips, low, middle)
+            choose(u, low, middle)
 
         @pl.when(starts[first_slot + u] > middle)
         def _():
-            choose(u, trips, middle + 1, high)
+            choose(u, middle + 1, high)
 
     @pl.loop(0, fresh)
     def _(u):
-        filled = jnp.int32(0)
-        for k in range(stage + 1):
-
-            def gather(e, filled, k=k):
-                v = names[k, u, e]
-                for c in range(4):
-                    packed[c, pl.ds(filled, deep), :] = (known[k] if k < stage else blocks)[v, c, 0]
-                return filled + starts[k * fresh + v]
-
-            filled = lax.fori_loop(0, names[k, u, fresh], gather, filled)
-        for c in range(4):
-            fill = -FAR if c == 0 else 1.0
-            packed[c, pl.ds(filled, SUB), :] = jnp.full((SUB, LANES), fill, jnp.float32)
-        choose(u, (filled + SUB - 1) // SUB, lowest, rows)
-
-        filled = jnp.int32(0)
-        for k in range(stage + 1):
-
-            def hand_out(e, filled, k=k):
-                v = k * fresh + names[k, u, e]
-                value = totals[v]
-                for p in range(parts):
-                    line = sums[pl.ds(filled + p * SUB, SUB), :]
-                    value = value + jnp.where(sub + p * SUB < starts[v], line, 0.0)
-                totals[v] = value
-                return filled + starts[v]
-
-            filled = lax.fori_loop(0, names[k, u, fresh], hand_out, filled)
+        choose(u, lowest, rows)
+        if parts > 1:
+
+            def hand_out(state):
+                bits, filled = state
+                v = lowest_bit(bits)
+                more = jnp.maximum(starts[v] - SUB, 0)
+                totals[v] = totals[v] + jnp.where(sub < more, sums[pl.ds(filled, SUB), :], 0.0)
+                return bits & (bits - 1), filled + more
+
+            lax.while_loop(lambda state: state[0] != 0, hand_out, (links[u], jnp.int32(0)))
 
     if not ends:
         return
@@ -352,36 +377,28 @@
             out[pl.ds((me ^ k) * here + l, 1), :] = value
 
 
-def cost(plan, stage, chunks, known, before):
+def cost(plan, stage, chunks, before):
     fresh, g = 2 * plan.here, plan.lane_groups
     slots = (stage + 1) * fresh
     deep = plan.parts * SUB
-    long = round_up(slots * plan.rows + deep + SUB, SUB)
-    block = (fresh, 4, g, deep, LANES)
-    total = (slots, SUB, LANES)
+    long = round_up(slots * max(plan.rows - SUB, 0) + 2 * SUB, SUB)
+    carried = [(slots, 4, deep, LANES), (slots, SUB, LANES)]
     ends = stage == plan.chips - 1
-    if ends:
-        out_shape = [jax.ShapeDtypeStruct((slots, LANES), jnp.float32)]
-    else:
-        out_shape = [jax.ShapeDtypeStruct(shape, jnp.float32) for shape in (block, total)]
+    outs = [(slots, LANES)] if ends else carried
+    scratch = (carried if ends else []) + [(fresh, 4, g, deep, LANES), (4, long, LANES), (long, LANES)]
     return pl.pallas_call(
         functools.partial(cost_kernel, plan, stage),
-        out_shape=out_shape,
-        in_specs=[VMEM] * (len(chunks) + len(known) + len(before)),
-        out_specs=[VMEM] * len(out_shape),
-        scratch_shapes=([pltpu.VMEM(block, jnp.float32)] if ends else [])
-        + [pltpu.VMEM((4, long, LANES), jnp.float32), pltpu.VMEM((long, LANES), jnp.float32)]
-        + ([pltpu.VMEM(total, jnp.float32)] if ends else [])
-        + [
-            pltpu.SMEM((stage + 1, fresh, fresh + 1), jnp.int32),
-            pltpu.SMEM((slots,), jnp.int32),
-        ],
+        out_shape=[jax.ShapeDtypeStruct(shape, jnp.float32) for shape in outs],
+        in_specs=[VMEM] * (len(chunks) + len(before)),
+        out_specs=[VMEM] * len(outs),
+        scratch_shapes=[pltpu.VMEM(shape, jnp.float32) for shape in scratch]
+        + [pltpu.SMEM((slots,), jnp.int32), pltpu.SMEM((fresh,), jnp.int32)],
         compiler_params=PARAMS,
         cost_estimate=pl.CostEstimate(
             flops=20_000_000 * (stage + 1), bytes_accessed=1000, transcendentals=0
         ),
         name=f"cost{stage}",
-    )(*chunks, *known, *before)
+    )(*chunks, *before)
 
 
 def blend_kernel(plan, seeds_here, costs, stored, cost_out, sums):
@@ -490,12 +507,10 @@
     mine, theirs = pack(plan, counts, sphere_radius, adjacency, stored)
     chunks = join(plan, mine, exchanged(theirs, "robot", 1))
     chunks = [chunks[0]] + [exchanged(chunks[k], "robot", 2 * k) for k in range(1, plan.chips)]
-    known, before = [], []
-    for stage in range(plan.chips - 1):
-        block, total = cost(plan, stage, chunks[: stage + 1], known, before)
-        known.append(block)
-        before = [total]
-    (costs,) = cost(plan, plan.chips - 1, chunks, known, before)
+    carried = []
+    for stage in range(plan.chips):
+        carried = cost(plan, stage, chunks[: stage + 1], carried)
+    (costs,) = carried
     costs = lax.all_to_all(costs, "robot", 0, 0, tiled=True)
     robot_cost, sums = blend(plan, costs, stored)
     parts = [sums] + [exchanged(sums, "seed", k) for k in range(1, lax.axis_size("seed"))]

time: 39.8 us -> 39 us (0.980); the launches traced: 39.9 us -> 38.3 us
  Pallas kernels: 13.3 us -> 12.4 us
  local copies, waits for them, and re-layouts: 2.33 us -> 1.65 us
    unnamed x10, local copies, waits for them, and re-layouts: 2.33 us -> 1.65 us
    pallas_call x4, Pallas kernels: 10.7 us -> 10.1 us  [cost(): pl.pallas_call(functools.partial(cost_kernel, plan, stage), out_shape=[ja...]
  transfers between devices with their start and end apart: 7 -> 7, of which waited for: 4 -> 4; matrix products, arithmetic and copies ran while one was open for 0% -> 0% of each run, Pallas kernels for 15% -> 18%
where the time goes in v4:
time: 39 us; the launch traced here: 38.3 us
  Pallas kernels  12.4 us (32%)
  starting transfers between devices  9.39 us (24%)
  blocking collectives  8.76 us (22%)
  waiting for transfers between devices  5.28 us (14%)
  local copies, waits for them, and re-layouts  1.65 us (4%)
  between operations  0.73 us (2%)
    pallas_call x4, Pallas kernels, cost(): pl.pallas_call(functools.partial(cost_kernel, plan, stage), out_shape=[ja...  10.1 us
    ppermute x7, starting transfers between devices, exchanged(): return lax.ppermute(block, axis, [(i, i ^ k) for i in range(size)])  9.39 us
    all_to_all x1, blocking collectives, local(): costs = lax.all_to_all(costs, 'robot', 0, 0, tiled=True)  8.76 us
    ppermute x7, waiting for transfers between devices, exchanged(): return lax.ppermute(block, axis, [(i, i ^ k) for i in range(size)])  5.28 us
    unnamed x10, local copies, waits for them, and re-layouts  1.65 us
    pallas_call x1, Pallas kernels, finish(): pl.pallas_call(functools.partial(finish_kernel, plan), out_shape=jax.Shap...  0.86 us
  transfers between devices with their start and end apart: 7, of which 4 were waited for; matrix products, arithmetic and copies ran while one was open for 0% of the time, Pallas kernels for 18%

profile of v4, /device:TPU:0, one launch (start us, length us, event | category | flops | bytes accessed | tf_op | source)
XLA Modules:
  0.0 38.3 jit_solution(4791119286644972421)
XLA Ops:
  0.6 0.0 copy-start.3
  0.6 0.0 copy-start.2
  0.7 0.0 copy-start.4
  0.7 0.7 %copy-done.3 = s32[2,16]{1,0:T(2,128)S(1)} copy-done((s32[2,16]{1,0:T(2,128)S(1)}, s32[2,16]{1,0:T(2,128)}, u32[]{:S(2)}) %copy-start.3) | copy-done | bytes 152
  1.3 0.0 copy-done.2
  1.3 0.0 copy-done.4
  1.3 0.0 copy-start
  1.3 1.0 %copy-done = f32[2,3,52,256]{3,0,2,1:T(2,128)S(1)} copy-done((f32[2,3,52,256]{3,0,2,1:T(2,128)S(1)}, f32[2,3,52,256]{3,0,2,1:T(2,128)}, u32[]{:S(2)}) %copy-start) | copy-done | bytes 319512
  2.3 0.7 %pack.1 = (f32[4,80,128]{2,1,0:T(8,128)S(1)}, f32[4,80,128]{2,1,0:T(8,128)S(1)}) custom-call(s32[1,2]{1,0:T(1,128)S(1)} %bitcast.13, f32[2,52]{1,0:T(2,128)S(1)} %copy-done.2, s32[2,16]{1,0:T(2,128)S(1)} %copy-done.3, f32[624,128]{1,0:T(8,128)S(1)} %bitcast.9), custom_call_target="tpu_custom_call" | custom-call | tf_op jit(solution)/shard_map/pack/pallas_call | solution.py:136
  3.0 0.6 %collective-permute-start = (f32[4,80,128]{2,1,0:T(8,128)S(1)}, f32[4,80,128]{2,1,0:T(8,128)S(1)}, u32[]{:S(2)}, u32[]{:S(2)}) collective-permute-start(f32[4,80,128]{2,1,0:T(8,128)S(1)} %get-tuple-element.17), channel_id=1, source_target_pairs={{0,4},{4,0},{8,12},{12,8},{16,20},{20,16},{24,28},{28,24},{1,5},{5... | collective-permute-start | bytes 491528 | tf_op jit(solution)/shard_map/ppermute | solution.py:499
  3.6 1.0 %collective-permute-done.theirs = f32[4,80,128]{2,1,0:T(8,128)S(1)} collective-permute-done((f32[4,80,128]{2,1,0:T(8,128)S(1)}, f32[4,80,128]{2,1,0:T(8,128)S(1)}, u32[]{:S(2)}, u32[]{:S(2)}) %collective-permute-start) | collective-permute-done | bytes 163872 | tf_op jit(solution)/shard_map/ppermute | solution.py:499
  4.7 2.9 %collective-permute-start.1 = (f32[2,80,128]{2,1,0:T(8,128)S(1)}, f32[2,80,128]{2,1,0:T(8,128)S(1)}, u32[]{:S(2)}, u32[]{:S(2)}) collective-permute-start(f32[2,80,128]{2,1,0:T(8,128)S(1)} %get-tuple-element.19), channel_id=1, source_target_pairs={{0,8},{4,12},{8,0},{12,4},{16,24},{20,28},{24,16},{28,20},{1,9},{5... | collective-permute-start | bytes 245768 | tf_op jit(solution)/shard_map/ppermute | solution.py:499
  7.6 1.5 %collective-permute-start.2 = (f32[2,80,128]{2,1,0:T(8,128)S(1)}, f32[2,80,128]{2,1,0:T(8,128)S(1)}, u32[]{:S(2)}, u32[]{:S(2)}) collective-permute-start(f32[2,80,128]{2,1,0:T(8,128)S(1)} %get-tuple-element.20), channel_id=1, source_target_pairs={{0,16},{4,20},{8,24},{12,28},{16,0},{20,4},{24,8},{28,12},{1,17},{... | collective-permute-start | bytes 245768 | tf_op jit(solution)/shard_map/ppermute | solution.py:499
  9.1 0.0 collective-permute-start.3
  9.1 1.3 %cost0.1 = (f32[4,4,16,128]{3,2,1,0:T(8,128)S(1)}, f32[4,8,128]{2,1,0:T(8,128)S(1)}) custom-call(f32[2,80,128]{2,1,0:T(8,128)S(1)} %get-tuple-element.18.refs_0_), custom_call_target="tpu_custom_call" | custom-call | flops 20000000 | bytes 1000 | tf_op jit(solution)/shard_map/cost0/pallas_call | solution.py:389
  10.4 0.0 collective-permute-done.1.refs_1_
  10.4 2.3 %cost1.1 = (f32[8,4,16,128]{3,2,1,0:T(8,128)S(1)}, f32[8,8,128]{2,1,0:T(8,128)S(1)}) custom-call(f32[2,80,128]{2,1,0:T(8,128)S(1)} %get-tuple-element.18.refs_0_, f32[2,80,128]{2,1,0:T(8,128)S(1)} %collective-permute-done.1.refs_1_, f32[4,4,16,128]{3,2,1,0:T(8,128)S(1)} %get-tuple-element.22.refs_2_, f32[4,8,128]{2,1,0:T(8,128)S(1)} %get-tuple-element.23.refs_3_), custom_call_target="tpu_custom_call" | custom-call | flops 40000000 | bytes 1000 | tf_op jit(solution)/shard_map/cost1/pallas_call | solution.py:389
  12.7 0.1 collective-permute-done.2.refs_2_
  12.8 3.1 %cost2.1 = (f32[12,4,16,128]{3,2,1,0:T(8,128)S(1)}, f32[12,8,128]{2,1,0:T(8,128)S(1)}) custom-call(f32[2,80,128]{2,1,0:T(8,128)S(1)} %get-tuple-element.18.refs_0_, f32[2,80,128]{2,1,0:T(8,128)S(1)} %collective-permute-done.1.refs_1_, f32[2,80,128]{2,1,0:T(8,128)S(1)} %collective-permute-done.2.refs_2_, f32[8,4,16,128]{3,2,1,0:T(8,128)S(1)} %get-tuple-element.24.refs_3_, ...), custom_call_target="tpu_custom_call" | custom-call | flops 60000000 | bytes 1000 | tf_op jit(solution)/shard_map/cost2/pallas_call | solution.py:389
  16.0 0.0 collective-permute-done.3.refs_3_
  16.0 0.0 copy-start.1
  16.0 3.4 %cost3.1 = f32[16,128]{1,0:T(8,128)S(1)} custom-call(f32[2,80,128]{2,1,0:T(8,128)S(1)} %get-tuple-element.18.refs_0_, f32[2,80,128]{2,1,0:T(8,128)S(1)} %collective-permute-done.1.refs_1_, f32[2,80,128]{2,1,0:T(8,128)S(1)} %collective-permute-done.2.refs_2_, f32[2,80,128]{2,1,0:T(8,128)S(1)} %collective-permute-done.3.refs_3_, ...), custom_call_target="tpu_custom_call" | custom-call | flops 80000000 | bytes 1000 | tf_op jit(solution)/shard_map/cost3/pallas_call | solution.py:389
  19.4 8.8 %all_to_all.11 = f32[8,2,128]{2,1,0:T(2,128)S(1)} all-to-all(f32[8,2,128]{2,1,0:T(2,128)S(1)} %bitcast.11), channel_id=1, replica_groups=mesh['robot'=8,'seed'=4] {'robot'}, dimensions={0} | all-to-all | bytes 16384 | tf_op jit(solution)/shard_map/all_to_all | solution.py:514
  28.2 0.0 copy-done.1
  28.2 0.7 %blend.1 = (f32[2,256]{1,0:T(2,128)}, f32[80,128]{1,0:T(8,128)S(1)}) custom-call(f32[16,128]{1,0:T(8,128)S(1)} %bitcast.12, f32[624,128]{1,0:T(8,128)S(1)} %bitcast.10), custom_call_target="tpu_custom_call" | custom-call | tf_op jit(solution)/shard_map/blend/pallas_call | solution.py:451
  28.9 3.6 %collective-permute-start.6 = (f32[80,128]{1,0:T(8,128)S(1)}, f32[80,128]{1,0:T(8,128)S(1)}, u32[]{:S(2)}, u32[]{:S(2)}) collective-permute-start(f32[80,128]{1,0:T(8,128)S(1)} %get-tuple-element.29.refs_0_), channel_id=1, source_target_pairs={{0,3},{1,2},{2,1},{3,0},{4,7},{5,6},{6,5},{7,4},{8,11},{9,10},{10,... | collective-permute-start | bytes 122888 | tf_op jit(solution)/shard_map/ppermute | solution.py:499
  32.5 0.0 collective-permute-start.5
  32.5 0.8 %collective-permute-start.4 = (f32[80,128]{1,0:T(8,128)S(1)}, f32[80,128]{1,0:T(8,128)S(1)}, u32[]{:S(2)}, u32[]{:S(2)}) collective-permute-start(f32[80,128]{1,0:T(8,128)S(1)} %get-tuple-element.29.refs_0_), channel_id=1, source_target_pairs={{0,1},{1,0},{2,3},{3,2},{4,5},{5,4},{6,7},{7,6},{8,9},{9,8},{10,11... | collective-permute-start | bytes 122888 | tf_op jit(solution)/shard_map/ppermute | solution.py:499
  33.3 1.6 %collective-permute-done.6.refs_3_ = f32[80,128]{1,0:T(8,128)S(1)} collective-permute-done((f32[80,128]{1,0:T(8,128)S(1)}, f32[80,128]{1,0:T(8,128)S(1)}, u32[]{:S(2)}, u32[]{:S(2)}) %collective-permute-start.6) | collective-permute-done | bytes 40992 | tf_op jit(solution)/shard_map/ppermute | solution.py:499
  34.9 2.5 %collective-permute-done.5.refs_2_ = f32[80,128]{1,0:T(8,128)S(1)} collective-permute-done((f32[80,128]{1,0:T(8,128)S(1)}, f32[80,128]{1,0:T(8,128)S(1)}, u32[]{:S(2)}, u32[]{:S(2)}) %collective-permute-start.5) | collective-permute-done | bytes 40992 | tf_op jit(solution)/shard_map/ppermute | solution.py:499
  37.4 0.0 collective-permute-done.4.refs_1_
  37.4 0.9 %finish.1 = f32[2,3,32,52]{3,2,1,0:T(8,128)} custom-call(f32[80,128]{1,0:T(8,128)S(1)} %get-tuple-element.29.refs_0_, f32[80,128]{1,0:T(8,128)S(1)} %collective-permute-done.4.refs_1_, f32[80,128]{1,0:T(8,128)S(1)} %collective-permute-done.5.refs_2_, f32[80,128]{1,0:T(8,128)S(1)} %collective-permute-done.6.refs_3_), custom_call_target="tpu_custom_call" | custom-call | tf_op jit(solution)/shard_map/finish/pallas_call | solution.py:486
  (1 shorter events, 0.0 us)
Async XLA Ops:
  0.6 0.7 %copy-start.3 = (s32[2,16]{1,0:T(2,128)S(1)}, s32[2,16]{1,0:T(2,128)}, u32[]{:S(2)}) copy-start(s32[2,16]{1,0:T(2,128)} %adjacency_hbm.1) | copy-start | bytes 388
  0.6 0.7 %copy-start.2 = (f32[2,52]{1,0:T(2,128)S(1)}, f32[2,52]{1,0:T(2,128)}, u32[]{:S(2)}) copy-start(f32[2,52]{1,0:T(2,128)} %radius_hbm.1) | copy-start | bytes 1252
  0.7 0.7 %copy-start.4 = (s32[2]{0:T(128)S(1)}, s32[2]{0:T(128)}, u32[]{:S(2)}) copy-start(s32[2]{0:T(128)} %param.6) | copy-start | bytes 28
  1.3 1.0 %copy-start = (f32[2,3,52,256]{3,0,2,1:T(2,128)S(1)}, f32[2,3,52,256]{3,0,2,1:T(2,128)}, u32[]{:S(2)}) copy-start(f32[2,3,52,256]{3,0,2,1:T(2,128)} %param.4) | copy-start | bytes 958468
  3.0 1.6 %collective-permute-start = (f32[4,80,128]{2,1,0:T(8,128)S(1)}, f32[4,80,128]{2,1,0:T(8,128)S(1)}, u32[]{:S(2)}, u32[]{:S(2)}) collective-permute-start(f32[4,80,128]{2,1,0:T(8,128)S(1)} %get-tuple-element.17), channel_id=1, source_target_pairs={{0,4},{4,0},{8,12},{12,8},{16,20},{20,16},{24,28},{28,24},{1,5},{5... | collective-permute-start | bytes 491528 | tf_op jit(solution)/shard_map/ppermute | solution.py:499
  4.7 5.7 %collective-permute-start.1 = (f32[2,80,128]{2,1,0:T(8,128)S(1)}, f32[2,80,128]{2,1,0:T(8,128)S(1)}, u32[]{:S(2)}, u32[]{:S(2)}) collective-permute-start(f32[2,80,128]{2,1,0:T(8,128)S(1)} %get-tuple-element.19), channel_id=1, source_target_pairs={{0,8},{4,12},{8,0},{12,4},{16,24},{20,28},{24,16},{28,20},{1,9},{5... | collective-permute-start | bytes 245768 | tf_op jit(solution)/shard_map/ppermute | solution.py:499
  7.6 5.3 %collective-permute-start.2 = (f32[2,80,128]{2,1,0:T(8,128)S(1)}, f32[2,80,128]{2,1,0:T(8,128)S(1)}, u32[]{:S(2)}, u32[]{:S(2)}) collective-permute-start(f32[2,80,128]{2,1,0:T(8,128)S(1)} %get-tuple-element.20), channel_id=1, source_target_pairs={{0,16},{4,20},{8,24},{12,28},{16,0},{20,4},{24,8},{28,12},{1,17},{... | collective-permute-start | bytes 245768 | tf_op jit(solution)/shard_map/ppermute | solution.py:499
  9.1 6.9 %collective-permute-start.3 = (f32[2,80,128]{2,1,0:T(8,128)S(1)}, f32[2,80,128]{2,1,0:T(8,128)S(1)}, u32[]{:S(2)}, u32[]{:S(2)}) collective-permute-start(f32[2,80,128]{2,1,0:T(8,128)S(1)} %get-tuple-element.21), channel_id=1, source_target_pairs={{0,24},{4,28},{8,16},{12,20},{16,8},{20,12},{24,0},{28,4},{1,25},{... | collective-permute-start | bytes 245768 | tf_op jit(solution)/shard_map/ppermute | solution.py:499
  16.0 12.2 %copy-start.1 = (f32[2,3,52,256]{3,0,2,1:T(2,128)S(1)}, f32[2,3,52,256]{3,0,2,1:T(2,128)}, u32[]{:S(2)}) copy-start(f32[2,3,52,256]{3,0,2,1:T(2,128)} %param.4) | copy-start | bytes 958468
  28.9 6.0 %collective-permute-start.6 = (f32[80,128]{1,0:T(8,128)S(1)}, f32[80,128]{1,0:T(8,128)S(1)}, u32[]{:S(2)}, u32[]{:S(2)}) collective-permute-start(f32[80,128]{1,0:T(8,128)S(1)} %get-tuple-element.29.refs_0_), channel_id=1, source_target_pairs={{0,3},{1,2},{2,1},{3,0},{4,7},{5,6},{6,5},{7,4},{8,11},{9,10},{10,... | collective-permute-start | bytes 122888 | tf_op jit(solution)/shard_map/ppermute | solution.py:499
  32.5 4.9 %collective-permute-start.5 = (f32[80,128]{1,0:T(8,128)S(1)}, f32[80,128]{1,0:T(8,128)S(1)}, u32[]{:S(2)}, u32[]{:S(2)}) collective-permute-start(f32[80,128]{1,0:T(8,128)S(1)} %get-tuple-element.29.refs_0_), channel_id=1, source_target_pairs={{0,2},{1,3},{2,0},{3,1},{4,6},{5,7},{6,4},{7,5},{8,10},{9,11},{10,... | collective-permute-start | bytes 122888 | tf_op jit(solution)/shard_map/ppermute | solution.py:499
  32.5 4.9 %collective-permute-start.4 = (f32[80,128]{1,0:T(8,128)S(1)}, f32[80,128]{1,0:T(8,128)S(1)}, u32[]{:S(2)}, u32[]{:S(2)}) collective-permute-start(f32[80,128]{1,0:T(8,128)S(1)} %get-tuple-element.29.refs_0_), channel_id=1, source_target_pairs={{0,1},{1,0},{2,3},{3,2},{4,5},{5,4},{6,7},{7,6},{8,9},{9,8},{10,11... | collective-permute-start | bytes 122888 | tf_op jit(solution)/shard_map/ppermute | solution.py:499

commit v5 on v4

--- a/solution.py
+++ b/solution.py
@@ -42,6 +42,10 @@
         self.chunk_rows = round_up(self.data_rows + robots_here, SUB)
         self.tiles = columns // LANES
 
+    def arrival(self, stage):
+        k = stage if stage < 2 else 2 * (stage - 1)
+        return k * self.here, self.here if stage < 2 else 2 * self.here
+
 
 def iota(shape, axis):
     return lax.broadcasted_iota(jnp.int32, shape, axis)
@@ -58,16 +62,11 @@
     return middles, radius + 0.5 * jnp.sqrt(squares + 1e-06)
 
 
-def pack_kernel(plan, counts_hbm, radius_hbm, adjacency_hbm, stored_hbm, mine, theirs, *scratch):
-    counts, radius, adjacency, stored, source, sem = scratch
-    me = lax.axis_index("robot")
-    n, g, rows, width, here = plan.spheres, plan.lane_groups, plan.rows, plan.width, plan.here
-    step = plan.tiles * here
+def fetch(plan, sources, stored, lines, counts, radius, adjacency, sem):
+    n = plan.spheres
     copies = [
         pltpu.make_async_copy(src, dst, sem.at[i])
-        for i, (src, dst) in enumerate(
-            zip((stored_hbm, counts_hbm, radius_hbm, adjacency_hbm), (stored, counts, radius, adjacency))
-        )
+        for i, (src, dst) in enumerate(zip(sources, (stored, counts, radius, adjacency)))
     ]
     for copy in copies:
         copy.start()
@@ -75,21 +74,33 @@
         copy.wait()
     lane = iota((1, LANES), 1)
     links = iota((1, plan.slots), 1)
-    heads = []
-    for l in range(here):
+    for l in range(plan.here):
         head = jnp.where(lane == n, counts[:, l : l + 1].astype(jnp.float32), 0.0)
         for h in range(plan.halves):
             bits = jnp.where(
                 (adjacency[l : l + 1, :] != 0) & (links // 16 == h), 1 << (links % 16), 0
             ).astype(jnp.float32)
             head = jnp.where(lane == n + 1 + h, jnp.sum(bits, axis=1, keepdims=True), head)
-        heads.append(head)
+        lines[l : l + 1, :] = head
+        lines[l : l + 1, 0:n] = radius[l : l + 1, :]
     copies[0].wait()
+
+
+def pack_kernel(plan, core, *refs):
+    if core:
+        out, stored, lines, source = refs[4:8]
+        fetch(plan, refs[:4], stored, lines, *refs[8:])
+    else:
+        lines, stored, out, source = refs
+    me = lax.axis_index("robot")
+    n, g, rows, width, here = plan.spheres, plan.lane_groups, plan.rows, plan.width, plan.here
+    step = plan.tiles * here
     if not plan.sweep_late:
         order = iota((n, LANES), 0)
         diagonal = iota((n, n), 0) == iota((n, n), 1)
         for l in range(here):
-            column = jnp.sum(jnp.where(diagonal, radius[l : l + 1, :], 0.0), axis=1, keepdims=True)
+            column = jnp.sum(jnp.where(diagonal, lines[l : l + 1, 0:n], 0.0), axis=1, keepdims=True)
+            count = lines[l : l + 1, n : n + 1].astype(jnp.int32)
             robot = me * here + l
             off = FAR * (1 + order + plan.padded * robot).astype(jnp.float32)
             for t in range(plan.tiles):
@@ -97,7 +108,7 @@
                     stored[pl.ds(c * n * step + t * here + l, n, stride=step), :] for c in range(3)
                 ]
                 fields, swept = sweep(points, iota((n, LANES), 1) % W == W - 1, column)
-                fields[0] = jnp.where(order < counts[:, l : l + 1], fields[0], off)
+                fields[0] = jnp.where(order < count, fields[0], off)
                 for c, x in enumerate(fields + [swept]):
                     source[t, l * 4 + c, 0:n, :] = x
                 if plan.padded > n:
@@ -106,9 +117,8 @@
                     for c in range(4):
                         source[t, l * 4 + c, n:, :] = fill if c == 0 else jnp.ones_like(fill)
     lane_group = iota((rows, LANES), 1) // width
-    for k in [*range(1, plan.group, 2), *range(0, plan.group, 2)]:
-        out = (mine, theirs)[k % 2]
-        dest = me ^ k
+    for k in range(plan.chips):
+        dest = me ^ (2 * k + core)
         tile = dest // g
         spot = dest % g
         for l in range(here):
@@ -123,44 +133,47 @@
                     x = pltpu.roll(x, ((j + g - spot) % g) * width, 1)
                     y = jnp.where(lane_group == j, x, y)
                 at = (l * plan.fields + c) * rows
-                out[k // 2, at : at + rows, :] = y
+                out[k, at : at + rows, :] = y
             at = plan.data_rows + l
-            out[k // 2, at : at + 1, :] = heads[l]
-            out[k // 2, at : at + 1, 0:n] = radius[l : l + 1, :]
-
-
-def pack(plan, counts, radius, adjacency, stored):
-    half = jax.ShapeDtypeStruct((plan.chips, plan.chunk_rows, LANES), jnp.float32)
-    args = (counts.reshape(1, -1), radius, adjacency, stored)
+            out[k, at : at + 1, :] = lines[l : l + 1, :]
+
+
+def pack(plan, core, *args):
+    shapes = [(plan.chips, plan.chunk_rows, LANES)]
     swept = (plan.tiles, plan.here * 4, plan.padded, LANES)
+    scratch = [pltpu.VMEM((SUB, LANES) if plan.sweep_late else swept, jnp.float32)]
+    specs = [VMEM, VMEM]
+    if core:
+        shapes += [args[0].shape, (plan.here, LANES)]
+        scratch += [pltpu.VMEM(x.shape, x.dtype) for x in args[1:]]
+        scratch += [pltpu.SemaphoreType.DMA((len(args),))]
+        specs = [pl.BlockSpec(memory_space=pltpu.HBM)] * len(args)
+        args = [pltpu.with_memory_space_constraint(x, pltpu.HBM) for x in args]
     return pl.pallas_call(
-        functools.partial(pack_kernel, plan),
-        out_shape=[half, half],
-        in_specs=[pl.BlockSpec(memory_space=pltpu.HBM)] * len(args),
-        out_specs=[VMEM, VMEM],
-        scratch_shapes=[pltpu.VMEM(x.shape, x.dtype) for x in args]
-        + [
-            pltpu.VMEM((SUB, LANES) if plan.sweep_late else swept, jnp.float32),
-            pltpu.SemaphoreType.DMA((len(args),)),
-        ],
+        functools.partial(pack_kernel, plan, core),
+        out_shape=[jax.ShapeDtypeStruct(shape, jnp.float32) for shape in shapes],
+        in_specs=specs,
+        out_specs=[VMEM] * len(shapes),
+        scratch_shapes=scratch,
         compiler_params=PARAMS,
-        name="pack",
+        cost_estimate=pl.CostEstimate(flops=4_000_000, bytes_accessed=1000, transcendentals=0),
+        name=f"pack{core}",
     )(*args)
 
 
 def join_kernel(plan, mine, theirs, *outs):
-    for k in range(plan.chips):
-        outs[k][0] = mine[k]
-        outs[k][1] = theirs[k]
+    for k in range(1, plan.chips):
+        outs[k - 1][0] = mine[k]
+        outs[k - 1][1] = theirs[k]
 
 
 def join(plan, mine, theirs):
     pair = jax.ShapeDtypeStruct((2, plan.chunk_rows, LANES), jnp.float32)
     return pl.pallas_call(
         functools.partial(join_kernel, plan),
-        out_shape=[pair] * plan.chips,
+        out_shape=[pair] * (plan.chips - 1),
         in_specs=[VMEM, VMEM],
-        out_specs=[VMEM] * plan.chips,
+        out_specs=[VMEM] * (plan.chips - 1),
         compiler_params=PARAMS,
         name="join",
     )(mine, theirs)
@@ -183,20 +196,24 @@
 def cost_kernel(plan, stage, *refs):
     chunks, refs = refs[: stage + 1], refs[stage + 1 :]
     before, refs = refs[: 2 if stage else 0], refs[2 if stage else 0 :]
-    ends = stage == plan.chips - 1
+    ends = stage == plan.chips
     if ends:
         out, store, totals, blocks, tails, sums, starts, links = refs
     else:
         store, totals, blocks, tails, sums, starts, links = refs
     me = lax.axis_index("robot")
     g, rows, width, here, n = plan.lane_groups, plan.rows, plan.width, plan.here, plan.spheres
-    parts, fresh = plan.parts, 2 * plan.here
-    first_slot = stage * fresh
+    parts = plan.parts
+    first_slot, fresh = plan.arrival(stage)
     deep = parts * SUB
+
+    def chunk_of(slot):
+        k = slot // here
+        return chunks[k].at[0] if k < 2 else chunks[k // 2 + 1].at[k % 2]
 
     def line_of(slot):
         at = plan.data_rows + slot % here
-        return chunks[slot // fresh][slot % fresh // here, at : at + 1, :]
+        return chunk_of(slot)[at : at + 1, :]
 
     for u in range(first_slot + fresh):
         count = line_of(u)[0, n].astype(jnp.int32)
@@ -219,8 +236,8 @@
     last = iota((rows, LANES), 1) % W == W - 1
     for i in range(fresh):
         slot = first_slot + i
-        chunk = chunks[stage].at[i // here]
-        at = i % here * plan.fields * rows
+        chunk = chunk_of(slot)
+        at = slot % here * plan.fields * rows
         fields = [chunk[at + f * rows : at + (f + 1) * rows, :] for f in range(plan.fields)]
         if plan.sweep_late:
             line = line_of(slot)
@@ -378,12 +395,12 @@
 
 
 def cost(plan, stage, chunks, before):
-    fresh, g = 2 * plan.here, plan.lane_groups
-    slots = (stage + 1) * fresh
+    first_slot, fresh = plan.arrival(stage)
+    slots, g = first_slot + fresh, plan.lane_groups
     deep = plan.parts * SUB
     long = round_up(slots * max(plan.rows - SUB, 0) + 2 * SUB, SUB)
     carried = [(slots, 4, deep, LANES), (slots, SUB, LANES)]
-    ends = stage == plan.chips - 1
+    ends = stage == plan.chips
     outs = [(slots, LANES)] if ends else carried
     scratch = (carried if ends else []) + [(fresh, 4, g, deep, LANES), (4, long, LANES), (long, LANES)]
     return pl.pallas_call(
@@ -395,14 +412,40 @@
         + [pltpu.SMEM((slots,), jnp.int32), pltpu.SMEM((fresh,), jnp.int32)],
         compiler_params=PARAMS,
         cost_estimate=pl.CostEstimate(
-            flops=20_000_000 * (stage + 1), bytes_accessed=1000, transcendentals=0
+            flops=10_000_000 * (stage + 1), bytes_accessed=1000, transcendentals=0
         ),
         name=f"cost{stage}",
     )(*chunks, *before)
 
 
-def blend_kernel(plan, seeds_here, costs, stored, cost_out, sums):
-    n, here, g = plan.spheres, plan.here, plan.lane_groups
+def owner_kernel(plan, costs, out):
+    for l in range(plan.here):
+        for t in range(plan.tiles):
+            out[l : l + 1, t * LANES : (t + 1) * LANES] = owned(plan, costs, l, t)
+
+
+def owned(plan, costs, l, t):
+    here, g = plan.here, plan.lane_groups
+    line = costs[t * g * here + l : t * g * here + l + 1, :]
+    for d in range(t * g + 1, (t + 1) * g):
+        line = line + costs[d * here + l : d * here + l + 1, :]
+    return line
+
+
+def owner(plan, costs):
+    return pl.pallas_call(
+        functools.partial(owner_kernel, plan),
+        out_shape=jax.ShapeDtypeStruct((plan.here, plan.columns), jnp.float32),
+        in_specs=[VMEM],
+        out_specs=VMEM,
+        compiler_params=PARAMS,
+        cost_estimate=pl.CostEstimate(flops=4_000_000, bytes_accessed=1000, transcendentals=0),
+        name="owner",
+    )(costs)
+
+
+def blend_kernel(plan, seeds_here, costs, stored, sums):
+    n, here = plan.spheres, plan.here
     n_rows = n // 4
     step = plan.tiles * here
     seed_of = iota((seeds_here, LANES), 1) // W
@@ -410,14 +453,9 @@
     fold = iota((n_rows, LANES), 1) // W
     per_tile = LANES // W
     for l in range(here):
-        lines = []
         seed_cost = jnp.zeros((seeds_here, 1), jnp.float32)
         for t in range(plan.tiles):
-            line = costs[t * g * here + l : t * g * here + l + 1, :]
-            for d in range(t * g + 1, (t + 1) * g):
-                line = line + costs[d * here + l : d * here + l + 1, :]
-            cost_out[l : l + 1, t * LANES : (t + 1) * LANES] = line
-            lines.append(line)
+            line = owned(plan, costs, l, t)
             mine = seed_of + t * per_tile == seed
             seed_cost = seed_cost + jnp.sum(jnp.where(mine, line, 0.0), axis=1, keepdims=True)
         weight = 1.0 / (1.0 + seed_cost)
@@ -450,12 +488,9 @@
     rows = round_up(plan.here * (3 * plan.spheres // 4 + 1), SUB)
     return pl.pallas_call(
         functools.partial(blend_kernel, plan, seeds_here),
-        out_shape=[
-            jax.ShapeDtypeStruct((plan.here, plan.columns), jnp.float32),
-            jax.ShapeDtypeStruct((rows, LANES), jnp.float32),
-        ],
+        out_shape=jax.ShapeDtypeStruct((rows, LANES), jnp.float32),
         in_specs=[VMEM, VMEM],
-        out_specs=[VMEM, VMEM],
+        out_specs=VMEM,
         compiler_params=PARAMS,
         name="blend",
     )(costs, stored)
@@ -504,17 +539,21 @@
     plan = Plan(lax.axis_size("robot"), here, spheres, columns)
     stored = centres.reshape(here, 3, spheres, plan.tiles, LANES)
     stored = stored.transpose(1, 2, 3, 0, 4).reshape(-1, LANES)
-    mine, theirs = pack(plan, counts, sphere_radius, adjacency, stored)
-    chunks = join(plan, mine, exchanged(theirs, "robot", 1))
-    chunks = [chunks[0]] + [exchanged(chunks[k], "robot", 2 * k) for k in range(1, plan.chips)]
-    carried = []
-    for stage in range(plan.chips):
+    theirs, stored, lines = pack(plan, 1, stored, counts.reshape(1, -1), sphere_radius, adjacency)
+    theirs = exchanged(theirs, "robot", 1)
+    (mine,) = pack(plan, 0, lines, stored)
+    carried = cost(plan, 0, [mine], [])
+    mine, *carried = lax.optimization_barrier((mine, *carried))
+    chunks = [mine, theirs]
+    for k, pair in enumerate(join(plan, mine, theirs), 1):
+        chunks.append(exchanged(pair, "robot", 2 * k))
+    for stage in range(1, plan.chips + 1):
         carried = cost(plan, stage, chunks[: stage + 1], carried)
     (costs,) = carried
     costs = lax.all_to_all(costs, "robot", 0, 0, tiled=True)
-    robot_cost, sums = blend(plan, costs, stored)
+    sums = blend(plan, costs, stored)
     parts = [sums] + [exchanged(sums, "seed", k) for k in range(1, lax.axis_size("seed"))]
-    return robot_cost, finish(plan, parts).transpose(0, 1, 3, 2)
+    return owner(plan, costs), finish(plan, parts).transpose(0, 1, 3, 2)
 
 
 def solution(mesh):

time: 39 us -> 37.9 us (0.972)
  Pallas kernels: 12.4 us -> 14.2 us
  local copies, waits for them, and re-layouts: 1.65 us -> 0 us
  blocking collectives: 8.76 us -> 7.84 us
    unnamed x10 -> x0, local copies, waits for them, and re-layouts: 1.65 us -> none
    pallas_call x2 -> x4, Pallas kernels: 0.75 us -> 2.18 us  [the longest x2 1.58 us: pack(): pl.pallas_call(functools.partial(pack_kernel, plan, core), out_shape=[jax...]
    all_to_all x1, blocking collectives: 8.76 us -> 7.84 us  [local(): costs = lax.all_to_all(costs, 'robot', 0, 0, tiled=True)]
    pallas_call x4 -> x5, Pallas kernels: 10.1 us -> 10.9 us  [cost(): pl.pallas_call(functools.partial(cost_kernel, plan, stage), out_shape=[ja...]
    pallas_call x1, Pallas kernels: 0.73 us -> 0.23 us  [blend(): pl.pallas_call(functools.partial(blend_kernel, plan, seeds_here), out_sha...]
  transfers between devices with their start and end apart: 7 -> 7, of which waited for: 4 -> 5; matrix products, arithmetic and copies ran while one was open for 0% -> 0% of each run, Pallas kernels for 18% -> 20%
where the time goes in v5:
time: 37.9 us; the launch traced here: 37.3 us
  Pallas kernels  14.2 us (37%)
  starting transfers between devices  9.46 us (25%)
  blocking collectives  7.84 us (21%)
  waiting for transfers between devices  5.12 us (14%)
  between operations  0.71 us (2%)
    pallas_call x5, Pallas kernels, cost(): pl.pallas_call(functools.partial(cost_kernel, plan, stage), out_shape=[ja...  10.9 us
    ppermute x7, starting transfers between devices, exchanged(): return lax.ppermute(block, axis, [(i, i ^ k) for i in range(size)])  9.46 us
    all_to_all x1, blocking collectives, local(): costs = lax.all_to_all(costs, 'robot', 0, 0, tiled=True)  7.84 us
    ppermute x7, waiting for transfers between devices, exchanged(): return lax.ppermute(block, axis, [(i, i ^ k) for i in range(size)])  5.12 us
    pallas_call x2, Pallas kernels, pack(): pl.pallas_call(functools.partial(pack_kernel, plan, core), out_shape=[jax...  1.58 us
    pallas_call x1, Pallas kernels, finish(): pl.pallas_call(functools.partial(finish_kernel, plan), out_shape=jax.Shap...  0.86 us
  transfers between devices with their start and end apart: 7, of which 5 were waited for; matrix products, arithmetic and copies ran while one was open for 0% of the time, Pallas kernels for 20%

profile of v5, /device:TPU:0, one launch (start us, length us, event | category | flops | bytes accessed | tf_op | source)
XLA Modules:
  0.0 37.3 jit_solution(10206608877428785112)
XLA Ops:
  0.6 1.3 %pack1.1 = (f32[4,80,128]{2,1,0:T(8,128)S(1)}, f32[624,128]{1,0:T(8,128)S(1)}, f32[2,128]{1,0:T(2,128)S(1)}) custom-call(f32[624,128]{1,0:T(8,128)} %bitcast.12, s32[1,2]{1,0:T(1,128)} %bitcast.14, f32[2,52]{1,0:T(2,128)} %refs_2_.1, s32[2,16]{1,0:T(2,128)} %refs_3_.1), custom_call_target="tpu_custom_call" | custom-call | flops 4000000 | bytes 1000 | tf_op jit(solution)/shard_map/pack1/pallas_call | solution.py:152
  1.9 0.6 %collective-permute-start = (f32[4,80,128]{2,1,0:T(8,128)S(1)}, f32[4,80,128]{2,1,0:T(8,128)S(1)}, u32[]{:S(2)}, u32[]{:S(2)}) collective-permute-start(f32[4,80,128]{2,1,0:T(8,128)S(1)} %get-tuple-element.24), channel_id=1, source_target_pairs={{0,4},{4,0},{8,12},{12,8},{16,20},{20,16},{24,28},{28,24},{1,5},{5... | collective-permute-start | bytes 491528 | tf_op jit(solution)/shard_map/ppermute | solution.py:534
  2.5 0.3 pack0.1.refs_0_.mine
  2.8 0.6 %cost0.1 = (f32[2,4,16,128]{3,2,1,0:T(8,128)S(1)}, f32[2,8,128]{2,1,0:T(8,128)S(1)}) custom-call(f32[4,80,128]{2,1,0:T(8,128)S(1)} %pack0.1.refs_0_.mine), custom_call_target="tpu_custom_call" | custom-call | flops 10000000 | bytes 1000 | tf_op jit(solution)/shard_map/cost0/pallas_call | solution.py:406
  3.4 0.2 collective-permute-done.theirs.refs_1_
  3.5 2.9 %collective-permute-start.1 = (f32[2,80,128]{2,1,0:T(8,128)S(1)}, f32[2,80,128]{2,1,0:T(8,128)S(1)}, u32[]{:S(2)}, u32[]{:S(2)}) collective-permute-start(f32[2,80,128]{2,1,0:T(8,128)S(1)} %get-tuple-element.25), channel_id=1, source_target_pairs={{0,8},{4,12},{8,0},{12,4},{16,24},{20,28},{24,16},{28,20},{1,9},{5... | collective-permute-start | bytes 245768 | tf_op jit(solution)/shard_map/ppermute | solution.py:534
  6.4 1.5 %collective-permute-start.2 = (f32[2,80,128]{2,1,0:T(8,128)S(1)}, f32[2,80,128]{2,1,0:T(8,128)S(1)}, u32[]{:S(2)}, u32[]{:S(2)}) collective-permute-start(f32[2,80,128]{2,1,0:T(8,128)S(1)} %get-tuple-element.26), channel_id=1, source_target_pairs={{0,16},{4,20},{8,24},{12,28},{16,0},{20,4},{24,8},{28,12},{1,17},{... | collective-permute-start | bytes 245768 | tf_op jit(solution)/shard_map/ppermute | solution.py:534
  8.0 0.0 collective-permute-start.3
  8.0 0.5 %cost1.1 = (f32[4,4,16,128]{3,2,1,0:T(8,128)S(1)}, f32[4,8,128]{2,1,0:T(8,128)S(1)}) custom-call(f32[4,80,128]{2,1,0:T(8,128)S(1)} %pack0.1.refs_0_.mine, f32[4,80,128]{2,1,0:T(8,128)S(1)} %collective-permute-done.theirs.refs_1_, f32[2,4,16,128]{3,2,1,0:T(8,128)S(1)} %get-tuple-element.28.refs_2_, f32[2,8,128]{2,1,0:T(8,128)S(1)} %get-tuple-element.29.refs_3_), custom_call_target="tpu_custom_call" | custom-call | flops 20000000 | bytes 1000 | tf_op jit(solution)/shard_map/cost1/pallas_call | solution.py:406
  8.5 0.7 %collective-permute-done.1.refs_2_ = f32[2,80,128]{2,1,0:T(8,128)S(1)} collective-permute-done((f32[2,80,128]{2,1,0:T(8,128)S(1)}, f32[2,80,128]{2,1,0:T(8,128)S(1)}, u32[]{:S(2)}, u32[]{:S(2)}) %collective-permute-start.1) | collective-permute-done | bytes 81952 | tf_op jit(solution)/shard_map/ppermute | solution.py:534
  9.2 1.8 %cost2.1 = (f32[8,4,16,128]{3,2,1,0:T(8,128)S(1)}, f32[8,8,128]{2,1,0:T(8,128)S(1)}) custom-call(f32[4,80,128]{2,1,0:T(8,128)S(1)} %pack0.1.refs_0_.mine, f32[4,80,128]{2,1,0:T(8,128)S(1)} %collective-permute-done.theirs.refs_1_, f32[2,80,128]{2,1,0:T(8,128)S(1)} %collective-permute-done.1.refs_2_, f32[4,4,16,128]{3,2,1,0:T(8,128)S(1)} %get-tuple-element.30.refs_3_, ...), custom_call_target="tpu_custom_call" | custom-call | flops 30000000 | bytes 1000 | tf_op jit(solution)/shard_map/cost2/pallas_call | solution.py:406
  11.0 0.7 %collective-permute-done.2.refs_3_ = f32[2,80,128]{2,1,0:T(8,128)S(1)} collective-permute-done((f32[2,80,128]{2,1,0:T(8,128)S(1)}, f32[2,80,128]{2,1,0:T(8,128)S(1)}, u32[]{:S(2)}, u32[]{:S(2)}) %collective-permute-start.2) | collective-permute-done | bytes 81952 | tf_op jit(solution)/shard_map/ppermute | solution.py:534
  11.7 3.6 %cost3.1 = (f32[12,4,16,128]{3,2,1,0:T(8,128)S(1)}, f32[12,8,128]{2,1,0:T(8,128)S(1)}) custom-call(f32[4,80,128]{2,1,0:T(8,128)S(1)} %pack0.1.refs_0_.mine, f32[4,80,128]{2,1,0:T(8,128)S(1)} %collective-permute-done.theirs.refs_1_, f32[2,80,128]{2,1,0:T(8,128)S(1)} %collective-permute-done.1.refs_2_, f32[2,80,128]{2,1,0:T(8,128)S(1)} %collective-permute-done.2.refs_3_, ...), custom_call_target="tpu_custom_call" | custom-call | flops 40000000 | bytes 1000 | tf_op jit(solution)/shard_map/cost3/pallas_call | solution.py:406
  15.3 0.0 collective-permute-done.3.refs_4_
  15.4 4.4 %cost4.1 = f32[16,128]{1,0:T(8,128)S(1)} custom-call(f32[4,80,128]{2,1,0:T(8,128)S(1)} %pack0.1.refs_0_.mine, f32[4,80,128]{2,1,0:T(8,128)S(1)} %collective-permute-done.theirs.refs_1_, f32[2,80,128]{2,1,0:T(8,128)S(1)} %collective-permute-done.1.refs_2_, f32[2,80,128]{2,1,0:T(8,128)S(1)} %collective-permute-done.2.refs_3_, ...), custom_call_target="tpu_custom_call" | custom-call | flops 50000000 | bytes 1000 | tf_op jit(solution)/shard_map/cost4/pallas_call | solution.py:406
  19.8 7.8 %all_to_all.11 = f32[8,2,128]{2,1,0:T(2,128)S(1)} all-to-all(f32[8,2,128]{2,1,0:T(2,128)S(1)} %bitcast.9), channel_id=1, replica_groups=mesh['robot'=8,'seed'=4] {'robot'}, dimensions={0} | all-to-all | bytes 16384 | tf_op jit(solution)/shard_map/all_to_all | solution.py:553
  27.6 0.2 blend.1.refs_0_
  27.9 3.7 %collective-permute-start.6 = (f32[80,128]{1,0:T(8,128)S(1)}, f32[80,128]{1,0:T(8,128)S(1)}, u32[]{:S(2)}, u32[]{:S(2)}) collective-permute-start(f32[80,128]{1,0:T(8,128)S(1)} %blend.1.refs_0_), channel_id=1, source_target_pairs={{0,3},{1,2},{2,1},{3,0},{4,7},{5,6},{6,5},{7,4},{8,11},{9,10},{10,... | collective-permute-start | bytes 122888 | tf_op jit(solution)/shard_map/ppermute | solution.py:534
  31.5 0.0 collective-permute-start.5
  31.5 0.8 %collective-permute-start.4 = (f32[80,128]{1,0:T(8,128)S(1)}, f32[80,128]{1,0:T(8,128)S(1)}, u32[]{:S(2)}, u32[]{:S(2)}) collective-permute-start(f32[80,128]{1,0:T(8,128)S(1)} %blend.1.refs_0_), channel_id=1, source_target_pairs={{0,1},{1,0},{2,3},{3,2},{4,5},{5,4},{6,7},{7,6},{8,9},{9,8},{10,11... | collective-permute-start | bytes 122888 | tf_op jit(solution)/shard_map/ppermute | solution.py:534
  32.3 0.6 %owner.1 = f32[2,256]{1,0:T(2,128)} custom-call(f32[16,128]{1,0:T(8,128)S(1)} %bitcast.11), custom_call_target="tpu_custom_call" | custom-call | flops 4000000 | bytes 1000 | tf_op jit(solution)/shard_map/owner/pallas_call | solution.py:436
  32.9 1.0 %collective-permute-done.6.refs_3_ = f32[80,128]{1,0:T(8,128)S(1)} collective-permute-done((f32[80,128]{1,0:T(8,128)S(1)}, f32[80,128]{1,0:T(8,128)S(1)}, u32[]{:S(2)}, u32[]{:S(2)}) %collective-permute-start.6) | collective-permute-done | bytes 40992 | tf_op jit(solution)/shard_map/ppermute | solution.py:534
  33.9 2.5 %collective-permute-done.5.refs_2_ = f32[80,128]{1,0:T(8,128)S(1)} collective-permute-done((f32[80,128]{1,0:T(8,128)S(1)}, f32[80,128]{1,0:T(8,128)S(1)}, u32[]{:S(2)}, u32[]{:S(2)}) %collective-permute-start.5) | collective-permute-done | bytes 40992 | tf_op jit(solution)/shard_map/ppermute | solution.py:534
  36.4 0.0 collective-permute-done.4.refs_1_
  36.4 0.9 %finish.1 = f32[2,3,32,52]{3,2,1,0:T(8,128)} custom-call(f32[80,128]{1,0:T(8,128)S(1)} %blend.1.refs_0_, f32[80,128]{1,0:T(8,128)S(1)} %collective-permute-done.4.refs_1_, f32[80,128]{1,0:T(8,128)S(1)} %collective-permute-done.5.refs_2_, f32[80,128]{1,0:T(8,128)S(1)} %collective-permute-done.6.refs_3_), custom_call_target="tpu_custom_call" | custom-call | tf_op jit(solution)/shard_map/finish/pallas_call | solution.py:521
  (1 shorter events, 0.0 us)
Async XLA Ops:
  1.9 1.6 %collective-permute-start = (f32[4,80,128]{2,1,0:T(8,128)S(1)}, f32[4,80,128]{2,1,0:T(8,128)S(1)}, u32[]{:S(2)}, u32[]{:S(2)}) collective-permute-start(f32[4,80,128]{2,1,0:T(8,128)S(1)} %get-tuple-element.24), channel_id=1, source_target_pairs={{0,4},{4,0},{8,12},{12,8},{16,20},{20,16},{24,28},{28,24},{1,5},{5... | collective-permute-start | bytes 491528 | tf_op jit(solution)/shard_map/ppermute | solution.py:534
  3.5 5.7 %collective-permute-start.1 = (f32[2,80,128]{2,1,0:T(8,128)S(1)}, f32[2,80,128]{2,1,0:T(8,128)S(1)}, u32[]{:S(2)}, u32[]{:S(2)}) collective-permute-start(f32[2,80,128]{2,1,0:T(8,128)S(1)} %get-tuple-element.25), channel_id=1, source_target_pairs={{0,8},{4,12},{8,0},{12,4},{16,24},{20,28},{24,16},{28,20},{1,9},{5... | collective-permute-start | bytes 245768 | tf_op jit(solution)/shard_map/ppermute | solution.py:534
  6.4 5.3 %collective-permute-start.2 = (f32[2,80,128]{2,1,0:T(8,128)S(1)}, f32[2,80,128]{2,1,0:T(8,128)S(1)}, u32[]{:S(2)}, u32[]{:S(2)}) collective-permute-start(f32[2,80,128]{2,1,0:T(8,128)S(1)} %get-tuple-element.26), channel_id=1, source_target_pairs={{0,16},{4,20},{8,24},{12,28},{16,0},{20,4},{24,8},{28,12},{1,17},{... | collective-permute-start | bytes 245768 | tf_op jit(solution)/shard_map/ppermute | solution.py:534
  8.0 7.4 %collective-permute-start.3 = (f32[2,80,128]{2,1,0:T(8,128)S(1)}, f32[2,80,128]{2,1,0:T(8,128)S(1)}, u32[]{:S(2)}, u32[]{:S(2)}) collective-permute-start(f32[2,80,128]{2,1,0:T(8,128)S(1)} %get-tuple-element.27), channel_id=1, source_target_pairs={{0,24},{4,28},{8,16},{12,20},{16,8},{20,12},{24,0},{28,4},{1,25},{... | collective-permute-start | bytes 245768 | tf_op jit(solution)/shard_map/ppermute | solution.py:534
  27.9 6.1 %collective-permute-start.6 = (f32[80,128]{1,0:T(8,128)S(1)}, f32[80,128]{1,0:T(8,128)S(1)}, u32[]{:S(2)}, u32[]{:S(2)}) collective-permute-start(f32[80,128]{1,0:T(8,128)S(1)} %blend.1.refs_0_), channel_id=1, source_target_pairs={{0,3},{1,2},{2,1},{3,0},{4,7},{5,6},{6,5},{7,4},{8,11},{9,10},{10,... | collective-permute-start | bytes 122888 | tf_op jit(solution)/shard_map/ppermute | solution.py:534
  31.5 4.9 %collective-permute-start.5 = (f32[80,128]{1,0:T(8,128)S(1)}, f32[80,128]{1,0:T(8,128)S(1)}, u32[]{:S(2)}, u32[]{:S(2)}) collective-permute-start(f32[80,128]{1,0:T(8,128)S(1)} %blend.1.refs_0_), channel_id=1, source_target_pairs={{0,2},{1,3},{2,0},{3,1},{4,6},{5,7},{6,4},{7,5},{8,10},{9,11},{10,... | collective-permute-start | bytes 122888 | tf_op jit(solution)/shard_map/ppermute | solution.py:534
  31.5 4.9 %collective-permute-start.4 = (f32[80,128]{1,0:T(8,128)S(1)}, f32[80,128]{1,0:T(8,128)S(1)}, u32[]{:S(2)}, u32[]{:S(2)}) collective-permute-start(f32[80,128]{1,0:T(8,128)S(1)} %blend.1.refs_0_), channel_id=1, source_target_pairs={{0,1},{1,0},{2,3},{3,2},{4,5},{5,4},{6,7},{7,6},{8,9},{9,8},{10,11... | collective-permute-start | bytes 122888 | tf_op jit(solution)/shard_map/ppermute | solution.py:534

commit v6 on v5

--- a/solution.py
+++ b/solution.py
@@ -13,6 +13,7 @@
 SUB = 8
 SCALE = math.sqrt(math.log2(math.e))
 FAR = 1e15
+COUNTS = 64
 VMEM = pl.BlockSpec(memory_space=pltpu.VMEM)
 SMEM = pl.BlockSpec(memory_space=pltpu.SMEM)
 PARAMS = pltpu.CompilerParams(vmem_limit_bytes=16 * 1024 * 1024)
@@ -75,12 +76,15 @@
     lane = iota((1, LANES), 1)
     links = iota((1, plan.slots), 1)
     for l in range(plan.here):
-        head = jnp.where(lane == n, counts[:, l : l + 1].astype(jnp.float32), 0.0)
+        head = jnp.zeros((1, LANES), jnp.float32)
         for h in range(plan.halves):
             bits = jnp.where(
                 (adjacency[l : l + 1, :] != 0) & (links // 16 == h), 1 << (links % 16), 0
-            ).astype(jnp.float32)
-            head = jnp.where(lane == n + 1 + h, jnp.sum(bits, axis=1, keepdims=True), head)
+            )
+            value = jnp.sum(bits.astype(jnp.float32), axis=1, keepdims=True)
+            if h == 0:
+                value = value * COUNTS + counts[:, l : l + 1].astype(jnp.float32)
+            head = jnp.where(lane == n + h, value, head)
         lines[l : l + 1, :] = head
         lines[l : l + 1, 0:n] = radius[l : l + 1, :]
     copies[0].wait()
@@ -100,7 +104,7 @@
         diagonal = iota((n, n), 0) == iota((n, n), 1)
         for l in range(here):
             column = jnp.sum(jnp.where(diagonal, lines[l : l + 1, 0:n], 0.0), axis=1, keepdims=True)
-            count = lines[l : l + 1, n : n + 1].astype(jnp.int32)
+            count = lines[l : l + 1, n : n + 1].astype(jnp.int32) % COUNTS
             robot = me * here + l
             off = FAR * (1 + order + plan.padded * robot).astype(jnp.float32)
             for t in range(plan.tiles):
@@ -215,14 +219,29 @@
         at = plan.data_rows + slot % here
         return chunk_of(slot)[at : at + 1, :]
 
-    for u in range(first_slot + fresh):
-        count = line_of(u)[0, n].astype(jnp.int32)
-        starts[u] = jnp.minimum((count + g - 1) // g, rows)
+    per_word = 8
+    words = []
+    if parts > 1:
+        for at in range(0, first_slot, per_word):
+            word = before[1][first_slot, 0:1, :][0, at // per_word].astype(jnp.int32)
+            words.append(word)
+            for u in range(at, min(at + per_word, first_slot)):
+                starts[u] = SUB + ((word >> (3 * (u - at))) & 7)
     for i in range(fresh):
-        line = line_of(first_slot + i)
-        bits = line[0, n + 1].astype(jnp.int32)
+        slot = first_slot + i
+        line = line_of(slot)
+        bits = line[0, n].astype(jnp.int32)
+        count = bits % COUNTS
+        bits = bits // COUNTS
         for h in range(1, plan.halves):
-            bits = bits | (line[0, n + 1 + h].astype(jnp.int32) << (16 * h))
+            bits = bits | (line[0, n + h].astype(jnp.int32) << (16 * h))
+        filled = jnp.minimum((count + g - 1) // g, rows)
+        starts[slot] = filled
+        if parts > 1:
+            if slot % per_word == 0:
+                words.append(jnp.int32(0))
+            more = jnp.maximum(filled - SUB, 0)
+            words[-1] = words[-1] + (more << (3 * (slot % per_word)))
         step = 1
         while step < plan.slots:
             low = sum(1 << b for b in range(plan.slots) if not b & step)
@@ -251,14 +270,14 @@
                 for p in range(parts)
             ]
             fields, swept = sweep(fields, last, jnp.concatenate(radius, axis=0)[:rows])
-            count = line[:, n : n + 1].astype(jnp.int32)
+            count = line[:, n : n + 1].astype(jnp.int32) % COUNTS
             off = FAR * (1 + sphere + plan.padded * slot).astype(jnp.float32)
             fields[0] = jnp.where(sphere < count, fields[0], off)
             fields.append(swept)
         for c in range(4):
             x = fields[c]
-            for m in range(g):
-                blocks[i, c, m, 0:rows, :] = pltpu.roll(x, m * width, 1) if m else x
+            for m in range(1, g):
+                blocks[i, c, m, 0:rows, :] = pltpu.roll(x, m * width, 1)
             store[slot, c, 0:rows, :] = x
             if deep > rows:
                 fill = jnp.full((deep - rows, LANES), -FAR if c == 0 else 1.0, jnp.float32)
@@ -267,8 +286,16 @@
     for u in range(first_slot):
         store[u] = before[0][u]
         totals[u] = before[1][u]
+    if parts > 1 and not ends:
+        lane = iota((SUB, LANES), 1)
+        line = jnp.zeros((SUB, LANES), jnp.float32)
+        for at, word in enumerate(words):
+            line = jnp.where(lane == at, word.astype(jnp.float32), line)
+        totals[first_slot + fresh] = line
 
     def row(i, m, r):
+        if m == 0:
+            return [store[first_slot + i, c, r : r + 1, :] for c in range(4)]
         return [blocks[i, c, m, r : r + 1, :] for c in range(4)]
 
     def part(slot, p):
@@ -296,7 +323,7 @@
                     keep = sub < d
                 else:
                     keep = None
-                first = [blocks[u, c, m, 0:SUB, :] for c in range(4)]
+                first = [blocks[u, c, m, 0:SUB, :] for c in range(4)] if m else second
                 total = total + masked(term(first, turned), keep)
         for r in range(SUB, high):
             for p in range(parts):
@@ -386,10 +413,7 @@
     for k in range(plan.group):
         for l in range(here):
             value = jnp.sum(totals[k * here + l], axis=0, keepdims=True)
-            shift = width
-            while shift < LANES:
-                value = value + pltpu.roll(value, shift, 1)
-                shift *= 2
+            value = sum([pltpu.roll(value, m * width, 1) for m in range(1, g)], value)
             value = jnp.where(spot, value, 0.0) / (n * n)
             out[pl.ds((me ^ k) * here + l, 1), :] = value
 
@@ -399,7 +423,7 @@
     slots, g = first_slot + fresh, plan.lane_groups
     deep = plan.parts * SUB
     long = round_up(slots * max(plan.rows - SUB, 0) + 2 * SUB, SUB)
-    carried = [(slots, 4, deep, LANES), (slots, SUB, LANES)]
+    carried = [(slots, 4, deep, LANES), (slots + 1, SUB, LANES)]
     ends = stage == plan.chips
     outs = [(slots, LANES)] if ends else carried
     scratch = (carried if ends else []) + [(fresh, 4, g, deep, LANES), (4, long, LANES), (long, LANES)]

time: 37.9 us -> 36.9 us (0.974)
  waiting for transfers between devices: 5.12 us -> 4.28 us
  blocking collectives: 7.84 us -> 8.6 us
  Pallas kernels: 14.2 us -> 13.6 us
    ppermute x7, waiting for transfers between devices: 5.12 us -> 4.28 us  [exchanged(): return lax.ppermute(block, axis, [(i, i ^ k) for i in range(size)])]
    all_to_all x1, blocking collectives: 7.84 us -> 8.6 us  [local(): costs = lax.all_to_all(costs, 'robot', 0, 0, tiled=True)]
    pallas_call x5, Pallas kernels: 10.9 us -> 10.3 us  [cost(): pl.pallas_call(functools.partial(cost_kernel, plan, stage), out_shape=[ja...]
  transfers between devices with their start and end apart: 7 -> 7, of which waited for: 5 -> 5; matrix products, arithmetic and copies ran while one was open for 0% -> 0% of each run, Pallas kernels for 20% -> 19%
where the time goes in v6:
time: 36.9 us; the launch traced here: 36.6 us
  Pallas kernels  13.6 us (37%)
  starting transfers between devices  9.46 us (26%)
  blocking collectives  8.6 us (23%)
  waiting for transfers between devices  4.28 us (12%)
  between operations  0.71 us (2%)
    pallas_call x5, Pallas kernels, cost(): pl.pallas_call(functools.partial(cost_kernel, plan, stage), out_shape=[ja...  10.3 us
    ppermute x7, starting transfers between devices, exchanged(): return lax.ppermute(block, axis, [(i, i ^ k) for i in range(size)])  9.46 us
    all_to_all x1, blocking collectives, local(): costs = lax.all_to_all(costs, 'robot', 0, 0, tiled=True)  8.6 us
    ppermute x7, waiting for transfers between devices, exchanged(): return lax.ppermute(block, axis, [(i, i ^ k) for i in range(size)])  4.28 us
    pallas_call x2, Pallas kernels, pack(): pl.pallas_call(functools.partial(pack_kernel, plan, core), out_shape=[jax...  1.59 us
    pallas_call x1, Pallas kernels, finish(): pl.pallas_call(functools.partial(finish_kernel, plan), out_shape=jax.Shap...  0.86 us
  transfers between devices with their start and end apart: 7, of which 5 were waited for; matrix products, arithmetic and copies ran while one was open for 0% of the time, Pallas kernels for 19%

profile of v6, /device:TPU:0, one launch (start us, length us, event | category | flops | bytes accessed | tf_op | source)
XLA Modules:
  0.0 36.6 jit_solution(5178954551117790338)
XLA Ops:
  0.6 1.3 %pack1.1 = (f32[4,80,128]{2,1,0:T(8,128)S(1)}, f32[624,128]{1,0:T(8,128)S(1)}, f32[2,128]{1,0:T(2,128)S(1)}) custom-call(f32[624,128]{1,0:T(8,128)} %bitcast.12, s32[1,2]{1,0:T(1,128)} %bitcast.14, f32[2,52]{1,0:T(2,128)} %refs_2_.1, s32[2,16]{1,0:T(2,128)} %refs_3_.1), custom_call_target="tpu_custom_call" | custom-call | flops 4000000 | bytes 1000 | tf_op jit(solution)/shard_map/pack1/pallas_call | solution.py:156
  1.9 0.6 %collective-permute-start = (f32[4,80,128]{2,1,0:T(8,128)S(1)}, f32[4,80,128]{2,1,0:T(8,128)S(1)}, u32[]{:S(2)}, u32[]{:S(2)}) collective-permute-start(f32[4,80,128]{2,1,0:T(8,128)S(1)} %get-tuple-element.24), channel_id=1, source_target_pairs={{0,4},{4,0},{8,12},{12,8},{16,20},{20,16},{24,28},{28,24},{1,5},{5... | collective-permute-start | bytes 491528 | tf_op jit(solution)/shard_map/ppermute | solution.py:558
  2.5 0.3 pack0.1.refs_0_.mine
  2.8 0.6 %cost0.1 = (f32[2,4,16,128]{3,2,1,0:T(8,128)S(1)}, f32[3,8,128]{2,1,0:T(8,128)S(1)}) custom-call(f32[4,80,128]{2,1,0:T(8,128)S(1)} %pack0.1.refs_0_.mine), custom_call_target="tpu_custom_call" | custom-call | flops 10000000 | bytes 1000 | tf_op jit(solution)/shard_map/cost0/pallas_call | solution.py:430
  3.4 0.1 collective-permute-done.theirs.refs_1_
  3.5 2.9 %collective-permute-start.1 = (f32[2,80,128]{2,1,0:T(8,128)S(1)}, f32[2,80,128]{2,1,0:T(8,128)S(1)}, u32[]{:S(2)}, u32[]{:S(2)}) collective-permute-start(f32[2,80,128]{2,1,0:T(8,128)S(1)} %get-tuple-element.25), channel_id=1, source_target_pairs={{0,8},{4,12},{8,0},{12,4},{16,24},{20,28},{24,16},{28,20},{1,9},{5... | collective-permute-start | bytes 245768 | tf_op jit(solution)/shard_map/ppermute | solution.py:558
  6.5 1.5 %collective-permute-start.2 = (f32[2,80,128]{2,1,0:T(8,128)S(1)}, f32[2,80,128]{2,1,0:T(8,128)S(1)}, u32[]{:S(2)}, u32[]{:S(2)}) collective-permute-start(f32[2,80,128]{2,1,0:T(8,128)S(1)} %get-tuple-element.26), channel_id=1, source_target_pairs={{0,16},{4,20},{8,24},{12,28},{16,0},{20,4},{24,8},{28,12},{1,17},{... | collective-permute-start | bytes 245768 | tf_op jit(solution)/shard_map/ppermute | solution.py:558
  8.0 0.0 collective-permute-start.3
  8.0 1.0 %cost1.1 = (f32[4,4,16,128]{3,2,1,0:T(8,128)S(1)}, f32[5,8,128]{2,1,0:T(8,128)S(1)}) custom-call(f32[4,80,128]{2,1,0:T(8,128)S(1)} %pack0.1.refs_0_.mine, f32[4,80,128]{2,1,0:T(8,128)S(1)} %collective-permute-done.theirs.refs_1_, f32[2,4,16,128]{3,2,1,0:T(8,128)S(1)} %get-tuple-element.28.refs_2_, f32[3,8,128]{2,1,0:T(8,128)S(1)} %get-tuple-element.29.refs_3_), custom_call_target="tpu_custom_call" | custom-call | flops 20000000 | bytes 1000 | tf_op jit(solution)/shard_map/cost1/pallas_call | solution.py:430
  9.0 0.2 collective-permute-done.1.refs_2_
  9.2 2.1 %cost2.1 = (f32[8,4,16,128]{3,2,1,0:T(8,128)S(1)}, f32[9,8,128]{2,1,0:T(8,128)S(1)}) custom-call(f32[4,80,128]{2,1,0:T(8,128)S(1)} %pack0.1.refs_0_.mine, f32[4,80,128]{2,1,0:T(8,128)S(1)} %collective-permute-done.theirs.refs_1_, f32[2,80,128]{2,1,0:T(8,128)S(1)} %collective-permute-done.1.refs_2_, f32[4,4,16,128]{3,2,1,0:T(8,128)S(1)} %get-tuple-element.30.refs_3_, ...), custom_call_target="tpu_custom_call" | custom-call | flops 30000000 | bytes 1000 | tf_op jit(solution)/shard_map/cost2/pallas_call | solution.py:430
  11.3 0.4 %collective-permute-done.2.refs_3_ = f32[2,80,128]{2,1,0:T(8,128)S(1)} collective-permute-done((f32[2,80,128]{2,1,0:T(8,128)S(1)}, f32[2,80,128]{2,1,0:T(8,128)S(1)}, u32[]{:S(2)}, u32[]{:S(2)}) %collective-permute-start.2) | collective-permute-done | bytes 81952 | tf_op jit(solution)/shard_map/ppermute | solution.py:558
  11.7 2.4 %cost3.1 = (f32[12,4,16,128]{3,2,1,0:T(8,128)S(1)}, f32[13,8,128]{2,1,0:T(8,128)S(1)}) custom-call(f32[4,80,128]{2,1,0:T(8,128)S(1)} %pack0.1.refs_0_.mine, f32[4,80,128]{2,1,0:T(8,128)S(1)} %collective-permute-done.theirs.refs_1_, f32[2,80,128]{2,1,0:T(8,128)S(1)} %collective-permute-done.1.refs_2_, f32[2,80,128]{2,1,0:T(8,128)S(1)} %collective-permute-done.2.refs_3_, ...), custom_call_target="tpu_custom_call" | custom-call | flops 40000000 | bytes 1000 | tf_op jit(solution)/shard_map/cost3/pallas_call | solution.py:430
  14.2 0.0 collective-permute-done.3.refs_4_
  14.2 4.2 %cost4.1 = f32[16,128]{1,0:T(8,128)S(1)} custom-call(f32[4,80,128]{2,1,0:T(8,128)S(1)} %pack0.1.refs_0_.mine, f32[4,80,128]{2,1,0:T(8,128)S(1)} %collective-permute-done.theirs.refs_1_, f32[2,80,128]{2,1,0:T(8,128)S(1)} %collective-permute-done.1.refs_2_, f32[2,80,128]{2,1,0:T(8,128)S(1)} %collective-permute-done.2.refs_3_, ...), custom_call_target="tpu_custom_call" | custom-call | flops 50000000 | bytes 1000 | tf_op jit(solution)/shard_map/cost4/pallas_call | solution.py:430
  18.4 8.6 %all_to_all.11 = f32[8,2,128]{2,1,0:T(2,128)S(1)} all-to-all(f32[8,2,128]{2,1,0:T(2,128)S(1)} %bitcast.9), channel_id=1, replica_groups=mesh['robot'=8,'seed'=4] {'robot'}, dimensions={0} | all-to-all | bytes 16384 | tf_op jit(solution)/shard_map/all_to_all | solution.py:577
  26.9 0.2 blend.1.refs_0_
  27.2 3.7 %collective-permute-start.6 = (f32[80,128]{1,0:T(8,128)S(1)}, f32[80,128]{1,0:T(8,128)S(1)}, u32[]{:S(2)}, u32[]{:S(2)}) collective-permute-start(f32[80,128]{1,0:T(8,128)S(1)} %blend.1.refs_0_), channel_id=1, source_target_pairs={{0,3},{1,2},{2,1},{3,0},{4,7},{5,6},{6,5},{7,4},{8,11},{9,10},{10,... | collective-permute-start | bytes 122888 | tf_op jit(solution)/shard_map/ppermute | solution.py:558
  30.9 0.0 collective-permute-start.5
  30.9 0.8 %collective-permute-start.4 = (f32[80,128]{1,0:T(8,128)S(1)}, f32[80,128]{1,0:T(8,128)S(1)}, u32[]{:S(2)}, u32[]{:S(2)}) collective-permute-start(f32[80,128]{1,0:T(8,128)S(1)} %blend.1.refs_0_), channel_id=1, source_target_pairs={{0,1},{1,0},{2,3},{3,2},{4,5},{5,4},{6,7},{7,6},{8,9},{9,8},{10,11... | collective-permute-start | bytes 122888 | tf_op jit(solution)/shard_map/ppermute | solution.py:558
  31.6 0.6 %owner.1 = f32[2,256]{1,0:T(2,128)} custom-call(f32[16,128]{1,0:T(8,128)S(1)} %bitcast.11), custom_call_target="tpu_custom_call" | custom-call | flops 4000000 | bytes 1000 | tf_op jit(solution)/shard_map/owner/pallas_call | solution.py:460
  32.2 1.0 %collective-permute-done.6.refs_3_ = f32[80,128]{1,0:T(8,128)S(1)} collective-permute-done((f32[80,128]{1,0:T(8,128)S(1)}, f32[80,128]{1,0:T(8,128)S(1)}, u32[]{:S(2)}, u32[]{:S(2)}) %collective-permute-start.6) | collective-permute-done | bytes 40992 | tf_op jit(solution)/shard_map/ppermute | solution.py:558
  33.3 2.5 %collective-permute-done.5.refs_2_ = f32[80,128]{1,0:T(8,128)S(1)} collective-permute-done((f32[80,128]{1,0:T(8,128)S(1)}, f32[80,128]{1,0:T(8,128)S(1)}, u32[]{:S(2)}, u32[]{:S(2)}) %collective-permute-start.5) | collective-permute-done | bytes 40992 | tf_op jit(solution)/shard_map/ppermute | solution.py:558
  35.8 0.0 collective-permute-done.4.refs_1_
  35.8 0.9 %finish.1 = f32[2,3,32,52]{3,2,1,0:T(8,128)} custom-call(f32[80,128]{1,0:T(8,128)S(1)} %blend.1.refs_0_, f32[80,128]{1,0:T(8,128)S(1)} %collective-permute-done.4.refs_1_, f32[80,128]{1,0:T(8,128)S(1)} %collective-permute-done.5.refs_2_, f32[80,128]{1,0:T(8,128)S(1)} %collective-permute-done.6.refs_3_), custom_call_target="tpu_custom_call" | custom-call | tf_op jit(solution)/shard_map/finish/pallas_call | solution.py:545
  (1 shorter events, 0.0 us)
Async XLA Ops:
  1.9 1.6 %collective-permute-start = (f32[4,80,128]{2,1,0:T(8,128)S(1)}, f32[4,80,128]{2,1,0:T(8,128)S(1)}, u32[]{:S(2)}, u32[]{:S(2)}) collective-permute-start(f32[4,80,128]{2,1,0:T(8,128)S(1)} %get-tuple-element.24), channel_id=1, source_target_pairs={{0,4},{4,0},{8,12},{12,8},{16,20},{20,16},{24,28},{28,24},{1,5},{5... | collective-permute-start | bytes 491528 | tf_op jit(solution)/shard_map/ppermute | solution.py:558
  3.5 5.7 %collective-permute-start.1 = (f32[2,80,128]{2,1,0:T(8,128)S(1)}, f32[2,80,128]{2,1,0:T(8,128)S(1)}, u32[]{:S(2)}, u32[]{:S(2)}) collective-permute-start(f32[2,80,128]{2,1,0:T(8,128)S(1)} %get-tuple-element.25), channel_id=1, source_target_pairs={{0,8},{4,12},{8,0},{12,4},{16,24},{20,28},{24,16},{28,20},{1,9},{5... | collective-permute-start | bytes 245768 | tf_op jit(solution)/shard_map/ppermute | solution.py:558
  6.5 5.3 %collective-permute-start.2 = (f32[2,80,128]{2,1,0:T(8,128)S(1)}, f32[2,80,128]{2,1,0:T(8,128)S(1)}, u32[]{:S(2)}, u32[]{:S(2)}) collective-permute-start(f32[2,80,128]{2,1,0:T(8,128)S(1)} %get-tuple-element.26), channel_id=1, source_target_pairs={{0,16},{4,20},{8,24},{12,28},{16,0},{20,4},{24,8},{28,12},{1,17},{... | collective-permute-start | bytes 245768 | tf_op jit(solution)/shard_map/ppermute | solution.py:558
  8.0 6.2 %collective-permute-start.3 = (f32[2,80,128]{2,1,0:T(8,128)S(1)}, f32[2,80,128]{2,1,0:T(8,128)S(1)}, u32[]{:S(2)}, u32[]{:S(2)}) collective-permute-start(f32[2,80,128]{2,1,0:T(8,128)S(1)} %get-tuple-element.27), channel_id=1, source_target_pairs={{0,24},{4,28},{8,16},{12,20},{16,8},{20,12},{24,0},{28,4},{1,25},{... | collective-permute-start | bytes 245768 | tf_op jit(solution)/shard_map/ppermute | solution.py:558
  27.2 6.1 %collective-permute-start.6 = (f32[80,128]{1,0:T(8,128)S(1)}, f32[80,128]{1,0:T(8,128)S(1)}, u32[]{:S(2)}, u32[]{:S(2)}) collective-permute-start(f32[80,128]{1,0:T(8,128)S(1)} %blend.1.refs_0_), channel_id=1, source_target_pairs={{0,3},{1,2},{2,1},{3,0},{4,7},{5,6},{6,5},{7,4},{8,11},{9,10},{10,... | collective-permute-start | bytes 122888 | tf_op jit(solution)/shard_map/ppermute | solution.py:558
  30.9 4.9 %collective-permute-start.5 = (f32[80,128]{1,0:T(8,128)S(1)}, f32[80,128]{1,0:T(8,128)S(1)}, u32[]{:S(2)}, u32[]{:S(2)}) collective-permute-start(f32[80,128]{1,0:T(8,128)S(1)} %blend.1.refs_0_), channel_id=1, source_target_pairs={{0,2},{1,3},{2,0},{3,1},{4,6},{5,7},{6,4},{7,5},{8,10},{9,11},{10,... | collective-permute-start | bytes 122888 | tf_op jit(solution)/shard_map/ppermute | solution.py:558
  30.9 4.9 %collective-permute-start.4 = (f32[80,128]{1,0:T(8,128)S(1)}, f32[80,128]{1,0:T(8,128)S(1)}, u32[]{:S(2)}, u32[]{:S(2)}) collective-permute-start(f32[80,128]{1,0:T(8,128)S(1)} %blend.1.refs_0_), channel_id=1, source_target_pairs={{0,1},{1,0},{2,3},{3,2},{4,5},{5,4},{6,7},{7,6},{8,9},{9,8},{10,11... | collective-permute-start | bytes 122888 | tf_op jit(solution)/shard_map/ppermute | solution.py:558

commit v7 on v6

--- a/solution.py
+++ b/solution.py
@@ -350,19 +350,35 @@
     def with_rows(u, high):
         total = self_terms(u, high)
 
-        def neighbour(state):
-            bits, filled, total = state
-            v = lowest_bit(bits)
+        def take(bits, v, filled):
+            rest = bits & (bits - 1)
+            after = lowest_bit(rest)
             value = against(u, high, part(v, 0))
             totals[v] = totals[v] + value
             if parts > 1:
                 for c, x in enumerate(part(v, 1)):
                     tails[c, pl.ds(filled, SUB), :] = x
                 filled = filled + jnp.maximum(starts[v] - SUB, 0)
-            return bits & (bits - 1), filled, total + value
-
-        state = (links[u], jnp.int32(0), total)
-        _, filled, total = lax.while_loop(lambda state: state[0] != 0, neighbour, state)
+            return rest, after, filled, value
+
+        def two(state):
+            bits, filled, total = state
+            bits, v, filled, value = take(bits, lowest_bit(bits), filled)
+            bits, v, filled, other = take(bits, lowest_bit(bits), filled)
+            return bits, filled, total + (value + other)
+
+        def one(state):
+            bits, v, filled, total = state
+            bits, v, filled, value = take(bits, v, filled)
+            return bits, v, filled, total + value
+
+        bits, filled = links[u], jnp.int32(0)
+        if ends:
+            bits, filled, total = lax.while_loop(
+                lambda state: state[0] & (state[0] - 1) != 0, two, (bits, filled, total)
+            )
+        state = (bits, lowest_bit(bits), filled, total)
+        _, _, filled, total = lax.while_loop(lambda state: state[0] != 0, one, state)
         if parts > 1:
             for c in range(4):
                 fill = jnp.full((SUB, LANES), -FAR if c == 0 else 1.0, jnp.float32)
@@ -399,13 +415,15 @@
         if parts > 1:
 
             def hand_out(state):
-                bits, filled = state
-                v = lowest_bit(bits)
+                bits, v, filled = state
+                rest = bits & (bits - 1)
+                after = lowest_bit(rest)
                 more = jnp.maximum(starts[v] - SUB, 0)
                 totals[v] = totals[v] + jnp.where(sub < more, sums[pl.ds(filled, SUB), :], 0.0)
-                return bits & (bits - 1), filled + more
-
-            lax.while_loop(lambda state: state[0] != 0, hand_out, (links[u], jnp.int32(0)))
+                return rest, after, filled + more
+
+            state = (links[u], lowest_bit(links[u]), jnp.int32(0))
+            lax.while_loop(lambda state: state[0] != 0, hand_out, state)
 
     if not ends:
         return

time: 36.9 us -> 36.4 us (0.986)
  blocking collectives: 8.6 us -> 7.6 us
  waiting for transfers between devices: 4.28 us -> 5.07 us
  Pallas kernels: 13.6 us -> 13.2 us
    all_to_all x1, blocking collectives: 8.6 us -> 7.6 us  [local(): costs = lax.all_to_all(costs, 'robot', 0, 0, tiled=True)]
    ppermute x7, waiting for transfers between devices: 4.28 us -> 5.07 us  [exchanged(): return lax.ppermute(block, axis, [(i, i ^ k) for i in range(size)])]
    pallas_call x5, Pallas kernels: 10.3 us -> 9.9 us  [cost(): pl.pallas_call(functools.partial(cost_kernel, plan, stage), out_shape=[ja...]
  transfers between devices with their start and end apart: 7 -> 7, of which waited for: 5 -> 5; matrix products, arithmetic and copies ran while one was open for 0% -> 0% of each run, Pallas kernels for 19% -> 17%
where the time goes in v7:
time: 36.4 us; the launch traced here: 36 us
  Pallas kernels  13.2 us (36%)
  starting transfers between devices  9.46 us (26%)
  blocking collectives  7.6 us (21%)
  waiting for transfers between devices  5.07 us (14%)
  between operations  0.71 us (2%)
    pallas_call x5, Pallas kernels, cost(): pl.pallas_call(functools.partial(cost_kernel, plan, stage), out_shape=[ja...  9.9 us
    ppermute x7, starting transfers between devices, exchanged(): return lax.ppermute(block, axis, [(i, i ^ k) for i in range(size)])  9.46 us
    all_to_all x1, blocking collectives, local(): costs = lax.all_to_all(costs, 'robot', 0, 0, tiled=True)  7.6 us
    ppermute x7, waiting for transfers between devices, exchanged(): return lax.ppermute(block, axis, [(i, i ^ k) for i in range(size)])  5.07 us
    pallas_call x2, Pallas kernels, pack(): pl.pallas_call(functools.partial(pack_kernel, plan, core), out_shape=[jax...  1.59 us
    pallas_call x1, Pallas kernels, finish(): pl.pallas_call(functools.partial(finish_kernel, plan), out_shape=jax.Shap...  0.86 us
  transfers between devices with their start and end apart: 7, of which 5 were waited for; matrix products, arithmetic and copies ran while one was open for 0% of the time, Pallas kernels for 17%

profile of v7, /device:TPU:0, one launch (start us, length us, event | category | flops | bytes accessed | tf_op | source)
XLA Modules:
  0.0 36.0 jit_solution(515103200540203752)
XLA Ops:
  0.6 1.3 %pack1.1 = (f32[4,80,128]{2,1,0:T(8,128)S(1)}, f32[624,128]{1,0:T(8,128)S(1)}, f32[2,128]{1,0:T(2,128)S(1)}) custom-call(f32[624,128]{1,0:T(8,128)} %bitcast.12, s32[1,2]{1,0:T(1,128)} %bitcast.14, f32[2,52]{1,0:T(2,128)} %refs_2_.1, s32[2,16]{1,0:T(2,128)} %refs_3_.1), custom_call_target="tpu_custom_call" | custom-call | flops 4000000 | bytes 1000 | tf_op jit(solution)/shard_map/pack1/pallas_call | solution.py:156
  1.9 0.6 %collective-permute-start = (f32[4,80,128]{2,1,0:T(8,128)S(1)}, f32[4,80,128]{2,1,0:T(8,128)S(1)}, u32[]{:S(2)}, u32[]{:S(2)}) collective-permute-start(f32[4,80,128]{2,1,0:T(8,128)S(1)} %get-tuple-element.24), channel_id=1, source_target_pairs={{0,4},{4,0},{8,12},{12,8},{16,20},{20,16},{24,28},{28,24},{1,5},{5... | collective-permute-start | bytes 491528 | tf_op jit(solution)/shard_map/ppermute | solution.py:576
  2.5 0.3 pack0.1.refs_0_.mine
  2.8 0.6 %cost0.1 = (f32[2,4,16,128]{3,2,1,0:T(8,128)S(1)}, f32[3,8,128]{2,1,0:T(8,128)S(1)}) custom-call(f32[4,80,128]{2,1,0:T(8,128)S(1)} %pack0.1.refs_0_.mine), custom_call_target="tpu_custom_call" | custom-call | flops 10000000 | bytes 1000 | tf_op jit(solution)/shard_map/cost0/pallas_call | solution.py:448
  3.4 0.1 collective-permute-done.theirs.refs_1_
  3.5 2.9 %collective-permute-start.1 = (f32[2,80,128]{2,1,0:T(8,128)S(1)}, f32[2,80,128]{2,1,0:T(8,128)S(1)}, u32[]{:S(2)}, u32[]{:S(2)}) collective-permute-start(f32[2,80,128]{2,1,0:T(8,128)S(1)} %get-tuple-element.25), channel_id=1, source_target_pairs={{0,8},{4,12},{8,0},{12,4},{16,24},{20,28},{24,16},{28,20},{1,9},{5... | collective-permute-start | bytes 245768 | tf_op jit(solution)/shard_map/ppermute | solution.py:576
  6.5 1.5 %collective-permute-start.2 = (f32[2,80,128]{2,1,0:T(8,128)S(1)}, f32[2,80,128]{2,1,0:T(8,128)S(1)}, u32[]{:S(2)}, u32[]{:S(2)}) collective-permute-start(f32[2,80,128]{2,1,0:T(8,128)S(1)} %get-tuple-element.26), channel_id=1, source_target_pairs={{0,16},{4,20},{8,24},{12,28},{16,0},{20,4},{24,8},{28,12},{1,17},{... | collective-permute-start | bytes 245768 | tf_op jit(solution)/shard_map/ppermute | solution.py:576
  8.0 0.0 collective-permute-start.3
  8.0 0.5 %cost1.1 = (f32[4,4,16,128]{3,2,1,0:T(8,128)S(1)}, f32[5,8,128]{2,1,0:T(8,128)S(1)}) custom-call(f32[4,80,128]{2,1,0:T(8,128)S(1)} %pack0.1.refs_0_.mine, f32[4,80,128]{2,1,0:T(8,128)S(1)} %collective-permute-done.theirs.refs_1_, f32[2,4,16,128]{3,2,1,0:T(8,128)S(1)} %get-tuple-element.28.refs_2_, f32[3,8,128]{2,1,0:T(8,128)S(1)} %get-tuple-element.29.refs_3_), custom_call_target="tpu_custom_call" | custom-call | flops 20000000 | bytes 1000 | tf_op jit(solution)/shard_map/cost1/pallas_call | solution.py:448
  8.5 0.7 %collective-permute-done.1.refs_2_ = f32[2,80,128]{2,1,0:T(8,128)S(1)} collective-permute-done((f32[2,80,128]{2,1,0:T(8,128)S(1)}, f32[2,80,128]{2,1,0:T(8,128)S(1)}, u32[]{:S(2)}, u32[]{:S(2)}) %collective-permute-start.1) | collective-permute-done | bytes 81952 | tf_op jit(solution)/shard_map/ppermute | solution.py:576
  9.2 1.8 %cost2.1 = (f32[8,4,16,128]{3,2,1,0:T(8,128)S(1)}, f32[9,8,128]{2,1,0:T(8,128)S(1)}) custom-call(f32[4,80,128]{2,1,0:T(8,128)S(1)} %pack0.1.refs_0_.mine, f32[4,80,128]{2,1,0:T(8,128)S(1)} %collective-permute-done.theirs.refs_1_, f32[2,80,128]{2,1,0:T(8,128)S(1)} %collective-permute-done.1.refs_2_, f32[4,4,16,128]{3,2,1,0:T(8,128)S(1)} %get-tuple-element.30.refs_3_, ...), custom_call_target="tpu_custom_call" | custom-call | flops 30000000 | bytes 1000 | tf_op jit(solution)/shard_map/cost2/pallas_call | solution.py:448
  11.0 0.7 %collective-permute-done.2.refs_3_ = f32[2,80,128]{2,1,0:T(8,128)S(1)} collective-permute-done((f32[2,80,128]{2,1,0:T(8,128)S(1)}, f32[2,80,128]{2,1,0:T(8,128)S(1)}, u32[]{:S(2)}, u32[]{:S(2)}) %collective-permute-start.2) | collective-permute-done | bytes 81952 | tf_op jit(solution)/shard_map/ppermute | solution.py:576
  11.7 2.5 %cost3.1 = (f32[12,4,16,128]{3,2,1,0:T(8,128)S(1)}, f32[13,8,128]{2,1,0:T(8,128)S(1)}) custom-call(f32[4,80,128]{2,1,0:T(8,128)S(1)} %pack0.1.refs_0_.mine, f32[4,80,128]{2,1,0:T(8,128)S(1)} %collective-permute-done.theirs.refs_1_, f32[2,80,128]{2,1,0:T(8,128)S(1)} %collective-permute-done.1.refs_2_, f32[2,80,128]{2,1,0:T(8,128)S(1)} %collective-permute-done.2.refs_3_, ...), custom_call_target="tpu_custom_call" | custom-call | flops 40000000 | bytes 1000 | tf_op jit(solution)/shard_map/cost3/pallas_call | solution.py:448
  14.2 0.0 collective-permute-done.3.refs_4_
  14.2 4.5 %cost4.1 = f32[16,128]{1,0:T(8,128)S(1)} custom-call(f32[4,80,128]{2,1,0:T(8,128)S(1)} %pack0.1.refs_0_.mine, f32[4,80,128]{2,1,0:T(8,128)S(1)} %collective-permute-done.theirs.refs_1_, f32[2,80,128]{2,1,0:T(8,128)S(1)} %collective-permute-done.1.refs_2_, f32[2,80,128]{2,1,0:T(8,128)S(1)} %collective-permute-done.2.refs_3_, ...), custom_call_target="tpu_custom_call" | custom-call | flops 50000000 | bytes 1000 | tf_op jit(solution)/shard_map/cost4/pallas_call | solution.py:448
  18.7 7.6 %all_to_all.11 = f32[8,2,128]{2,1,0:T(2,128)S(1)} all-to-all(f32[8,2,128]{2,1,0:T(2,128)S(1)} %bitcast.9), channel_id=1, replica_groups=mesh['robot'=8,'seed'=4] {'robot'}, dimensions={0} | all-to-all | bytes 16384 | tf_op jit(solution)/shard_map/all_to_all | solution.py:595
  26.3 0.2 blend.1.refs_0_
  26.6 3.7 %collective-permute-start.6 = (f32[80,128]{1,0:T(8,128)S(1)}, f32[80,128]{1,0:T(8,128)S(1)}, u32[]{:S(2)}, u32[]{:S(2)}) collective-permute-start(f32[80,128]{1,0:T(8,128)S(1)} %blend.1.refs_0_), channel_id=1, source_target_pairs={{0,3},{1,2},{2,1},{3,0},{4,7},{5,6},{6,5},{7,4},{8,11},{9,10},{10,... | collective-permute-start | bytes 122888 | tf_op jit(solution)/shard_map/ppermute | solution.py:576
  30.2 0.0 collective-permute-start.5
  30.2 0.8 %collective-permute-start.4 = (f32[80,128]{1,0:T(8,128)S(1)}, f32[80,128]{1,0:T(8,128)S(1)}, u32[]{:S(2)}, u32[]{:S(2)}) collective-permute-start(f32[80,128]{1,0:T(8,128)S(1)} %blend.1.refs_0_), channel_id=1, source_target_pairs={{0,1},{1,0},{2,3},{3,2},{4,5},{5,4},{6,7},{7,6},{8,9},{9,8},{10,11... | collective-permute-start | bytes 122888 | tf_op jit(solution)/shard_map/ppermute | solution.py:576
  31.0 0.6 %owner.1 = f32[2,256]{1,0:T(2,128)} custom-call(f32[16,128]{1,0:T(8,128)S(1)} %bitcast.11), custom_call_target="tpu_custom_call" | custom-call | flops 4000000 | bytes 1000 | tf_op jit(solution)/shard_map/owner/pallas_call | solution.py:478
  31.6 1.0 %collective-permute-done.6.refs_3_ = f32[80,128]{1,0:T(8,128)S(1)} collective-permute-done((f32[80,128]{1,0:T(8,128)S(1)}, f32[80,128]{1,0:T(8,128)S(1)}, u32[]{:S(2)}, u32[]{:S(2)}) %collective-permute-start.6) | collective-permute-done | bytes 40992 | tf_op jit(solution)/shard_map/ppermute | solution.py:576
  32.6 2.5 %collective-permute-done.5.refs_2_ = f32[80,128]{1,0:T(8,128)S(1)} collective-permute-done((f32[80,128]{1,0:T(8,128)S(1)}, f32[80,128]{1,0:T(8,128)S(1)}, u32[]{:S(2)}, u32[]{:S(2)}) %collective-permute-start.5) | collective-permute-done | bytes 40992 | tf_op jit(solution)/shard_map/ppermute | solution.py:576
  35.1 0.0 collective-permute-done.4.refs_1_
  35.1 0.9 %finish.1 = f32[2,3,32,52]{3,2,1,0:T(8,128)} custom-call(f32[80,128]{1,0:T(8,128)S(1)} %blend.1.refs_0_, f32[80,128]{1,0:T(8,128)S(1)} %collective-permute-done.4.refs_1_, f32[80,128]{1,0:T(8,128)S(1)} %collective-permute-done.5.refs_2_, f32[80,128]{1,0:T(8,128)S(1)} %collective-permute-done.6.refs_3_), custom_call_target="tpu_custom_call" | custom-call | tf_op jit(solution)/shard_map/finish/pallas_call | solution.py:563
  (1 shorter events, 0.0 us)
Async XLA Ops:
  1.9 1.6 %collective-permute-start = (f32[4,80,128]{2,1,0:T(8,128)S(1)}, f32[4,80,128]{2,1,0:T(8,128)S(1)}, u32[]{:S(2)}, u32[]{:S(2)}) collective-permute-start(f32[4,80,128]{2,1,0:T(8,128)S(1)} %get-tuple-element.24), channel_id=1, source_target_pairs={{0,4},{4,0},{8,12},{12,8},{16,20},{20,16},{24,28},{28,24},{1,5},{5... | collective-permute-start | bytes 491528 | tf_op jit(solution)/shard_map/ppermute | solution.py:576
  3.5 5.7 %collective-permute-start.1 = (f32[2,80,128]{2,1,0:T(8,128)S(1)}, f32[2,80,128]{2,1,0:T(8,128)S(1)}, u32[]{:S(2)}, u32[]{:S(2)}) collective-permute-start(f32[2,80,128]{2,1,0:T(8,128)S(1)} %get-tuple-element.25), channel_id=1, source_target_pairs={{0,8},{4,12},{8,0},{12,4},{16,24},{20,28},{24,16},{28,20},{1,9},{5... | collective-permute-start | bytes 245768 | tf_op jit(solution)/shard_map/ppermute | solution.py:576
  6.5 5.3 %collective-permute-start.2 = (f32[2,80,128]{2,1,0:T(8,128)S(1)}, f32[2,80,128]{2,1,0:T(8,128)S(1)}, u32[]{:S(2)}, u32[]{:S(2)}) collective-permute-start(f32[2,80,128]{2,1,0:T(8,128)S(1)} %get-tuple-element.26), channel_id=1, source_target_pairs={{0,16},{4,20},{8,24},{12,28},{16,0},{20,4},{24,8},{28,12},{1,17},{... | collective-permute-start | bytes 245768 | tf_op jit(solution)/shard_map/ppermute | solution.py:576
  8.0 6.2 %collective-permute-start.3 = (f32[2,80,128]{2,1,0:T(8,128)S(1)}, f32[2,80,128]{2,1,0:T(8,128)S(1)}, u32[]{:S(2)}, u32[]{:S(2)}) collective-permute-start(f32[2,80,128]{2,1,0:T(8,128)S(1)} %get-tuple-element.27), channel_id=1, source_target_pairs={{0,24},{4,28},{8,16},{12,20},{16,8},{20,12},{24,0},{28,4},{1,25},{... | collective-permute-start | bytes 245768 | tf_op jit(solution)/shard_map/ppermute | solution.py:576
  26.6 6.1 %collective-permute-start.6 = (f32[80,128]{1,0:T(8,128)S(1)}, f32[80,128]{1,0:T(8,128)S(1)}, u32[]{:S(2)}, u32[]{:S(2)}) collective-permute-start(f32[80,128]{1,0:T(8,128)S(1)} %blend.1.refs_0_), channel_id=1, source_target_pairs={{0,3},{1,2},{2,1},{3,0},{4,7},{5,6},{6,5},{7,4},{8,11},{9,10},{10,... | collective-permute-start | bytes 122888 | tf_op jit(solution)/shard_map/ppermute | solution.py:576
  30.2 4.9 %collective-permute-start.5 = (f32[80,128]{1,0:T(8,128)S(1)}, f32[80,128]{1,0:T(8,128)S(1)}, u32[]{:S(2)}, u32[]{:S(2)}) collective-permute-start(f32[80,128]{1,0:T(8,128)S(1)} %blend.1.refs_0_), channel_id=1, source_target_pairs={{0,2},{1,3},{2,0},{3,1},{4,6},{5,7},{6,4},{7,5},{8,10},{9,11},{10,... | collective-permute-start | bytes 122888 | tf_op jit(solution)/shard_map/ppermute | solution.py:576
  30.2 4.9 %collective-permute-start.4 = (f32[80,128]{1,0:T(8,128)S(1)}, f32[80,128]{1,0:T(8,128)S(1)}, u32[]{:S(2)}, u32[]{:S(2)}) collective-permute-start(f32[80,128]{1,0:T(8,128)S(1)} %blend.1.refs_0_), channel_id=1, source_target_pairs={{0,1},{1,0},{2,3},{3,2},{4,5},{5,4},{6,7},{7,6},{8,9},{9,8},{10,11... | collective-permute-start | bytes 122888 | tf_op jit(solution)/shard_map/ppermute | solution.py:576

commit v8 on v7

--- a/solution.py
+++ b/solution.py
@@ -278,6 +278,9 @@
             x = fields[c]
             for m in range(1, g):
                 blocks[i, c, m, 0:rows, :] = pltpu.roll(x, m * width, 1)
+                if rows < SUB:
+                    fill = jnp.full((SUB - rows, LANES), -2 * FAR if c == 0 else 1.0, jnp.float32)
+                    blocks[i, c, m, rows:SUB, :] = fill
             store[slot, c, 0:rows, :] = x
             if deep > rows:
                 fill = jnp.full((deep - rows, LANES), -FAR if c == 0 else 1.0, jnp.float32)

time: 36.4 us -> 36.3 us (level)
  transfers between devices with their start and end apart: 7 -> 7, of which waited for: 5 -> 5; matrix products, arithmetic and copies ran while one was open for 0% -> 0% of each run, Pallas kernels for 17% -> 18%
where the time goes in v8:
time: 36.3 us; the launch traced here: 36.2 us
  Pallas kernels  13.2 us (36%)
  starting transfers between devices  9.46 us (26%)
  blocking collectives  7.83 us (22%)
  waiting for transfers between devices  4.98 us (14%)
  between operations  0.71 us (2%)
    pallas_call x5, Pallas kernels, cost(): pl.pallas_call(functools.partial(cost_kernel, plan, stage), out_shape=[ja...  9.91 us
    ppermute x7, starting transfers between devices, exchanged(): return lax.ppermute(block, axis, [(i, i ^ k) for i in range(size)])  9.46 us
    all_to_all x1, blocking collectives, local(): costs = lax.all_to_all(costs, 'robot', 0, 0, tiled=True)  7.83 us
    ppermute x7, waiting for transfers between devices, exchanged(): return lax.ppermute(block, axis, [(i, i ^ k) for i in range(size)])  4.98 us
    pallas_call x2, Pallas kernels, pack(): pl.pallas_call(functools.partial(pack_kernel, plan, core), out_shape=[jax...  1.59 us
    pallas_call x1, Pallas kernels, finish(): pl.pallas_call(functools.partial(finish_kernel, plan), out_shape=jax.Shap...  0.86 us
  transfers between devices with their start and end apart: 7, of which 5 were waited for; matrix products, arithmetic and copies ran while one was open for 0% of the time, Pallas kernels for 18%

profile of v8, /device:TPU:0, one launch (start us, length us, event | category | flops | bytes accessed | tf_op | source)
XLA Modules:
  0.0 36.2 jit_solution(515103200540203752)
XLA Ops:
  0.6 1.3 %pack1.1 = (f32[4,80,128]{2,1,0:T(8,128)S(1)}, f32[624,128]{1,0:T(8,128)S(1)}, f32[2,128]{1,0:T(2,128)S(1)}) custom-call(f32[624,128]{1,0:T(8,128)} %bitcast.12, s32[1,2]{1,0:T(1,128)} %bitcast.14, f32[2,52]{1,0:T(2,128)} %refs_2_.1, s32[2,16]{1,0:T(2,128)} %refs_3_.1), custom_call_target="tpu_custom_call" | custom-call | flops 4000000 | bytes 1000 | tf_op jit(solution)/shard_map/pack1/pallas_call | solution.py:156
  1.9 0.6 %collective-permute-start = (f32[4,80,128]{2,1,0:T(8,128)S(1)}, f32[4,80,128]{2,1,0:T(8,128)S(1)}, u32[]{:S(2)}, u32[]{:S(2)}) collective-permute-start(f32[4,80,128]{2,1,0:T(8,128)S(1)} %get-tuple-element.24), channel_id=1, source_target_pairs={{0,4},{4,0},{8,12},{12,8},{16,20},{20,16},{24,28},{28,24},{1,5},{5... | collective-permute-start | bytes 491528 | tf_op jit(solution)/shard_map/ppermute | solution.py:579
  2.5 0.3 pack0.1.refs_0_.mine
  2.8 0.5 %cost0.1 = (f32[2,4,16,128]{3,2,1,0:T(8,128)S(1)}, f32[3,8,128]{2,1,0:T(8,128)S(1)}) custom-call(f32[4,80,128]{2,1,0:T(8,128)S(1)} %pack0.1.refs_0_.mine), custom_call_target="tpu_custom_call" | custom-call | flops 10000000 | bytes 1000 | tf_op jit(solution)/shard_map/cost0/pallas_call | solution.py:451
  3.3 0.2 collective-permute-done.theirs.refs_1_
  3.5 2.9 %collective-permute-start.1 = (f32[2,80,128]{2,1,0:T(8,128)S(1)}, f32[2,80,128]{2,1,0:T(8,128)S(1)}, u32[]{:S(2)}, u32[]{:S(2)}) collective-permute-start(f32[2,80,128]{2,1,0:T(8,128)S(1)} %get-tuple-element.25), channel_id=1, source_target_pairs={{0,8},{4,12},{8,0},{12,4},{16,24},{20,28},{24,16},{28,20},{1,9},{5... | collective-permute-start | bytes 245768 | tf_op jit(solution)/shard_map/ppermute | solution.py:579
  6.5 1.5 %collective-permute-start.2 = (f32[2,80,128]{2,1,0:T(8,128)S(1)}, f32[2,80,128]{2,1,0:T(8,128)S(1)}, u32[]{:S(2)}, u32[]{:S(2)}) collective-permute-start(f32[2,80,128]{2,1,0:T(8,128)S(1)} %get-tuple-element.26), channel_id=1, source_target_pairs={{0,16},{4,20},{8,24},{12,28},{16,0},{20,4},{24,8},{28,12},{1,17},{... | collective-permute-start | bytes 245768 | tf_op jit(solution)/shard_map/ppermute | solution.py:579
  8.0 0.0 collective-permute-start.3
  8.0 0.5 %cost1.1 = (f32[4,4,16,128]{3,2,1,0:T(8,128)S(1)}, f32[5,8,128]{2,1,0:T(8,128)S(1)}) custom-call(f32[4,80,128]{2,1,0:T(8,128)S(1)} %pack0.1.refs_0_.mine, f32[4,80,128]{2,1,0:T(8,128)S(1)} %collective-permute-done.theirs.refs_1_, f32[2,4,16,128]{3,2,1,0:T(8,128)S(1)} %get-tuple-element.28.refs_2_, f32[3,8,128]{2,1,0:T(8,128)S(1)} %get-tuple-element.29.refs_3_), custom_call_target="tpu_custom_call" | custom-call | flops 20000000 | bytes 1000 | tf_op jit(solution)/shard_map/cost1/pallas_call | solution.py:451
  8.5 0.7 %collective-permute-done.1.refs_2_ = f32[2,80,128]{2,1,0:T(8,128)S(1)} collective-permute-done((f32[2,80,128]{2,1,0:T(8,128)S(1)}, f32[2,80,128]{2,1,0:T(8,128)S(1)}, u32[]{:S(2)}, u32[]{:S(2)}) %collective-permute-start.1) | collective-permute-done | bytes 81952 | tf_op jit(solution)/shard_map/ppermute | solution.py:579
  9.2 2.0 %cost2.1 = (f32[8,4,16,128]{3,2,1,0:T(8,128)S(1)}, f32[9,8,128]{2,1,0:T(8,128)S(1)}) custom-call(f32[4,80,128]{2,1,0:T(8,128)S(1)} %pack0.1.refs_0_.mine, f32[4,80,128]{2,1,0:T(8,128)S(1)} %collective-permute-done.theirs.refs_1_, f32[2,80,128]{2,1,0:T(8,128)S(1)} %collective-permute-done.1.refs_2_, f32[4,4,16,128]{3,2,1,0:T(8,128)S(1)} %get-tuple-element.30.refs_3_, ...), custom_call_target="tpu_custom_call" | custom-call | flops 30000000 | bytes 1000 | tf_op jit(solution)/shard_map/cost2/pallas_call | solution.py:451
  11.2 0.5 %collective-permute-done.2.refs_3_ = f32[2,80,128]{2,1,0:T(8,128)S(1)} collective-permute-done((f32[2,80,128]{2,1,0:T(8,128)S(1)}, f32[2,80,128]{2,1,0:T(8,128)S(1)}, u32[]{:S(2)}, u32[]{:S(2)}) %collective-permute-start.2) | collective-permute-done | bytes 81952 | tf_op jit(solution)/shard_map/ppermute | solution.py:579
  11.7 2.8 %cost3.1 = (f32[12,4,16,128]{3,2,1,0:T(8,128)S(1)}, f32[13,8,128]{2,1,0:T(8,128)S(1)}) custom-call(f32[4,80,128]{2,1,0:T(8,128)S(1)} %pack0.1.refs_0_.mine, f32[4,80,128]{2,1,0:T(8,128)S(1)} %collective-permute-done.theirs.refs_1_, f32[2,80,128]{2,1,0:T(8,128)S(1)} %collective-permute-done.1.refs_2_, f32[2,80,128]{2,1,0:T(8,128)S(1)} %collective-permute-done.2.refs_3_, ...), custom_call_target="tpu_custom_call" | custom-call | flops 40000000 | bytes 1000 | tf_op jit(solution)/shard_map/cost3/pallas_call | solution.py:451
  14.5 0.0 collective-permute-done.3.refs_4_
  14.5 4.1 %cost4.1 = f32[16,128]{1,0:T(8,128)S(1)} custom-call(f32[4,80,128]{2,1,0:T(8,128)S(1)} %pack0.1.refs_0_.mine, f32[4,80,128]{2,1,0:T(8,128)S(1)} %collective-permute-done.theirs.refs_1_, f32[2,80,128]{2,1,0:T(8,128)S(1)} %collective-permute-done.1.refs_2_, f32[2,80,128]{2,1,0:T(8,128)S(1)} %collective-permute-done.2.refs_3_, ...), custom_call_target="tpu_custom_call" | custom-call | flops 50000000 | bytes 1000 | tf_op jit(solution)/shard_map/cost4/pallas_call | solution.py:451
  18.7 7.8 %all_to_all.11 = f32[8,2,128]{2,1,0:T(2,128)S(1)} all-to-all(f32[8,2,128]{2,1,0:T(2,128)S(1)} %bitcast.9), channel_id=1, replica_groups=mesh['robot'=8,'seed'=4] {'robot'}, dimensions={0} | all-to-all | bytes 16384 | tf_op jit(solution)/shard_map/all_to_all | solution.py:598
  26.5 0.2 blend.1.refs_0_
  26.7 3.7 %collective-permute-start.6 = (f32[80,128]{1,0:T(8,128)S(1)}, f32[80,128]{1,0:T(8,128)S(1)}, u32[]{:S(2)}, u32[]{:S(2)}) collective-permute-start(f32[80,128]{1,0:T(8,128)S(1)} %blend.1.refs_0_), channel_id=1, source_target_pairs={{0,3},{1,2},{2,1},{3,0},{4,7},{5,6},{6,5},{7,4},{8,11},{9,10},{10,... | collective-permute-start | bytes 122888 | tf_op jit(solution)/shard_map/ppermute | solution.py:579
  30.4 0.0 collective-permute-start.5
  30.4 0.8 %collective-permute-start.4 = (f32[80,128]{1,0:T(8,128)S(1)}, f32[80,128]{1,0:T(8,128)S(1)}, u32[]{:S(2)}, u32[]{:S(2)}) collective-permute-start(f32[80,128]{1,0:T(8,128)S(1)} %blend.1.refs_0_), channel_id=1, source_target_pairs={{0,1},{1,0},{2,3},{3,2},{4,5},{5,4},{6,7},{7,6},{8,9},{9,8},{10,11... | collective-permute-start | bytes 122888 | tf_op jit(solution)/shard_map/ppermute | solution.py:579
  31.2 0.6 %owner.1 = f32[2,256]{1,0:T(2,128)} custom-call(f32[16,128]{1,0:T(8,128)S(1)} %bitcast.11), custom_call_target="tpu_custom_call" | custom-call | flops 4000000 | bytes 1000 | tf_op jit(solution)/shard_map/owner/pallas_call | solution.py:481
  31.8 1.0 %collective-permute-done.6.refs_3_ = f32[80,128]{1,0:T(8,128)S(1)} collective-permute-done((f32[80,128]{1,0:T(8,128)S(1)}, f32[80,128]{1,0:T(8,128)S(1)}, u32[]{:S(2)}, u32[]{:S(2)}) %collective-permute-start.6) | collective-permute-done | bytes 40992 | tf_op jit(solution)/shard_map/ppermute | solution.py:579
  32.8 2.5 %collective-permute-done.5.refs_2_ = f32[80,128]{1,0:T(8,128)S(1)} collective-permute-done((f32[80,128]{1,0:T(8,128)S(1)}, f32[80,128]{1,0:T(8,128)S(1)}, u32[]{:S(2)}, u32[]{:S(2)}) %collective-permute-start.5) | collective-permute-done | bytes 40992 | tf_op jit(solution)/shard_map/ppermute | solution.py:579
  35.3 0.0 collective-permute-done.4.refs_1_
  35.3 0.9 %finish.1 = f32[2,3,32,52]{3,2,1,0:T(8,128)} custom-call(f32[80,128]{1,0:T(8,128)S(1)} %blend.1.refs_0_, f32[80,128]{1,0:T(8,128)S(1)} %collective-permute-done.4.refs_1_, f32[80,128]{1,0:T(8,128)S(1)} %collective-permute-done.5.refs_2_, f32[80,128]{1,0:T(8,128)S(1)} %collective-permute-done.6.refs_3_), custom_call_target="tpu_custom_call" | custom-call | tf_op jit(solution)/shard_map/finish/pallas_call | solution.py:566
  (1 shorter events, 0.0 us)
Async XLA Ops:
  1.9 1.6 %collective-permute-start = (f32[4,80,128]{2,1,0:T(8,128)S(1)}, f32[4,80,128]{2,1,0:T(8,128)S(1)}, u32[]{:S(2)}, u32[]{:S(2)}) collective-permute-start(f32[4,80,128]{2,1,0:T(8,128)S(1)} %get-tuple-element.24), channel_id=1, source_target_pairs={{0,4},{4,0},{8,12},{12,8},{16,20},{20,16},{24,28},{28,24},{1,5},{5... | collective-permute-start | bytes 491528 | tf_op jit(solution)/shard_map/ppermute | solution.py:579
  3.5 5.7 %collective-permute-start.1 = (f32[2,80,128]{2,1,0:T(8,128)S(1)}, f32[2,80,128]{2,1,0:T(8,128)S(1)}, u32[]{:S(2)}, u32[]{:S(2)}) collective-permute-start(f32[2,80,128]{2,1,0:T(8,128)S(1)} %get-tuple-element.25), channel_id=1, source_target_pairs={{0,8},{4,12},{8,0},{12,4},{16,24},{20,28},{24,16},{28,20},{1,9},{5... | collective-permute-start | bytes 245768 | tf_op jit(solution)/shard_map/ppermute | solution.py:579
  6.5 5.3 %collective-permute-start.2 = (f32[2,80,128]{2,1,0:T(8,128)S(1)}, f32[2,80,128]{2,1,0:T(8,128)S(1)}, u32[]{:S(2)}, u32[]{:S(2)}) collective-permute-start(f32[2,80,128]{2,1,0:T(8,128)S(1)} %get-tuple-element.26), channel_id=1, source_target_pairs={{0,16},{4,20},{8,24},{12,28},{16,0},{20,4},{24,8},{28,12},{1,17},{... | collective-permute-start | bytes 245768 | tf_op jit(solution)/shard_map/ppermute | solution.py:579
  8.0 6.6 %collective-permute-start.3 = (f32[2,80,128]{2,1,0:T(8,128)S(1)}, f32[2,80,128]{2,1,0:T(8,128)S(1)}, u32[]{:S(2)}, u32[]{:S(2)}) collective-permute-start(f32[2,80,128]{2,1,0:T(8,128)S(1)} %get-tuple-element.27), channel_id=1, source_target_pairs={{0,24},{4,28},{8,16},{12,20},{16,8},{20,12},{24,0},{28,4},{1,25},{... | collective-permute-start | bytes 245768 | tf_op jit(solution)/shard_map/ppermute | solution.py:579
  26.7 6.1 %collective-permute-start.6 = (f32[80,128]{1,0:T(8,128)S(1)}, f32[80,128]{1,0:T(8,128)S(1)}, u32[]{:S(2)}, u32[]{:S(2)}) collective-permute-start(f32[80,128]{1,0:T(8,128)S(1)} %blend.1.refs_0_), channel_id=1, source_target_pairs={{0,3},{1,2},{2,1},{3,0},{4,7},{5,6},{6,5},{7,4},{8,11},{9,10},{10,... | collective-permute-start | bytes 122888 | tf_op jit(solution)/shard_map/ppermute | solution.py:579
  30.4 4.9 %collective-permute-start.5 = (f32[80,128]{1,0:T(8,128)S(1)}, f32[80,128]{1,0:T(8,128)S(1)}, u32[]{:S(2)}, u32[]{:S(2)}) collective-permute-start(f32[80,128]{1,0:T(8,128)S(1)} %blend.1.refs_0_), channel_id=1, source_target_pairs={{0,2},{1,3},{2,0},{3,1},{4,6},{5,7},{6,4},{7,5},{8,10},{9,11},{10,... | collective-permute-start | bytes 122888 | tf_op jit(solution)/shard_map/ppermute | solution.py:579
  30.4 4.9 %collective-permute-start.4 = (f32[80,128]{1,0:T(8,128)S(1)}, f32[80,128]{1,0:T(8,128)S(1)}, u32[]{:S(2)}, u32[]{:S(2)}) collective-permute-start(f32[80,128]{1,0:T(8,128)S(1)} %blend.1.refs_0_), channel_id=1, source_target_pairs={{0,1},{1,0},{2,3},{3,2},{4,5},{5,4},{6,7},{7,6},{8,9},{9,8},{10,11... | collective-permute-start | bytes 122888 | tf_op jit(solution)/shard_map/ppermute | solution.py:579
